TPU v7x, 32 devices: a whole 2x2x4 slice. The times are simulated.
32 devices in a mesh: head: 4 (over x, core), ctx: 8 (over z, y).
Axes of the slice: x: 2, y: 2, z: 4, core: 2. Of those that a mesh axis runs over, the one named last changes fastest.
Arguments:
- token_ids: int32 [2, 16], replicated, may hold values from 0 to 64127
- suffix_lengths: int32 [16], replicated, may hold values from 0 to 128, as said below
- embedding: bfloat16 [64128, 16384], P('ctx', 'head'), may hold values from -36 to 36
- attn_gain: float32 [16384], P('head'), may hold values from 0.25 to 1.75
- qkv_weight: bfloat16 [16384, 8, 1280], P('head', None, 'ctx'), may hold values from -0.046875 to 0.046875
- out_weight: bfloat16 [8192, 16384], P('head', 'ctx'), may hold values from -0.0625 to 0.0625
- prefix_keys: bfloat16 [8, 32768, 128], P('head', 'ctx'), may hold values from -32 to 32
- prefix_values: bfloat16 [8, 32768, 128], P('head', 'ctx'), may hold values from -8 to 8
- suffix_keys: bfloat16 [16, 128, 8, 128], P('ctx', None, 'head'), may hold values from -32 to 32
- suffix_values: bfloat16 [16, 128, 8, 128], P('ctx', None, 'head'), may hold values from -12 to 12
Outputs:
- attn_out: bfloat16 [16, 2, 16384], P('head', None, 'ctx')
Inputs may be any that keep to these rules, and one draw needn't show every extreme that they name: Sequence b's suffix cache holds its tokens in slots 0 .. suffix_lengths[b] - 1; some sequence fills all 128 slots.
All inputs are finite; a program needn't handle non-finite values.
Results may differ from a plain program's by a relative error of at most 0.02.
Values may be sent and summed in bfloat16 or wider, within the bound.
No kernel may reach another device: no remote copies, remote signals or barrier semaphores. Data moves between devices by JAX's collectives and lax.ppermute only.
A program may use at most 128 MiB of HBM per device.

v0:
```python
import jax
import jax.numpy as jnp
from jax import lax
from jax.sharding import PartitionSpec as P

EPSILON = 1e-05
ROTARY_THETA = 500000.0
MASKED = -1e30


def combined_all(part, axis, combine):
    gathered = jax.tree.map(lambda a: lax.all_gather(a, axis), part)

    def take(source):
        return jax.tree.map(lambda a: lax.dynamic_index_in_dim(a, source, 0, False), gathered)

    return lax.fori_loop(
        1, lax.axis_size(axis), lambda source, state: combine(state, take(source)), take(0)
    )


def rotary(vectors, positions):
    half_width = vectors.shape[-1] // 2
    frequency = ROTARY_THETA ** (
        -2.0 * jnp.arange(half_width).astype(jnp.float32) / vectors.shape[-1]
    )
    angles = positions[..., None] * frequency
    cosine = jnp.cos(angles)
    sine_values = jnp.sin(angles)
    front_half = vectors[..., :half_width]
    back_half = vectors[..., half_width:]
    return jnp.concatenate(
        [
            front_half * cosine - back_half * sine_values,
            back_half * cosine + front_half * sine_values,
        ],
        axis=-1,
    )


def combine(earlier, later):
    highest = jnp.maximum(earlier[0], later[0])
    first_scale = jnp.exp(earlier[0] - highest)
    second_scale = jnp.exp(later[0] - highest)
    return (
        highest,
        earlier[1] * first_scale + later[1] * second_scale,
        earlier[2] * first_scale[..., None] + later[2] * second_scale[..., None],
    )


def weigh_scores(scores):
    maxima = jnp.max(scores, axis=-1)
    weights = jnp.exp(scores - maxima[..., None]).astype(jnp.bfloat16)
    return (maxima, weights, jnp.sum(weights.astype(jnp.float32), axis=-1))


def lookup_rows(step_tokens, embedding):
    local_rows = embedding.shape[0]
    offsets = step_tokens - lax.axis_index("ctx") * local_rows
    inside_range = (offsets >= 0) & (offsets < local_rows)
    picked = jnp.take(embedding, jnp.clip(offsets, 0, local_rows - 1), axis=0)
    picked = jnp.where(inside_range[..., None], picked, jnp.zeros((), jnp.bfloat16))
    return lax.psum(picked, "ctx").astype(jnp.float32).astype(jnp.bfloat16)


def project(embedded, attn_gain, qkv_weight):
    features = embedded.astype(jnp.float32)
    square_sum = lax.psum(jnp.sum(features * features, axis=-1), "head")
    model_width = features.shape[-1] * lax.axis_size("head")
    normed = (
        features * lax.rsqrt(square_sum / model_width + EPSILON)[..., None] * attn_gain
    ).astype(jnp.bfloat16)
    flattened_rows = normed.reshape(-1, normed.shape[-1])
    local_heads = qkv_weight.shape[1] // lax.axis_size("head")

    def partial_summand(start, count):
        return jnp.einsum(
            "rd,dgf->grf", flattened_rows, qkv_weight, preferred_element_type=jnp.float32
        )

    summed = lax.psum_scatter(
        partial_summand(jnp.int32(0), lax.axis_size("head") * local_heads),
        "head",
        scatter_dimension=0,
        tiled=True,
    )
    return lax.all_gather(summed.astype(jnp.bfloat16), "ctx", axis=2, tiled=True)


def prefix_portion(flat_queries, prefix_keys, prefix_values):

    def one_head(operands):
        queries_block, keys_block, values_block = operands
        scores = jnp.einsum(
            "qd,kd->qk", queries_block, keys_block, preferred_element_type=jnp.float32
        )
        maxima, weights, totals = weigh_scores(scores)
        return (maxima, totals, jnp.dot(weights, values_block, preferred_element_type=jnp.float32))

    return lax.map(one_head, (flat_queries, prefix_keys, prefix_values))


def attend(
    qkv_rows,
    first_step,
    suffix_lengths,
    prefix_keys,
    prefix_values,
    suffix_keys,
    suffix_values,
    seen_keys,
    seen_values,
):
    local_heads, step_count, batch_rows, united_width = qkv_rows.shape
    head_dim = prefix_keys.shape[-1]
    query_width = united_width - 2 * head_dim
    group_size = query_width // head_dim
    queries = qkv_rows[..., :query_width].reshape(
        local_heads, step_count, batch_rows, group_size, head_dim
    )
    new_keys = qkv_rows[..., query_width : query_width + head_dim]
    new_values = qkv_rows[..., query_width + head_dim :]
    context = prefix_keys.shape[1] * lax.axis_size("ctx")
    step_index = first_step + jnp.arange(step_count, dtype=jnp.int32)
    positions = (context + suffix_lengths[None, :] + step_index[:, None]).astype(jnp.float32)
    queries_rot = (
        rotary(queries.astype(jnp.float32), positions[None, :, :, None]) * head_dim ** (-0.5)
    ).astype(jnp.bfloat16)
    keys_rot = rotary(new_keys.astype(jnp.float32), positions[None]).astype(jnp.bfloat16)
    maxima, totals, numerators = prefix_portion(
        queries_rot.reshape(local_heads, -1, head_dim), prefix_keys, prefix_values
    )
    maxima = maxima.reshape(local_heads, step_count, batch_rows, group_size)
    totals = totals.reshape(local_heads, step_count, batch_rows, group_size)
    numerators = numerators.reshape(local_heads, step_count, batch_rows, group_size, head_dim)
    owned_rows = suffix_keys.shape[0]
    own_start = lax.axis_index("ctx") * owned_rows
    own_queries = lax.dynamic_slice_in_dim(queries_rot, own_start, owned_rows, 2)
    own_lengths = lax.dynamic_slice_in_dim(suffix_lengths, own_start, owned_rows, 0)
    seen_keys = jnp.concatenate(
        [seen_keys, lax.dynamic_slice_in_dim(keys_rot, own_start, owned_rows, 2)], axis=1
    )
    seen_values = jnp.concatenate(
        [seen_values, lax.dynamic_slice_in_dim(new_values, own_start, owned_rows, 2)], axis=1
    )
    slot_count = suffix_keys.shape[1]
    near_scores = jnp.einsum(
        "gtbjd,bsgd->gtbjs", own_queries, suffix_keys, preferred_element_type=jnp.float32
    )
    live_slots = jnp.arange(slot_count, dtype=jnp.int32)[None, :] < own_lengths[:, None]
    near_scores = jnp.where(live_slots[None, None, :, None, :], near_scores, MASKED)
    fresh_scores = jnp.einsum(
        "gtbjd,gubd->gtbju", own_queries, seen_keys, preferred_element_type=jnp.float32
    )
    visible = jnp.arange(seen_keys.shape[1], dtype=jnp.int32)[None, :] <= step_index[:, None]
    fresh_scores = jnp.where(visible[None, :, None, None, :], fresh_scores, MASKED)
    nearby_maxima, weights, near_totals = weigh_scores(
        jnp.concatenate([near_scores, fresh_scores], axis=-1)
    )
    near_numerators = jnp.einsum(
        "gtbjs,bsgd->gtbjd",
        weights[..., :slot_count],
        suffix_values,
        preferred_element_type=jnp.float32,
    )
    near_numerators = near_numerators + jnp.einsum(
        "gtbju,gubd->gtbjd",
        weights[..., slot_count:],
        seen_values,
        preferred_element_type=jnp.float32,
    )
    own_part = (
        lax.dynamic_slice_in_dim(maxima, own_start, owned_rows, 2),
        lax.dynamic_slice_in_dim(totals, own_start, owned_rows, 2),
        lax.dynamic_slice_in_dim(numerators, own_start, owned_rows, 2),
    )
    joined = combine(own_part, (nearby_maxima, near_totals, near_numerators))
    maxima = lax.dynamic_update_slice_in_dim(maxima, joined[0], own_start, 2)
    totals = lax.dynamic_update_slice_in_dim(totals, joined[1], own_start, 2)
    numerators = lax.dynamic_update_slice_in_dim(numerators, joined[2], own_start, 2)
    maxima, totals, numerators = combined_all((maxima, totals, numerators), "ctx", combine)
    attention = (numerators / totals[..., None]).astype(jnp.bfloat16)
    return (attention, seen_keys, seen_values)


def project_out(attention, out_weight):
    local_heads, step_count, batch_rows, group_size, head_dim = attention.shape
    flattened_heads = attention.reshape(local_heads, step_count, batch_rows, group_size * head_dim)
    head_weights = out_weight.reshape(local_heads, group_size * head_dim, out_weight.shape[1])
    per_device = batch_rows // lax.axis_size("head")

    def partial_summand(start, count):
        return jnp.einsum(
            "lmie,len->imn", flattened_heads, head_weights, preferred_element_type=jnp.float32
        )

    return lax.psum_scatter(
        partial_summand(jnp.int32(0), lax.axis_size("head") * per_device).astype(jnp.bfloat16),
        "head",
        scatter_dimension=0,
        tiled=True,
    )


def body(
    token_ids,
    suffix_lengths,
    embedding,
    attn_gain,
    qkv_weight,
    out_weight,
    prefix_keys,
    prefix_values,
    suffix_keys,
    suffix_values,
):
    total_steps = token_ids.shape[0]
    batch_rows = token_ids.shape[1]
    local_heads = prefix_keys.shape[0]
    head_dim = prefix_keys.shape[-1]
    step_groups = (0, total_steps)
    seen_keys = jnp.zeros((local_heads, 0, suffix_keys.shape[0], head_dim), jnp.bfloat16)
    seen_values = jnp.zeros((local_heads, 0, suffix_keys.shape[0], head_dim), jnp.bfloat16)
    first_step, step_count = step_groups
    embedded = lookup_rows(token_ids, embedding)
    qkv_rows = project(embedded, attn_gain, qkv_weight)
    qkv_rows = qkv_rows.reshape(local_heads, step_count, batch_rows, qkv_rows.shape[-1])
    attention, seen_keys, seen_values = attend(
        qkv_rows,
        first_step,
        suffix_lengths,
        prefix_keys,
        prefix_values,
        suffix_keys,
        suffix_values,
        seen_keys,
        seen_values,
    )
    results = project_out(attention, out_weight)
    return results


def solution(mesh):
    placed = (
        P(),
        P(),
        P("ctx", "head"),
        P("head"),
        P("head", None, "ctx"),
        P("head", "ctx"),
        P("head", "ctx", None),
        P("head", "ctx", None),
        P("ctx", None, "head", None),
        P("ctx", None, "head", None),
    )
    return jax.shard_map(
        body, mesh=mesh, in_specs=placed, out_specs=P("head", None, "ctx"), check_vma=False
    )
```

profile of v0, /device:TPU:0, one launch (start us, length us, event | category | flops | bytes accessed | tf_op | source)
XLA Modules:
  0.0 286.2 jit_solution(10977653401740873123)
XLA Ops:
  7.4 2.6 gather_fusion
  9.9 0.8 select_select_fusion
  11.5 0.7 dynamic_slice.74
  12.4 73.3 %all-reduce.4.cloned.1.call-done = bf16[2,16,4096]{2,1,0:T(8,128)(2,1)} async-done(((bf16[2,16,4096]{2,1,0:T(8,128)(2,1)}), bf16[2,16,4096]{2,1,0:T(8,128)(2,1)}) %all-reduce.4.cloned.1.call-update) | async-done | bytes 262160 | tf_op jit(solution)/shard_map/psum | solution.py:64
  85.7 1.1 fusion.21
  86.8 5.7 %psum.15 = f32[2,16]{1,0:T(2,128)S(1)} all-reduce(f32[2,16]{1,0:T(2,128)S(1)} %fusion.21), channel_id=1, replica_groups=mesh['head'=4,'ctx'=8] {'head'}, use_global_device_ids=true, to_apply=%region_2.3 | all-reduce | flops 32 | bytes 256 | tf_op jit(solution)/shard_map/psum | solution.py:69
  92.4 1.1 fusion.23
  93.5 8.1 %convolution_bitcast_fusion.2 = f32[8,32,160]{2,1,0:T(8,128)} fusion(bf16[32,4096,1]{1,0,2:T(8,128)(2,1)S(1)} %bitcast.139, bf16[4096,8,160]{0,2,1:T(8,128)(2,1)} %param.18), kind=kOutput, calls=%fused_computation.25 | convolution fusion | flops 335544320 | bytes 10911744 | tf_op jit(solution)/shard_map/rd,dgf->grf/dot_general | solution.py:78
  102.0 19.3 %reduce-scatter.3.cloned.1.call-done = f32[2,32,160]{2,1,0:T(8,128)} async-done(((f32[8,32,160]{2,1,0:T(8,128)}), f32[2,32,160]{2,1,0:T(8,128)}) %reduce-scatter.3.cloned.1.call-update) | async-done | bytes 40976 | tf_op jit(solution)/shard_map/reduce_scatter | solution.py:82
  121.3 0.8 convert_element_type.73
  122.2 32.0 %all_gather.27 = bf16[2,32,1280]{1,0,2:T(2,128)(2,1)S(1)} all-gather(bf16[2,32,160]{1,0,2:T(2,128)(2,1)S(1)} %copy.73), channel_id=1, replica_groups=mesh['head'=4,'ctx'=8] {'ctx'}, dimensions={2}, use_global_device_ids=true | all-gather | bytes 184320 | tf_op jit(solution)/shard_map/all_gather | solution.py:88
  155.5 9.6 %while.33 = (s32[]{:T(128)}, f32[2,256]{1,0:T(2,128)S(1)}, f32[2,256]{1,0:T(2,128)S(1)}, f32[2,256,128]{2,1,0:T(8,128)S(1)}, bf16[2,256,128]{2,1,0:T(8,128)(2,1)...) while((s32[]{:T(128)}, f32[2,256]{1,0:T(2,128)S(1)}, ...), condition=%wide.region_7.8_spmd, body=%wide.region_4.7_spmd.sunk | while | flops 542113280 | bytes 14885997 | solution.py:101
  155.5 2.0 fusion.61
  157.5 0.8 convert_reduce_fusion.3
  158.3 1.9 fusion.62
  160.3 2.0 fusion.61
  162.3 0.8 convert_reduce_fusion.3
  163.1 1.9 fusion.62
  167.5 30.8 %all_gather.33 = f32[8,2,2,16,8]{3,4,2,1,0:T(8,128)S(1)} all-gather(f32[1,2,2,16,8]{3,4,2,1,0:T(8,128)S(1)} %copy.86), channel_id=1, replica_groups=mesh['head'=4,'ctx'=8] {'ctx'}, dimensions={0}, use_global_device_ids=true | all-gather | bytes 18432 | tf_op jit(solution)/shard_map/all_gather | solution.py:12
  198.4 30.9 %all_gather.30 = f32[8,2,2,16,8]{3,4,2,1,0:T(8,128)S(1)} all-gather(f32[1,2,2,16,8]{3,4,2,1,0:T(8,128)S(1)} %copy.83), channel_id=1, replica_groups=mesh['head'=4,'ctx'=8] {'ctx'}, dimensions={0}, use_global_device_ids=true | all-gather | bytes 18432 | tf_op jit(solution)/shard_map/all_gather | solution.py:12
  229.4 1.0 slice_bitcast_fusion
  230.3 9.9 %while.34 = (s32[]{:T(128)}, f32[2,2,16,8]{2,3,1,0:T(8,128)S(1)}, f32[2,2,16,8]{2,3,1,0:T(8,128)S(1)}, f32[2,2,16,8,128]{4,3,2,1,0:T(8,128)S(1)}, f32[8,2,2,16,8...) while((s32[]{:T(128)}, f32[2,2,16,8]{2,3,1,0:T(8,128)S(1)}, ...), condition=%wide.region_12.13_spmd, body=%wide.region_11.12_spmd.sunk | while | flops 199685 | bytes 815247 | solution.py:17
  230.5 1.2 fusion.64
  231.9 1.2 fusion.64
  233.3 1.2 fusion.64
  234.8 1.2 fusion.64
  236.2 1.2 fusion.64
  237.6 1.2 fusion.64
  239.0 1.2 fusion.64
  240.5 5.6 %fusion.14 = bf16[16,2,2048]{2,0,1:T(8,128)(2,1)} fusion(bf16[2,2,16,1024]{3,2,1,0:T(8,128)(2,1)S(1)} %reshape.165, bf16[2,1024,2048,1]{2,1,3,0:T(8,128)(2,1)} %bitcast.136), kind=kOutput, calls=%fused_computation.24 | convolution fusion | flops 268500992 | bytes 8650752 | tf_op jit(solution)/shard_map/lmie,len->imn/dot_general | solution.py:194
  247.4 30.7 %all-reduce.6.cloned.1.call-done = bf16[16,2,2048]{2,0,1:T(8,128)(2,1)} async-done(((bf16[16,2,2048]{2,0,1:T(8,128)(2,1)}), bf16[16,2,2048]{2,0,1:T(8,128)(2,1)}) %all-reduce.6.cloned.1.call-update) | async-done | bytes 131088
  278.1 0.9 constant_dynamic-slice_fusion.4
  (94 shorter events, 8.5 us)
Async XLA Ops:
  6.5 158.8 %copy-start = (bf16[2,128,2,128]{3,2,1,0:T(2,128)(2,1)S(1)}, bf16[2,128,2,128]{3,2,1,0:T(2,128)(2,1)}, u32[]{:S(2)}) copy-start(bf16[2,128,2,128]{3,2,1,0:T(2,128)(2,1)} %param.22) | copy-start | bytes 393220
  6.5 79.2 %all-reduce.4.cloned.1.call-start = ((), (), s32[]{:S(2)}) async-start(), calls=%async_computation.1 | async-start | bytes 524288 | tf_op jit(solution)/shard_map/psum | solution.py:64
  10.8 110.5 %reduce-scatter.3.cloned.1.call-start = ((), (), s32[]{:S(2)}) async-start(), calls=%async_computation.2 | async-start | bytes 327680 | tf_op jit(solution)/shard_map/reduce_scatter | solution.py:82
  101.6 127.7 %all-gather.2.cloned.1.call-start = ((), (), s32[]{:S(2)}) async-start(), calls=%async_computation.3 | async-start | bytes 2359296 | tf_op jit(solution)/shard_map/all_gather | solution.py:12
  155.4 10.6 %copy-start.2 = (bf16[2,128,2,128]{3,2,1,0:T(2,128)(2,1)S(1)}, bf16[2,128,2,128]{3,2,1,0:T(2,128)(2,1)}, u32[]{:S(2)}) copy-start(bf16[2,128,2,128]{3,2,1,0:T(2,128)(2,1)} %param.23) | copy-start | bytes 393220
  166.4 0.7 copy-start.1
  167.1 111.0 %all-reduce.6.cloned.1.call-start = ((), (), s32[]{:S(2)}) async-start(), calls=%async_computation.4 | async-start | bytes 262144
  240.5 5.6 %copy-start.3 = (u32[32]{0:T(128)S(1)}, u32[32]{0:T(128)}, u32[]{:S(2)}) copy-start(u32[32]{0:T(128)} %constant.135) | copy-start | bytes 388
Sparse Core Ops, SparseCore 0:
  10.9 74.7 all-reduce.3
  101.8 19.4 reduce-scatter.2
  167.3 50.6 all-gather.1
  246.3 31.8 all-reduce.5
where the time goes:
time: 287 us; the launch traced here: 286 us
  waiting for transfers between devices  123 us (43%)
  blocking collectives  99.4 us (35%)
  matrix products  22.4 us (8%)
  other arithmetic  16.7 us (6%)
  between operations  14.1 us (5%)
  local copies, waits for them, and re-layouts  9.79 us (3%)
    psum x1, waiting for transfers between devices, lookup_rows(): return lax.psum(picked, 'ctx').astype(jnp.float32).astype(jnp.bfloat16)  73.3 us
    all_gather x2, blocking collectives, combined_all(): gathered = jax.tree.map(lambda a: lax.all_gather(a, axis), part)  61.8 us
    all_gather x1, blocking collectives, project(): lax.all_gather(summed.astype(jnp.bfloat16), 'ctx', axis=2, tiled=True)  32 us
    unnamed x5, waiting for transfers between devices  30.8 us
    reduce_scatter x1, waiting for transfers between devices, project(): lax.psum_scatter(partial_summand(jnp.int32(0), lax.axis_size('head') * lo...  19.3 us
    add x7, other arithmetic, combine(): earlier[2] * first_scale[..., None] + later[2] * second_scale[..., None]  8.51 us
    dot_general x1, matrix products, partial_summand(): jnp.einsum('rd,dgf->grf', flattened_rows, qkv_weight, preferred_element_t...  8.08 us
  transfers between devices with their start and end apart: 4, of which 3 were waited for; matrix products, arithmetic and copies ran while one was open for 1% of the time, Pallas kernels for 0%

commit v1 on v0

v1 whole, which is shorter than its diff:
```python
import jax
import jax.numpy as jnp
from jax import lax
from jax.sharding import PartitionSpec as P

EPSILON = 1e-05
ROTARY_THETA = 500000.0
MASKED = -1e30
BF16 = jnp.bfloat16
F32 = jnp.float32


def exchange(blocks, axis):
    return lax.all_to_all(blocks, axis, 0, 0)


def gather_all(block, axis):
    count = lax.axis_size(axis)
    return exchange(jnp.broadcast_to(block[None], (count,) + block.shape), axis)


def scatter_direct(blocks, axis):
    count = lax.axis_size(axis)
    here = lax.axis_index(axis)
    received = [lax.dynamic_index_in_dim(blocks, here, 0, False)]
    for shift in range(1, count):
        target = lax.rem(here + shift, count)
        piece = lax.dynamic_index_in_dim(blocks, target, 0, False)
        pairs = [(i, (i + shift) % count) for i in range(count)]
        received.append(lax.ppermute(piece, axis, pairs))
    return received


def rotary_tables(positions, head_dim):
    half_width = head_dim // 2
    frequency = ROTARY_THETA ** (-2.0 * jnp.arange(half_width).astype(F32) / head_dim)
    angles = positions[..., None] * frequency
    return jnp.cos(angles), jnp.sin(angles)


def rotate(vectors, cosine, sine):
    half_width = vectors.shape[-1] // 2
    front = vectors[..., :half_width]
    back = vectors[..., half_width:]
    return jnp.concatenate([front * cosine - back * sine, back * cosine + front * sine], axis=-1)


def body(
    token_ids,
    suffix_lengths,
    embedding,
    attn_gain,
    qkv_weight,
    out_weight,
    prefix_keys,
    prefix_values,
    suffix_keys,
    suffix_values,
):
    steps, batch = token_ids.shape
    rows = steps * batch
    n_ctx = lax.axis_size("ctx")
    n_head = lax.axis_size("head")
    local_heads, _, head_dim = prefix_keys.shape
    width = embedding.shape[1]
    slots = suffix_keys.shape[1]
    owned = suffix_keys.shape[0]
    mine = lax.axis_index("ctx")
    tokens = token_ids.T.reshape(rows)
    offsets = tokens - mine * embedding.shape[0]
    inside = (offsets >= 0) & (offsets < embedding.shape[0])
    picked = jnp.take(embedding, jnp.clip(offsets, 0, embedding.shape[0] - 1), axis=0)
    picked = jnp.where(inside[:, None], picked, jnp.zeros((), BF16))
    arrived = exchange(picked.reshape(n_ctx, rows // n_ctx, width), "ctx")
    chunk = jnp.sum(arrived.astype(F32), axis=0).astype(BF16)
    features = gather_all(chunk, "ctx").reshape(rows, width).astype(F32)
    square_sum = jnp.sum(features * features, axis=-1)
    scaled = (features * attn_gain).astype(BF16)
    partial = jnp.einsum("rd,dgf->grf", scaled, qkv_weight, preferred_element_type=F32)
    partial = partial.reshape(n_head, local_heads, rows, -1)
    square_sum = jnp.broadcast_to(square_sum[None, None, :, None], (n_head, local_heads, rows, 1))
    pieces = scatter_direct(jnp.concatenate([partial, square_sum], axis=-1), "head")
    total = sum(pieces[1:], pieces[0])
    factor = lax.rsqrt(total[..., -1:] / (width * n_head) + EPSILON)
    columns = (total[..., :-1] * factor).astype(BF16)
    united = gather_all(columns, "ctx")
    united = jnp.transpose(united, (1, 2, 0, 3)).reshape(local_heads, batch, steps, -1)
    query_width = united.shape[-1] - 2 * head_dim
    group = query_width // head_dim
    queries = united[..., :query_width].reshape(local_heads, batch, steps, group, head_dim)
    step_index = jnp.arange(steps, dtype=jnp.int32)
    context = prefix_keys.shape[1] * n_ctx
    positions = (context + suffix_lengths[:, None] + step_index[None, :]).astype(F32)
    cosine, sine = rotary_tables(positions, head_dim)
    queries = (
        rotate(queries.astype(F32), cosine[:, :, None], sine[:, :, None]) * head_dim ** (-0.5)
    ).astype(BF16)
    flat = queries.reshape(local_heads, rows * group, head_dim)
    scores = jnp.einsum("gqd,gkd->gqk", flat, prefix_keys, preferred_element_type=F32)
    maxima = jnp.max(scores, axis=-1, keepdims=True)
    weights = jnp.exp(scores - maxima).astype(BF16)
    totals = jnp.sum(weights.astype(F32), axis=-1, keepdims=True)
    sums = jnp.einsum("gqk,gkd->gqd", weights, prefix_values, preferred_element_type=F32)
    packet = jnp.concatenate([sums, maxima, totals], axis=-1)
    packet = packet.reshape(local_heads, n_ctx, -1, head_dim + 2)
    packet = jnp.swapaxes(packet, 0, 1)
    parts = exchange(packet, "ctx")
    own = mine * owned
    near_queries = lax.dynamic_slice_in_dim(queries, own, owned, 1)
    near_keys = rotate(united[..., query_width : query_width + head_dim].astype(F32), cosine, sine)
    near_keys = lax.dynamic_slice_in_dim(near_keys.astype(BF16), own, owned, 1)
    near_values = lax.dynamic_slice_in_dim(united[..., query_width + head_dim :], own, owned, 1)
    lengths = lax.dynamic_slice_in_dim(suffix_lengths, own, owned, 0)
    slot_scores = jnp.einsum(
        "gbtjd,bsgd->gbtjs", near_queries, suffix_keys, preferred_element_type=F32
    )
    live = jnp.arange(slots, dtype=jnp.int32)[None, :] < lengths[:, None]
    slot_scores = jnp.where(live[None, :, None, None, :], slot_scores, MASKED)
    fresh = jnp.einsum("gbtjd,gbud->gbtju", near_queries, near_keys, preferred_element_type=F32)
    visible = step_index[None, :] <= step_index[:, None]
    fresh = jnp.where(visible[None, None, :, None, :], fresh, MASKED)
    near_scores = jnp.concatenate([slot_scores, fresh], axis=-1)
    near_max = jnp.max(near_scores, axis=-1, keepdims=True)
    near_weights = jnp.exp(near_scores - near_max).astype(BF16)
    near_total = jnp.sum(near_weights.astype(F32), axis=-1, keepdims=True)
    near_sum = jnp.einsum(
        "gbtjs,bsgd->gbtjd", near_weights[..., :slots], suffix_values, preferred_element_type=F32
    ) + jnp.einsum(
        "gbtju,gbud->gbtjd", near_weights[..., slots:], near_values, preferred_element_type=F32
    )
    near = jnp.concatenate([near_sum, near_max, near_total], axis=-1).reshape(parts.shape[1:])
    everything = jnp.concatenate([parts, near[None]], axis=0)
    highest = jnp.max(everything[..., head_dim : head_dim + 1], axis=0, keepdims=True)
    scale = jnp.exp(everything[..., head_dim : head_dim + 1] - highest)
    numerator = jnp.sum(everything[..., :head_dim] * scale, axis=0)
    denominator = jnp.sum(everything[..., head_dim + 1 :] * scale, axis=0)
    attention = (numerator / denominator).astype(BF16)
    attention = attention.reshape(local_heads, owned * steps, group * head_dim)
    attention = gather_all(attention, "ctx")
    attention = jnp.transpose(attention, (0, 2, 1, 3)).reshape(rows, -1)
    out = jnp.dot(attention, out_weight, preferred_element_type=F32).astype(BF16)
    out = out.reshape(n_head, rows // n_head, -1)
    pieces = scatter_direct(out, "head")
    result = sum([p.astype(F32) for p in pieces[1:]], pieces[0].astype(F32)).astype(BF16)
    return result.reshape(batch // n_head, steps, -1)


def solution(mesh):
    placed = (
        P(),
        P(),
        P("ctx", "head"),
        P("head"),
        P("head", None, "ctx"),
        P("head", "ctx"),
        P("head", "ctx", None),
        P("head", "ctx", None),
        P("ctx", None, "head", None),
        P("ctx", None, "head", None),
    )
    return jax.shard_map(
        body, mesh=mesh, in_specs=placed, out_specs=P("head", None, "ctx"), check_vma=False
    )
```

time: 287 us -> 121 us (0.42)
  waiting for transfers between devices: 123 us -> 34.5 us
  blocking collectives: 99.4 us -> 28.1 us
  starting transfers between devices: 0.13 us -> 17 us
  between operations: 14.1 us -> 0.23 us
  other arithmetic: 16.7 us -> 10.8 us
    all_gather x3 -> x0, blocking collectives: 93.8 us -> none  [the longest x2 61.8 us: combined_all(): gathered = jax.tree.map(lambda a: lax.all_gather(a, axis), part)]
    psum x1 -> x0, waiting for transfers between devices: 73.3 us -> none  [lookup_rows(): return lax.psum(picked, 'ctx').astype(jnp.float32).astype(jnp.bfloat16)]
    unnamed x5 -> x0, waiting for transfers between devices: 30.8 us -> none
    all_to_all x0 -> x3, waiting for transfers between devices: none -> 30.1 us  [exchange(): return lax.all_to_all(blocks, axis, 0, 0)]
    all_to_all x0 -> x2, blocking collectives: none -> 28.1 us  [exchange(): return lax.all_to_all(blocks, axis, 0, 0)]
    reduce_scatter x1 -> x0, waiting for transfers between devices: 19.3 us -> none  [project(): lax.psum_scatter(partial_summand(jnp.int32(0), lax.axis_size('head') * lo...]
    all_to_all x0 -> x3, starting transfers between devices: none -> 10.7 us  [exchange(): return lax.all_to_all(blocks, axis, 0, 0)]
    add x16 -> x3, other arithmetic: 9.34 us -> 0.9 us  [the longest x1 0.66 us: body(): context + suffix_lengths[:, None] + step_index[None, :]]
  transfers between devices with their start and end apart: 4 -> 9, of which waited for: 3 -> 8; matrix products, arithmetic and copies ran while one was open for 1% -> 3% of each run, Pallas kernels for 0% -> 0%
where the time goes in v1:
time: 121 us; the launch traced here: 120 us
  waiting for transfers between devices  34.5 us (29%)
  blocking collectives  28.1 us (23%)
  matrix products  20.8 us (17%)
  starting transfers between devices  17 us (14%)
  other arithmetic  10.8 us (9%)
  local copies, waits for them, and re-layouts  8.56 us (7%)
    all_to_all x3, waiting for transfers between devices, exchange(): return lax.all_to_all(blocks, axis, 0, 0)  30.1 us
    all_to_all x2, blocking collectives, exchange(): return lax.all_to_all(blocks, axis, 0, 0)  28.1 us
    all_to_all x3, starting transfers between devices, exchange(): return lax.all_to_all(blocks, axis, 0, 0)  10.7 us
    dot_general x1, matrix products, body(): jnp.einsum('rd,dgf->grf', scaled, qkv_weight, preferred_element_type=F32)  7.39 us
    ppermute x6, starting transfers between devices, scatter_direct(): received.append(lax.ppermute(piece, axis, pairs))  6.25 us
    dot_general x1, matrix products, body(): jnp.dot(attention, out_weight, preferred_element_type=F32).astype(BF16)  4.93 us
    reduce_sum x1, other arithmetic, body(): totals = jnp.sum(weights.astype(F32), axis=-1, keepdims=True)  4.78 us
    dot_general x1, matrix products, body(): jnp.einsum('gqd,gkd->gqk', flat, prefix_keys, preferred_element_type=F32)  4.52 us
  transfers between devices with their start and end apart: 9, of which 8 were waited for; matrix products, arithmetic and copies ran while one was open for 3% of the time, Pallas kernels for 0%

profile of v1, /device:TPU:0, one launch (start us, length us, event | category | flops | bytes accessed | tf_op | source)
XLA Modules:
  0.0 120.0 jit_solution(16091819340436717762)
XLA Ops:
  0.0 0.8 and_bitcast_fusion
  0.8 0.7 clamp_bitcast_fusion
  2.0 2.4 %gather_fusion = bf16[32,4096]{1,0:T(8,128)(2,1)S(1)} fusion(bf16[8016,4096]{1,0:T(8,128)(2,1)} %param.12, s32[1024]{0:T(1024)S(1)} %pad_clamp_fusion), kind=kCustom, calls=%fused_computation | custom fusion | bytes 524416 | tf_op jit(solution)/shard_map/jit(_take)/gather | solution.py:72
  4.8 17.3 %all_to_all.25 = bf16[8,4,4096]{2,1,0:T(4,128)(2,1)S(1)} all-to-all(bf16[8,4,4096]{2,1,0:T(4,128)(2,1)S(1)} %select_select_fusion), channel_id=1, replica_groups=mesh['head'=4,'ctx'=8] {'ctx'}, dimensions={0} | all-to-all | bytes 524288 | tf_op jit(solution)/shard_map/all_to_all | solution.py:14
  22.2 0.8 broadcast_in_dim.60
  23.0 3.6 %all-to-all-start.1 = ((bf16[8,4,4096]{2,1,0:T(4,128)(2,1)}), bf16[8,4,4096]{2,1,0:T(4,128)(2,1)S(1)}, u32[]{:S(2)}, u32[]{:S(2)}) async-start(bf16[8,4,4096]{2,1,0:T(4,128)(2,1)} %broadcast_in_dim.60), calls=%async_computation.1 | async-start | bytes 524288 | tf_op jit(solution)/shard_map/all_to_all | solution.py:14
  26.6 0.7 broadcast_add_fusion
  27.2 0.7 dynamic_slice.42
  28.1 7.0 %all-to-all-done.1 = bf16[8,4,4096]{2,1,0:T(4,128)(2,1)S(1)} async-done(((bf16[8,4,4096]{2,1,0:T(4,128)(2,1)}), bf16[8,4,4096]{2,1,0:T(4,128)(2,1)S(1)}, u32[]{:S(2)}, u32[]{:S(2)}) %all-to-all-start.1) | async-done | bytes 262176 | tf_op jit(solution)/shard_map/all_to_all | solution.py:14
  35.5 7.4 %fusion.5 = f32[32,8,160]{2,0,1:T(8,128)S(1)} fusion(bf16[4096,8,160]{0,2,1:T(8,128)(2,1)} %param.14, f32[32,4096]{1,0:T(8,128)S(1)} %reshape.221, f32[4096]{0:T(1024)} %param.13), kind=kOutput, calls=%fused_computation.24 | convolution fusion | flops 335806464 | bytes 11190272 | tf_op jit(solution)/shard_map/rd,dgf->grf/dot_general | solution.py:79
  43.1 1.6 %collective-permute-start.1 = (f32[2,32,161]{2,1,0:T(8,128)S(1)}, f32[2,32,161]{2,1,0:T(8,128)S(1)}, u32[]{:S(2)}, u32[]{:S(2)}) collective-permute-start(f32[2,32,161]{2,1,0:T(8,128)S(1)} %get-tuple-element.10), channel_id=1, source_target_pairs={{0,16},{8,24},{16,0},{24,8},{1,17},{9,25},{17,1},{25,9},{2,18},{10... | collective-permute-start | bytes 123656 | tf_op jit(solution)/shard_map/ppermute | solution.py:30
  44.7 1.4 %collective-permute-start.2 = (f32[2,32,161]{2,1,0:T(8,128)S(1)}, f32[2,32,161]{2,1,0:T(8,128)S(1)}, u32[]{:S(2)}, u32[]{:S(2)}) collective-permute-start(f32[2,32,161]{2,1,0:T(8,128)S(1)} %get-tuple-element.11), channel_id=1, source_target_pairs={{0,24},{8,0},{16,8},{24,16},{1,25},{9,1},{17,9},{25,17},{2,26},{10... | collective-permute-start | bytes 123656 | tf_op jit(solution)/shard_map/ppermute | solution.py:30
  46.1 0.8 collective-permute-done
  46.9 0.8 collective-permute-done.1
  48.3 0.7 broadcast_in_dim.63
  49.1 3.6 %all-to-all-start.2 = ((bf16[8,2,32,160]{3,2,1,0:T(8,128)(2,1)}), bf16[8,2,32,160]{3,2,1,0:T(8,128)(2,1)S(1)}, u32[]{:S(2)}, u32[]{:S(2)}) async-start(bf16[8,2,32,160]{3,2,1,0:T(8,128)(2,1)} %broadcast_in_dim.63), calls=%async_computation.2 | async-start | bytes 524288 | tf_op jit(solution)/shard_map/all_to_all | solution.py:14
  53.0 9.6 %all-to-all-done.2 = bf16[8,2,32,160]{3,2,1,0:T(8,128)(2,1)S(1)} async-done(((bf16[8,2,32,160]{3,2,1,0:T(8,128)(2,1)}), bf16[8,2,32,160]{3,2,1,0:T(8,128)(2,1)S(1)}, u32[]{:S(2)}, u32[]{:S(2)}) %all-to-all-start.2) | async-done | bytes 163872 | tf_op jit(solution)/shard_map/all_to_all | solution.py:14
  62.7 0.4 reshape.217
  63.8 4.5 %fusion.54 = (f32[2,256]{1,0:T(2,128)S(1)}, f32[2,256,4096]{2,1,0:T(8,128)}) fusion(bf16[2,4096,128]{2,1,0:T(8,128)(2,1)S(1)} %copy-done, f32[2,256,64]{2,1,0:T(8,128)S(1)} %bitcast.73, f32[2,256,64]{2,1,0:T(8,128)S(1)} %bitcast.74), kind=kOutput, calls=%fused_computation.107 | convolution fusion | flops 539164160 | bytes 10749952 | tf_op jit(solution)/shard_map/gqd,gkd->gqk/dot_general | solution.py:99
  68.4 4.8 %convert_reduce_fusion = f32[2,256]{1,0:T(2,128)S(1)} fusion(f32[2,256,4096]{2,1,0:T(8,128)} %get-tuple-element.28, f32[2,256]{1,0:T(2,128)S(1)} %get-tuple-element.27), kind=kLoop, calls=%fused_computation.1 | loop fusion | flops 8388096 | bytes 8392704 | tf_op jit(solution)/shard_map/reduce_sum | solution.py:102
  73.2 1.0 copy-done.2
  74.2 3.2 %fusion.1 = f32[2,256,128]{2,1,0:T(8,128)S(1)} fusion(bf16[2,4096,128]{2,1,0:T(8,128)(2,1)} %param.17, f32[2,256,4096]{2,1,0:T(8,128)S(1)} %copy-done.2, f32[2,256]{1,0:T(2,128)S(1)} %get-tuple-element.27), kind=kOutput, calls=%fused_computation.8 | convolution fusion | flops 541065216 | bytes 10749952 | tf_op jit(solution)/shard_map/gqk,gkd->gqd/dot_general | solution.py:103
  77.8 0.9 maximum_bitcast_fusion
  78.7 3.6 %all-to-all-start.3 = ((f32[8,2,32,130]{3,2,1,0:T(8,128)}), f32[8,2,32,130]{3,2,1,0:T(8,128)S(1)}, u32[]{:S(2)}, u32[]{:S(2)}) async-start(f32[8,2,32,130]{3,2,1,0:T(8,128)} %maximum_bitcast_fusion), calls=%async_computation.3 | async-start | bytes 1048576 | tf_op jit(solution)/shard_map/all_to_all | solution.py:14
  83.4 13.5 %all-to-all-done.3 = f32[8,2,32,130]{3,2,1,0:T(8,128)S(1)} async-done(((f32[8,2,32,130]{3,2,1,0:T(8,128)}), f32[8,2,32,130]{3,2,1,0:T(8,128)S(1)}, u32[]{:S(2)}, u32[]{:S(2)}) %all-to-all-start.3) | async-done | bytes 266272 | tf_op jit(solution)/shard_map/all_to_all | solution.py:14
  97.2 0.3 fusion.2
  97.9 10.8 %all_to_all.26 = bf16[8,2,4,1024]{3,1,2,0:T(2,128)(2,1)S(1)} all-to-all(bf16[8,2,4,1024]{3,1,2,0:T(2,128)(2,1)S(1)} %broadcast_in_dim.104), channel_id=1, replica_groups=mesh['head'=4,'ctx'=8] {'ctx'}, dimensions={0} | all-to-all | bytes 262144 | tf_op jit(solution)/shard_map/all_to_all | solution.py:14
  108.7 4.9 %fusion = bf16[4,8,2048]{2,1,0:T(8,128)(2,1)S(1)} fusion(bf16[32,2048]{1,0:T(8,128)(2,1)S(1)} %bitcast.77, bf16[2048,2048]{1,0:T(8,128)(2,1)} %param.15), kind=kOutput, calls=%fused_computation.4 | convolution fusion | flops 268500992 | bytes 8650752 | tf_op jit(solution)/shard_map/dot_general | solution.py:141
  113.7 1.7 %collective-permute-start.5 = (bf16[8,2048]{1,0:T(8,128)(2,1)S(1)}, bf16[8,2048]{1,0:T(8,128)(2,1)S(1)}, u32[]{:S(2)}, u32[]{:S(2)}) collective-permute-start(bf16[8,2048]{1,0:T(8,128)(2,1)S(1)} %get-tuple-element.17), channel_id=1, source_target_pairs={{0,24},{8,0},{16,8},{24,16},{1,25},{9,1},{17,9},{25,17},{2,26},{10... | collective-permute-start | bytes 98312 | tf_op jit(solution)/shard_map/ppermute | solution.py:30
  115.4 1.5 %collective-permute-start.4 = (bf16[8,2048]{1,0:T(8,128)(2,1)S(1)}, bf16[8,2048]{1,0:T(8,128)(2,1)S(1)}, u32[]{:S(2)}, u32[]{:S(2)}) collective-permute-start(bf16[8,2048]{1,0:T(8,128)(2,1)S(1)} %get-tuple-element.18), channel_id=1, source_target_pairs={{0,16},{8,24},{16,0},{24,8},{1,17},{9,25},{17,1},{25,9},{2,18},{10... | collective-permute-start | bytes 98312 | tf_op jit(solution)/shard_map/ppermute | solution.py:30
  117.0 2.3 %collective-permute-done.4 = bf16[8,2048]{1,0:T(8,128)(2,1)S(1)} collective-permute-done((bf16[8,2048]{1,0:T(8,128)(2,1)S(1)}, bf16[8,2048]{1,0:T(8,128)(2,1)S(1)}, u32[]{:S(2)}, u32[]{:S(2)}) %collective-permute-start.4) | collective-permute-done | bytes 32800 | tf_op jit(solution)/shard_map/ppermute | solution.py:30
  119.4 0.6 reshape.220
  (67 shorter events, 5.9 us)
Async XLA Ops:
  0.0 63.8 %copy-start = (bf16[2,4096,128]{2,1,0:T(8,128)(2,1)S(1)}, bf16[2,4096,128]{2,1,0:T(8,128)(2,1)}, u32[]{:S(2)}) copy-start(bf16[2,4096,128]{2,1,0:T(8,128)(2,1)} %param.16) | copy-start | bytes 6291460
  23.0 12.2 %all-to-all-start.1 = ((bf16[8,4,4096]{2,1,0:T(4,128)(2,1)}), bf16[8,4,4096]{2,1,0:T(4,128)(2,1)S(1)}, u32[]{:S(2)}, u32[]{:S(2)}) async-start(bf16[8,4,4096]{2,1,0:T(4,128)(2,1)} %broadcast_in_dim.60), calls=%async_computation.1 | async-start | bytes 524288 | tf_op jit(solution)/shard_map/all_to_all | solution.py:14
  43.1 3.8 %collective-permute-start = (f32[2,32,161]{2,1,0:T(8,128)S(1)}, f32[2,32,161]{2,1,0:T(8,128)S(1)}, u32[]{:S(2)}, u32[]{:S(2)}) collective-permute-start(f32[2,32,161]{2,1,0:T(8,128)S(1)} %get-tuple-element.9), channel_id=1, source_target_pairs={{0,8},{8,16},{16,24},{24,0},{1,9},{9,17},{17,25},{25,1},{2,10},{10... | collective-permute-start | bytes 123656 | tf_op jit(solution)/shard_map/ppermute | solution.py:30
  43.1 4.6 %collective-permute-start.1 = (f32[2,32,161]{2,1,0:T(8,128)S(1)}, f32[2,32,161]{2,1,0:T(8,128)S(1)}, u32[]{:S(2)}, u32[]{:S(2)}) collective-permute-start(f32[2,32,161]{2,1,0:T(8,128)S(1)} %get-tuple-element.10), channel_id=1, source_target_pairs={{0,16},{8,24},{16,0},{24,8},{1,17},{9,25},{17,1},{25,9},{2,18},{10... | collective-permute-start | bytes 123656 | tf_op jit(solution)/shard_map/ppermute | solution.py:30
  44.7 3.3 %collective-permute-start.2 = (f32[2,32,161]{2,1,0:T(8,128)S(1)}, f32[2,32,161]{2,1,0:T(8,128)S(1)}, u32[]{:S(2)}, u32[]{:S(2)}) collective-permute-start(f32[2,32,161]{2,1,0:T(8,128)S(1)} %get-tuple-element.11), channel_id=1, source_target_pairs={{0,24},{8,0},{16,8},{24,16},{1,25},{9,1},{17,9},{25,17},{2,26},{10... | collective-permute-start | bytes 123656 | tf_op jit(solution)/shard_map/ppermute | solution.py:30
  49.1 13.5 %all-to-all-start.2 = ((bf16[8,2,32,160]{3,2,1,0:T(8,128)(2,1)}), bf16[8,2,32,160]{3,2,1,0:T(8,128)(2,1)S(1)}, u32[]{:S(2)}, u32[]{:S(2)}) async-start(bf16[8,2,32,160]{3,2,1,0:T(8,128)(2,1)} %broadcast_in_dim.63), calls=%async_computation.2 | async-start | bytes 524288 | tf_op jit(solution)/shard_map/all_to_all | solution.py:14
  68.4 5.8 %copy-start.2 = (f32[2,256,4096]{2,1,0:T(8,128)S(1)}, f32[2,256,4096]{2,1,0:T(8,128)}, u32[]{:S(2)}) copy-start(f32[2,256,4096]{2,1,0:T(8,128)} %get-tuple-element.28) | copy-start | bytes 25165828
  74.2 8.1 %copy-start.3 = (bf16[2,128,2,128]{3,2,1,0:T(2,128)(2,1)S(1)}, bf16[2,128,2,128]{3,2,1,0:T(2,128)(2,1)}, u32[]{:S(2)}) copy-start(bf16[2,128,2,128]{3,2,1,0:T(2,128)(2,1)} %param.18) | copy-start | bytes 393220
  74.2 9.0 %copy-start.4 = (bf16[2,128,2,128]{3,2,1,0:T(2,128)(2,1)S(1)}, bf16[2,128,2,128]{3,2,1,0:T(2,128)(2,1)}, u32[]{:S(2)}) copy-start(bf16[2,128,2,128]{3,2,1,0:T(2,128)(2,1)} %param.19) | copy-start | bytes 393220
  78.7 18.3 %all-to-all-start.3 = ((f32[8,2,32,130]{3,2,1,0:T(8,128)}), f32[8,2,32,130]{3,2,1,0:T(8,128)S(1)}, u32[]{:S(2)}, u32[]{:S(2)}) async-start(f32[8,2,32,130]{3,2,1,0:T(8,128)} %maximum_bitcast_fusion), calls=%async_computation.3 | async-start | bytes 1048576 | tf_op jit(solution)/shard_map/all_to_all | solution.py:14
  97.2 22.8 %copy-start.1 = (bf16[2,4096,128]{2,1,0:T(8,128)(2,1)S(1)}, bf16[2,4096,128]{2,1,0:T(8,128)(2,1)}, u32[]{:S(2)}) copy-start(bf16[2,4096,128]{2,1,0:T(8,128)(2,1)} %param.16) | copy-start | bytes 6291460
  113.6 3.4 %collective-permute-start.3 = (bf16[8,2048]{1,0:T(8,128)(2,1)S(1)}, bf16[8,2048]{1,0:T(8,128)(2,1)S(1)}, u32[]{:S(2)}, u32[]{:S(2)}) collective-permute-start(bf16[8,2048]{1,0:T(8,128)(2,1)S(1)} %get-tuple-element.16), channel_id=1, source_target_pairs={{0,8},{8,16},{16,24},{24,0},{1,9},{9,17},{17,25},{25,1},{2,10},{10... | collective-permute-start | bytes 98312 | tf_op jit(solution)/shard_map/ppermute | solution.py:30
  113.7 3.3 %collective-permute-start.5 = (bf16[8,2048]{1,0:T(8,128)(2,1)S(1)}, bf16[8,2048]{1,0:T(8,128)(2,1)S(1)}, u32[]{:S(2)}, u32[]{:S(2)}) collective-permute-start(bf16[8,2048]{1,0:T(8,128)(2,1)S(1)} %get-tuple-element.17), channel_id=1, source_target_pairs={{0,24},{8,0},{16,8},{24,16},{1,25},{9,1},{17,9},{25,17},{2,26},{10... | collective-permute-start | bytes 98312 | tf_op jit(solution)/shard_map/ppermute | solution.py:30
  115.4 3.9 %collective-permute-start.4 = (bf16[8,2048]{1,0:T(8,128)(2,1)S(1)}, bf16[8,2048]{1,0:T(8,128)(2,1)S(1)}, u32[]{:S(2)}, u32[]{:S(2)}) collective-permute-start(bf16[8,2048]{1,0:T(8,128)(2,1)S(1)} %get-tuple-element.18), channel_id=1, source_target_pairs={{0,16},{8,24},{16,0},{24,8},{1,17},{9,25},{17,1},{25,9},{2,18},{10... | collective-permute-start | bytes 98312 | tf_op jit(solution)/shard_map/ppermute | solution.py:30

commit v2 on v1

v2 whole, which is shorter than its diff:
```python
import functools

import jax
import jax.numpy as jnp
from jax import lax
from jax.experimental import pallas as pl
from jax.experimental.pallas import tpu as pltpu
from jax.sharding import PartitionSpec as P

EPSILON = 1e-05
ROTARY_THETA = 500000.0
MASKED = -1e30
BF16 = jnp.bfloat16
F32 = jnp.float32
LANES = 128
MIB = 1 << 20
VMEM = pl.BlockSpec(memory_space=pltpu.VMEM)
SMEM = pl.BlockSpec(memory_space=pltpu.SMEM)
HBM = pl.BlockSpec(memory_space=pl.ANY)
NT = (((1,), (1,)), ((), ()))


def round_up(value, unit):
    return -(-value // unit) * unit


def params(limit):
    return pltpu.CompilerParams(vmem_limit_bytes=min(limit, 60 * MIB))


def cost(flops, moved, transcendentals=0):
    return pl.CostEstimate(flops=flops, bytes_accessed=moved, transcendentals=transcendentals)


def exchange(blocks, axis):
    return lax.all_to_all(blocks, axis, 0, 0)


def send_pieces(pieces, axis):
    count = lax.axis_size(axis)
    received = [pieces[0]]
    for shift in range(1, count):
        pairs = [(i, (i + shift) % count) for i in range(count)]
        received.append(lax.ppermute(pieces[shift], axis, pairs))
    return received


def lookup_kernel(tokens, table, out, blocks, rows_f32, sem):
    steps, batch = tokens.shape
    chunks, rows, width = out.shape
    local_rows = table.shape[0]
    base = lax.axis_index("ctx") * local_rows

    def place(row):
        offset = tokens[row % steps, row // steps] - base
        return offset, (offset >= 0) & (offset < local_rows)

    def copy(row, offset):
        start = pl.multiple_of((offset // 8) * 8, 8)
        return pltpu.make_async_copy(
            table.at[pl.ds(start, 8), :], blocks.at[row], sem.at[row]
        )

    for row in range(rows):
        offset, inside = place(row)

        @pl.when(inside)
        def _():
            copy(row, offset).start()

    rows_f32[...] = jnp.zeros_like(rows_f32)
    sublane = lax.broadcasted_iota(jnp.int32, (8, 1), 0)
    for row in range(rows):
        offset, inside = place(row)

        @pl.when(inside)
        def _():
            copy(row, offset).wait()
            picked = jnp.where(sublane == offset % 8, blocks[row].astype(F32), 0.0)
            rows_f32[row : row + 1, :] = jnp.sum(picked, axis=0, keepdims=True)

    for chunk in range(chunks):
        out[chunk] = rows_f32[:, chunk * width : (chunk + 1) * width].astype(BF16)


def lookup_rows(token_ids, embedding):
    steps, batch = token_ids.shape
    rows = steps * batch
    chunks = lax.axis_size("ctx")
    local_rows, width = embedding.shape
    if local_rows % 8 == 0:
        return pl.pallas_call(
            lookup_kernel,
            out_shape=jax.ShapeDtypeStruct((chunks, rows, width // chunks), BF16),
            in_specs=[SMEM, HBM],
            out_specs=VMEM,
            scratch_shapes=[
                pltpu.VMEM((rows, 8, width), BF16),
                pltpu.VMEM((rows, width), F32),
                pltpu.SemaphoreType.DMA((rows,)),
            ],
            compiler_params=params(6 * rows * width * 8),
            cost_estimate=cost(rows * width, rows * width * 16),
            name="lookup",
        )(token_ids, embedding)
    offsets = token_ids.T.reshape(rows) - lax.axis_index("ctx") * local_rows
    inside = (offsets >= 0) & (offsets < local_rows)
    picked = jnp.take(embedding, jnp.clip(offsets, 0, local_rows - 1), axis=0)
    picked = jnp.where(inside[:, None], picked, jnp.zeros((), BF16))
    return jnp.swapaxes(picked.reshape(rows, chunks, width // chunks), 0, 1)


def join_kernel(parts, out):
    total = parts[0].astype(F32)
    for source in range(1, parts.shape[0]):
        total = total + parts[source].astype(F32)
    joined = total.astype(BF16)
    for target in range(out.shape[0]):
        out[target] = joined


def join_copies(parts):
    return pl.pallas_call(
        join_kernel,
        out_shape=jax.ShapeDtypeStruct(parts.shape, BF16),
        in_specs=[VMEM],
        out_specs=VMEM,
        compiler_params=params(8 * MIB),
        name="join",
    )(parts)


def project_kernel(heads_here, x, gain, weight, *refs):
    count = weight.shape[0] // heads_here
    outs, (held, scaled, sem) = refs[:count], refs[count:]
    chunks, rows, chunk_width = x.shape
    columns = weight.shape[1]
    here = lax.axis_index("head")

    def copy(shift):
        first = lax.rem(here + shift, count) * heads_here
        return pltpu.make_async_copy(
            weight.at[pl.ds(first, heads_here)], held.at[shift], sem.at[shift]
        )

    for shift in range(count):
        copy(shift).start()
    squares = jnp.zeros((rows, 1), F32)
    for chunk in range(chunks):
        span = slice(chunk * chunk_width, (chunk + 1) * chunk_width)
        features = x[chunk].astype(F32)
        squares = squares + jnp.sum(features * features, axis=-1, keepdims=True)
        scaled[:, span] = (features * gain[:, span]).astype(BF16)
    used = heads_here * columns
    rest = outs[0].shape[1] - used
    for shift in range(count):
        copy(shift).wait()
        products = [
            lax.dot_general(scaled[...], held[shift, head], NT, preferred_element_type=F32)
            for head in range(heads_here)
        ]
        outs[shift][...] = jnp.concatenate(
            products + [jnp.broadcast_to(squares, (rows, rest))], axis=1
        )


def project(x, attn_gain, weight):
    count = lax.axis_size("head")
    chunks, rows, chunk_width = x.shape
    heads, columns, width = weight.shape
    heads_here = heads // count
    wide = round_up(heads_here * columns + 1, LANES)
    size = weight.size * 2
    return pl.pallas_call(
        functools.partial(project_kernel, heads_here),
        out_shape=[jax.ShapeDtypeStruct((rows, wide), F32)] * count,
        in_specs=[VMEM, VMEM, HBM],
        out_specs=[VMEM] * count,
        scratch_shapes=[
            pltpu.VMEM((count, heads_here, columns, width), BF16),
            pltpu.VMEM((rows, width), BF16),
            pltpu.SemaphoreType.DMA((count,)),
        ],
        compiler_params=params(size + 10 * MIB),
        cost_estimate=cost(2 * rows * weight.size, size),
        name="project",
    )(x, attn_gain.reshape(1, width), weight)


def norm_kernel(used, model_width, *refs):
    pieces, out = refs[:-1], refs[-1]
    total = pieces[0][...]
    for piece in pieces[1:]:
        total = total + piece[...]
    factor = lax.rsqrt(total[:, used : used + 1] * (1.0 / model_width) + EPSILON)
    united = (total * factor).astype(BF16)
    for target in range(out.shape[0]):
        out[target] = united


def norm_copies(pieces, used, model_width):
    rows, wide = pieces[0].shape
    return pl.pallas_call(
        functools.partial(norm_kernel, used, model_width),
        out_shape=jax.ShapeDtypeStruct((lax.axis_size("ctx"), rows, wide), BF16),
        in_specs=[VMEM] * len(pieces),
        out_specs=VMEM,
        compiler_params=params(8 * MIB),
        name="norm",
    )(*pieces)


def split3(value):
    first = value.astype(BF16).astype(F32)
    second = (value - first).astype(BF16).astype(F32)
    return first, second, value - first - second


def attend_kernel(columns, group, united, cosine, sine, keys, values, packet, ready, fresh, *scratch):
    key_buf, value_buf, query_buf, score_buf, key_sem, value_sem = scratch
    chunks, rows, _ = united.shape
    heads, context, head_dim = keys.shape
    per_dest = rows // chunks
    block = per_dest * group
    tile = min(512, context)
    tiles = context // tile

    def key_copy(head):
        return pltpu.make_async_copy(keys.at[head], key_buf.at[head], key_sem.at[head])

    def value_copy(head):
        return pltpu.make_async_copy(values.at[head], value_buf.at[head], value_sem.at[head])

    for head in range(heads):
        key_copy(head).start()
        value_copy(head).start()

    cos = cosine[...]
    sin = sine[...]

    def rotated(vectors):
        return vectors * cos + pltpu.roll(vectors, head_dim // 2, 1) * sin

    for head in range(heads):
        first = head * columns
        whole = jnp.concatenate(
            [united[chunk].astype(F32)[:, first : first + columns] for chunk in range(chunks)],
            axis=1,
        )
        for j in range(group):
            query = rotated(whole[:, j * head_dim : (j + 1) * head_dim]) * head_dim ** (-0.5)
            for dest in range(chunks):
                start = dest * block + j * per_dest
                query_buf[head, start : start + per_dest, :] = query[
                    dest * per_dest : (dest + 1) * per_dest
                ]
        new_key = whole[:, group * head_dim : (group + 1) * head_dim]
        fresh[head] = rotated(new_key).astype(BF16)
        fresh[heads + head] = whole[:, (group + 1) * head_dim :].astype(BF16)

    lane = lax.broadcasted_iota(jnp.int32, (chunks * block, LANES), 1)
    for head in range(heads):
        query = query_buf[head].astype(BF16)
        for dest in range(chunks):
            ready[dest, head] = query[dest * block : (dest + 1) * block]
        key_copy(head).wait()
        highest = None
        for step in range(tiles):
            span = slice(step * tile, (step + 1) * tile)
            scores = lax.dot_general(
                query, key_buf[head, span, :], NT, preferred_element_type=F32
            )
            score_buf[:, span] = scores
            for part in range(tile // LANES):
                piece = scores[:, part * LANES : (part + 1) * LANES]
                highest = piece if highest is None else jnp.maximum(highest, piece)
        maxima = jnp.max(highest, axis=-1, keepdims=True)
        value_copy(head).wait()
        sums = jnp.zeros((chunks * block, head_dim), F32)
        totals = jnp.zeros((chunks * block, LANES), F32)
        for step in range(tiles):
            span = slice(step * tile, (step + 1) * tile)
            weights = jnp.exp(score_buf[:, span] - maxima).astype(BF16)
            sums = sums + jnp.dot(weights, value_buf[head, span, :], preferred_element_type=F32)
            wide = weights.astype(F32)
            for part in range(tile // LANES):
                totals = totals + wide[:, part * LANES : (part + 1) * LANES]
        total = jnp.sum(totals, axis=-1, keepdims=True)
        table = jnp.zeros((chunks * block, LANES), F32)
        for index, piece in enumerate(split3(maxima) + split3(total)):
            table = jnp.where(lane == index, piece, table)
        rounded = sums.astype(BF16)
        for dest in range(chunks):
            packet[dest, head * block : (head + 1) * block] = rounded[
                dest * block : (dest + 1) * block
            ]
        turned = jnp.transpose(table)[:16]
        for dest in range(chunks):
            packet[dest, heads * block + head * 16 : heads * block + (head + 1) * 16, :block] = turned[
                :, dest * block : (dest + 1) * block
            ].astype(BF16)


def attend(united, columns, cosine, sine, keys, values):
    chunks, rows, _ = united.shape
    heads, context, head_dim = keys.shape
    group = columns * chunks // head_dim - 2
    block = rows // chunks * group
    size = keys.size * 2
    flat = chunks * block
    return pl.pallas_call(
        functools.partial(attend_kernel, columns, group),
        out_shape=[
            jax.ShapeDtypeStruct((chunks, heads * (block + 16), head_dim), BF16),
            jax.ShapeDtypeStruct((chunks, heads, block, head_dim), BF16),
            jax.ShapeDtypeStruct((2 * heads, rows, head_dim), BF16),
        ],
        in_specs=[VMEM, VMEM, VMEM, HBM, HBM],
        out_specs=[VMEM] * 3,
        scratch_shapes=[
            pltpu.VMEM(keys.shape, BF16),
            pltpu.VMEM(keys.shape, BF16),
            pltpu.VMEM((heads, flat, head_dim), F32),
            pltpu.VMEM((flat, context), F32),
            pltpu.SemaphoreType.DMA((heads,)),
            pltpu.SemaphoreType.DMA((heads,)),
        ],
        compiler_params=params(2 * size + flat * context * 4 + 16 * MIB),
        cost_estimate=cost(4 * heads * flat * context * head_dim, 2 * size, heads * flat * context),
        name="attend",
    )(united, cosine, sine, keys, values)


def near_kernel(owned, lengths, ready, fresh, keys, values, sums, maxima, totals):
    heads, rows, head_dim = fresh.shape
    heads //= 2
    _, _, block, _ = ready.shape
    slots_all = keys.shape[1]
    per_dest = rows // ready.shape[0]
    steps = per_dest // owned
    mine = lax.axis_index("ctx")

    def iota(shape, axis):
        return lax.broadcasted_iota(jnp.int32, shape, axis)

    query_place = iota((block, 1), 0) % per_dest
    sequence = query_place // steps
    step = query_place % steps
    slot = iota((1, slots_all), 1)
    fresh_row = iota((1, rows), 1)
    fresh_here = (fresh_row // steps == mine * owned + sequence) & (fresh_row % steps <= step)
    for head in range(heads):
        query = ready[mine, head]
        fresh_scores = lax.dot_general(query, fresh[head], NT, preferred_element_type=F32)
        fresh_scores = jnp.where(fresh_here, fresh_scores, MASKED)
        scores = []
        highest = jnp.max(fresh_scores, axis=-1, keepdims=True)
        for s in range(owned):
            found = lax.dot_general(query, keys[s], NT, preferred_element_type=F32)
            live = (sequence == s) & (slot % heads == head)
            live = live & (slot // heads < lengths[mine * owned + s])
            found = jnp.where(live, found, MASKED)
            scores.append(found)
            highest = jnp.maximum(highest, jnp.max(found, axis=-1, keepdims=True))
        weights = jnp.exp(fresh_scores - highest).astype(BF16)
        total = jnp.sum(weights.astype(F32), axis=-1, keepdims=True)
        result = jnp.dot(weights, fresh[heads + head], preferred_element_type=F32)
        for s in range(owned):
            weights = jnp.exp(scores[s] - highest).astype(BF16)
            total = total + jnp.sum(weights.astype(F32), axis=-1, keepdims=True)
            result = result + jnp.dot(weights, values[s], preferred_element_type=F32)
        span = slice(head * block, (head + 1) * block)
        sums[span, :] = result
        maxima[span, :] = jnp.broadcast_to(highest, (block, head_dim))
        totals[span, :] = jnp.broadcast_to(total, (block, head_dim))


def near(lengths, ready, fresh, keys, values):
    owned, slots, heads, head_dim = keys.shape
    block = ready.shape[2]
    shape = jax.ShapeDtypeStruct((heads * block, head_dim), F32)
    return pl.pallas_call(
        functools.partial(near_kernel, owned),
        out_shape=[shape] * 3,
        in_specs=[SMEM, VMEM, VMEM, VMEM, VMEM],
        out_specs=[VMEM] * 3,
        compiler_params=params(8 * MIB),
        cost_estimate=cost(4 * heads * block * owned * slots * heads * head_dim, keys.size * 4),
        name="near",
    )(
        lengths,
        ready,
        fresh,
        keys.reshape(owned, slots * heads, head_dim),
        values.reshape(owned, slots * heads, head_dim),
    )


def merge_kernel(group, parts, near_sums, near_maxima, near_totals, out, places, stats):
    chunks = parts.shape[0]
    per_dest = out.shape[1]
    block = per_dest * group
    queries, head_dim = near_sums.shape
    heads = queries // block
    highest = near_maxima[...][:, :1]
    maxima, totals = [], []
    for source in range(chunks):
        for head in range(heads):
            low = queries + head * 16
            found = parts[source, low : low + 16, :].astype(F32)[:8]
            row = (source * heads + head) * 8
            stats[row : row + 8, :] = found
    turned = jnp.transpose(stats[...])[:block]
    for source in range(chunks):
        m, t = [], []
        for head in range(heads):
            column = (source * heads + head) * 8
            get = lambda k: turned[:, column + k : column + k + 1]
            m.append(get(0) + get(1) + get(2))
            t.append(get(3) + get(4) + get(5))
        maxima.append(jnp.concatenate(m, axis=0))
        totals.append(jnp.concatenate(t, axis=0))
        highest = jnp.maximum(highest, maxima[-1])
    scale = jnp.exp(near_maxima[...][:, :1] - highest)
    numerator = near_sums[...] * scale
    denominator = near_totals[...][:, :1] * scale
    for source in range(chunks):
        scale = jnp.exp(maxima[source] - highest)
        numerator = numerator + parts[source, :queries, :].astype(F32) * scale
        denominator = denominator + totals[source] * scale
    attention = numerator / denominator
    for index in range(heads * group):
        places[:, index * head_dim : (index + 1) * head_dim] = attention[
            index * per_dest : (index + 1) * per_dest
        ]
    rounded = places[...].astype(BF16)
    for target in range(chunks):
        out[target] = rounded


def merge_copies(parts, sums, maxima, totals, group, per_dest):
    chunks = parts.shape[0]
    queries, head_dim = sums.shape
    heads = queries // (per_dest * group)
    width = heads * group * head_dim
    return pl.pallas_call(
        functools.partial(merge_kernel, group),
        out_shape=jax.ShapeDtypeStruct((chunks, per_dest, width), BF16),
        in_specs=[VMEM] * 4,
        out_specs=VMEM,
        scratch_shapes=[
            pltpu.VMEM((per_dest, width), F32),
            pltpu.VMEM((chunks * heads * 8, head_dim), F32),
        ],
        compiler_params=params(12 * MIB),
        name="merge",
    )(parts, sums, maxima, totals)


def output_kernel(x, weight, *refs):
    chunks, per_dest, depth = x.shape
    held, rows_f32, total, sem = refs[-4:]
    outs = refs[:-4]
    count = len(outs)
    pieces = held.shape[0]
    step = depth // pieces

    def copy(piece):
        return pltpu.make_async_copy(
            weight.at[pl.ds(piece * step, step), :], held.at[piece], sem.at[piece]
        )

    for piece in range(pieces):
        copy(piece).start()
    for chunk in range(chunks):
        rows_f32[chunk * per_dest : (chunk + 1) * per_dest, :] = x[chunk].astype(F32)
    rows = rows_f32[...].astype(BF16)
    for piece in range(pieces):
        copy(piece).wait()
        product = jnp.dot(
            rows[:, piece * step : (piece + 1) * step], held[piece], preferred_element_type=F32
        )
        if piece == 0:
            total[...] = product
        else:
            total[...] += product
    here = lax.axis_index("head")
    height = total.shape[0] // count
    for shift in range(count):
        first = pl.multiple_of(lax.rem(here + shift, count) * height, height)
        outs[shift][...] = total[pl.ds(first, height), :].astype(BF16)


def project_out(x, weight):
    count = lax.axis_size("head")
    chunks, per_dest, depth = x.shape
    rows = chunks * per_dest
    width = weight.shape[1]
    pieces = 8
    return pl.pallas_call(
        output_kernel,
        out_shape=[jax.ShapeDtypeStruct((rows // count, width), BF16)] * count,
        in_specs=[VMEM, HBM],
        out_specs=[VMEM] * count,
        scratch_shapes=[
            pltpu.VMEM((pieces, depth // pieces, width), BF16),
            pltpu.VMEM((rows, depth), F32),
            pltpu.VMEM((rows, width), F32),
            pltpu.SemaphoreType.DMA((pieces,)),
        ],
        compiler_params=params(weight.size * 2 + 10 * MIB),
        cost_estimate=cost(2 * rows * weight.size, weight.size * 2),
        name="output",
    )(x, weight)


def body(
    token_ids,
    suffix_lengths,
    embedding,
    attn_gain,
    qkv_weight,
    out_weight,
    prefix_keys,
    prefix_values,
    suffix_keys,
    suffix_values,
):
    steps, batch = token_ids.shape
    rows = steps * batch
    n_ctx = lax.axis_size("ctx")
    n_head = lax.axis_size("head")
    heads, block_context, head_dim = prefix_keys.shape
    width = embedding.shape[1]
    columns = qkv_weight.shape[2]
    group = columns * n_ctx // head_dim - 2
    step_index = jnp.arange(steps, dtype=jnp.int32)
    positions = block_context * n_ctx + suffix_lengths[:, None] + step_index[None, :]
    positions = positions.astype(F32).reshape(rows)
    half = head_dim // 2
    frequency = ROTARY_THETA ** (-2.0 * jnp.arange(half).astype(F32) / head_dim)
    angles = positions[:, None] * frequency
    cosine, sine = jnp.cos(angles), jnp.sin(angles)
    cosine = jnp.concatenate([cosine, cosine], axis=1)
    sine = jnp.concatenate([-sine, sine], axis=1)

    picked = lookup_rows(token_ids, embedding)
    joined = join_copies(exchange(picked, "ctx"))
    features = exchange(joined, "ctx")
    pieces = project(features, attn_gain, jnp.transpose(qkv_weight, (1, 2, 0)))
    pieces = send_pieces(pieces, "head")
    united = norm_copies(pieces, heads * columns, width * n_head)
    united = exchange(united, "ctx")
    packet, ready, fresh = attend(united, columns, cosine, sine, prefix_keys, prefix_values)
    parts = exchange(packet, "ctx")
    sums, maxima, totals = near(suffix_lengths, ready, fresh, suffix_keys, suffix_values)
    attention = merge_copies(parts, sums, maxima, totals, group, rows // n_ctx)
    attention = exchange(attention, "ctx")
    pieces = send_pieces(project_out(attention, out_weight), "head")
    result = pieces[0].astype(F32)
    for piece in pieces[1:]:
        result = result + piece.astype(F32)
    return result.astype(BF16).reshape(batch // n_head, steps, -1)


def solution(mesh):
    placed = (
        P(),
        P(),
        P("ctx", "head"),
        P("head"),
        P("head", None, "ctx"),
        P("head", "ctx"),
        P("head", "ctx", None),
        P("head", "ctx", None),
        P("ctx", None, "head", None),
        P("ctx", None, "head", None),
    )
    return jax.shard_map(
        body, mesh=mesh, in_specs=placed, out_specs=P("head", None, "ctx"), check_vma=False
    )
```

time: 121 us -> 99.6 us (0.82)
  matrix products: 20.8 us -> 0 us
  Pallas kernels: 0 us -> 18.2 us
  other arithmetic: 10.8 us -> 0.33 us
  waiting for transfers between devices: 34.5 us -> 27 us
  blocking collectives: 28.1 us -> 26 us
  local copies, waits for them, and re-layouts: 8.56 us -> 10.4 us
    dot_general x8 -> x0, matrix products: 20.8 us -> none  [the longest x1 7.39 us: body(): jnp.einsum('rd,dgf->grf', scaled, qkv_weight, preferred_element_type=F32)]
    pallas_call x0 -> x8, Pallas kernels: none -> 18.2 us  [the longest x1 5.08 us: attend(): pl.pallas_call(functools.partial(attend_kernel, columns, group), out_shap...]
    unnamed x11 -> x18, local copies, waits for them, and re-layouts: 1.03 us -> 9.66 us
    all_to_all x3, waiting for transfers between devices: 30.1 us -> 23.7 us  [exchange(): return lax.all_to_all(blocks, axis, 0, 0)]
    reduce_sum x6 -> x0, other arithmetic: 5.77 us -> none  [the longest x1 4.78 us: body(): totals = jnp.sum(weights.astype(F32), axis=-1, keepdims=True)]
    gather x2 -> x0, local copies, waits for them, and re-layouts: 2.51 us -> none  [body(): jnp.take(embedding, jnp.clip(offsets, 0, embedding.shape[0] - 1), axis=0)]
    all_to_all x2, blocking collectives: 28.1 us -> 26 us  [exchange(): return lax.all_to_all(blocks, axis, 0, 0)]
    broadcast_in_dim x5 -> x0, local copies, waits for them, and re-layouts: 1.73 us -> none  [the longest x3 1.56 us: gather_all(): return exchange(jnp.broadcast_to(block[None], (count,) + block.shape), axis)]
  transfers between devices with their start and end apart: 9 -> 9, of which waited for: 8 -> 9; matrix products, arithmetic and copies ran while one was open for 3% -> 0% of each run, Pallas kernels for 0% -> 1%
where the time goes in v2:
time: 99.6 us; the launch traced here: 98.8 us
  waiting for transfers between devices  27 us (27%)
  blocking collectives  26 us (26%)
  Pallas kernels  18.2 us (18%)
  starting transfers between devices  16.7 us (17%)
  local copies, waits for them, and re-layouts  10.4 us (10%)
    all_to_all x2, blocking collectives, exchange(): return lax.all_to_all(blocks, axis, 0, 0)  26 us
    all_to_all x3, waiting for transfers between devices, exchange(): return lax.all_to_all(blocks, axis, 0, 0)  23.7 us
    all_to_all x3, starting transfers between devices, exchange(): return lax.all_to_all(blocks, axis, 0, 0)  10.7 us
    unnamed x18, local copies, waits for them, and re-layouts  9.66 us
    ppermute x6, starting transfers between devices, send_pieces(): received.append(lax.ppermute(pieces[shift], axis, pairs))  6.03 us
    pallas_call x1, Pallas kernels, attend(): pl.pallas_call(functools.partial(attend_kernel, columns, group), out_shap...  5.08 us
    pallas_call x1, Pallas kernels, project(): pl.pallas_call(functools.partial(project_kernel, heads_here), out_shape=[...  4.89 us
    ppermute x6, waiting for transfers between devices, send_pieces(): received.append(lax.ppermute(pieces[shift], axis, pairs))  3.27 us
  transfers between devices with their start and end apart: 9, of which 9 were waited for; matrix products, arithmetic and copies ran while one was open for 0% of the time, Pallas kernels for 1%

profile of v2, /device:TPU:0, one launch (start us, length us, event | category | flops | bytes accessed | tf_op | source)
XLA Modules:
  0.0 98.8 jit_solution(8087566766309494874)
XLA Ops:
  0.0 0.7 copy-done.7
  0.7 2.4 %lookup.1 = bf16[8,32,512]{2,1,0:T(8,128)(2,1)S(1)} custom-call(s32[2,16]{1,0:T(2,128)S(1)} %copy-done.7, bf16[8016,4096]{1,0:T(8,128)(2,1)} %table.1), custom_call_target="tpu_custom_call" | custom-call | flops 131072 | bytes 2097152 | tf_op jit(solution)/shard_map/lookup/pallas_call | solution.py:92
  3.1 15.7 %all_to_all.25.parts = bf16[8,32,512]{2,1,0:T(8,128)(2,1)S(1)} all-to-all(bf16[8,32,512]{2,1,0:T(8,128)(2,1)S(1)} %lookup.1), channel_id=1, replica_groups=mesh['head'=4,'ctx'=8] {'ctx'}, dimensions={0} | all-to-all | bytes 524288 | tf_op jit(solution)/shard_map/all_to_all | solution.py:36
  18.9 0.7 join.1
  19.6 3.7 %all-to-all-start.1 = ((bf16[8,32,512]{2,1,0:T(8,128)(2,1)}), bf16[8,32,512]{2,1,0:T(8,128)(2,1)S(1)}, u32[]{:S(2)}, u32[]{:S(2)}) async-start(bf16[8,32,512]{2,1,0:T(8,128)(2,1)} %join.1), calls=%async_computation.1 | async-start | bytes 524288 | tf_op jit(solution)/shard_map/all_to_all | solution.py:36
  23.4 8.6 %all-to-all-done.1.x = bf16[8,32,512]{2,1,0:T(8,128)(2,1)S(1)} async-done(((bf16[8,32,512]{2,1,0:T(8,128)(2,1)}), bf16[8,32,512]{2,1,0:T(8,128)(2,1)S(1)}, u32[]{:S(2)}, u32[]{:S(2)}) %all-to-all-start.1) | async-done | bytes 262176 | tf_op jit(solution)/shard_map/all_to_all | solution.py:36
  31.9 4.0 %copy-done = bf16[4096,8,160]{0,2,1:T(8,128)(2,1)S(1)} copy-done((bf16[4096,8,160]{0,2,1:T(8,128)(2,1)S(1)}, bf16[4096,8,160]{0,2,1:T(8,128)(2,1)}, u32[]{:S(2)}) %copy-start) | copy-done | bytes 10485784
  35.9 4.9 %project.1 = (f32[32,384]{1,0:T(8,128)S(1)}, f32[32,384]{1,0:T(8,128)S(1)}, f32[32,384]{1,0:T(8,128)S(1)}, f32[32,384]{1,0:T(8,128)S(1)}) custom-call(bf16[8,32,512]{2,1,0:T(8,128)(2,1)S(1)} %all-to-all-done.1.x, f32[1,4096]{1,0:T(1,128)S(1)} %bitcast.7, bf16[8,160,4096]{2,1,0:T(8,128)(2,1)S(1)} %bitcast.4), custom_call_target="tpu_custom_call" | custom-call | flops 335544320 | bytes 10485760 | tf_op jit(solution)/shard_map/project/pallas_call | solution.py:174
  40.9 1.6 %collective-permute-start.1 = (f32[32,384]{1,0:T(8,128)S(1)}, f32[32,384]{1,0:T(8,128)S(1)}, u32[]{:S(2)}, u32[]{:S(2)}) collective-permute-start(f32[32,384]{1,0:T(8,128)S(1)} %get-tuple-element.21), channel_id=1, source_target_pairs={{0,16},{8,24},{16,0},{24,8},{1,17},{9,25},{17,1},{25,9},{2,18},{10... | collective-permute-start | bytes 147464 | tf_op jit(solution)/shard_map/ppermute | solution.py:44
  42.4 1.4 %collective-permute-start.2 = (f32[32,384]{1,0:T(8,128)S(1)}, f32[32,384]{1,0:T(8,128)S(1)}, u32[]{:S(2)}, u32[]{:S(2)}) collective-permute-start(f32[32,384]{1,0:T(8,128)S(1)} %get-tuple-element.22), channel_id=1, source_target_pairs={{0,24},{8,0},{16,8},{24,16},{1,25},{9,1},{17,9},{25,17},{2,26},{10... | collective-permute-start | bytes 147464 | tf_op jit(solution)/shard_map/ppermute | solution.py:44
  43.9 0.5 collective-permute-done.refs_1_
  44.4 0.7 collective-permute-done.1.refs_2_
  45.0 0.5 collective-permute-done.2.refs_3_
  45.6 0.8 norm.1
  46.3 3.6 %all-to-all-start.2 = ((bf16[8,32,384]{2,1,0:T(8,128)(2,1)}), bf16[8,32,384]{2,1,0:T(8,128)(2,1)S(1)}, u32[]{:S(2)}, u32[]{:S(2)}) async-start(bf16[8,32,384]{2,1,0:T(8,128)(2,1)} %norm.1), calls=%async_computation.2 | async-start | bytes 393216 | tf_op jit(solution)/shard_map/all_to_all | solution.py:36
  50.0 0.1 fusion
  50.3 8.5 %all-to-all-done.2.united = bf16[8,32,384]{2,1,0:T(8,128)(2,1)S(1)} async-done(((bf16[8,32,384]{2,1,0:T(8,128)(2,1)}), bf16[8,32,384]{2,1,0:T(8,128)(2,1)S(1)}, u32[]{:S(2)}, u32[]{:S(2)}) %all-to-all-start.2) | async-done | bytes 196640 | tf_op jit(solution)/shard_map/all_to_all | solution.py:36
  58.7 1.6 %copy-done.3 = bf16[2,4096,128]{2,1,0:T(8,128)(2,1)S(1)} copy-done((bf16[2,4096,128]{2,1,0:T(8,128)(2,1)S(1)}, bf16[2,4096,128]{2,1,0:T(8,128)(2,1)}, u32[]{:S(2)}) %copy-start.3) | copy-done | bytes 2097176
  60.3 5.1 %attend.1 = (bf16[8,96,128]{2,1,0:T(8,128)(2,1)}, bf16[8,2,32,128]{3,2,1,0:T(8,128)(2,1)S(1)}, bf16[4,32,128]{2,1,0:T(8,128)(2,1)S(1)}) custom-call(bf16[8,32,384]{2,1,0:T(8,128)(2,1)S(1)} %all-to-all-done.2.united, f32[32,128]{1,0:T(8,128)S(1)} %get-tuple-element.36.cosine, f32[32,128]{1,0:T(8,128)S(1)} %get-tuple-element.37.sine, ...), custom_call_target="tpu_custom_call" | custom-call | flops 1073741824 | bytes 4194304 | tf_op jit(solution)/shard_map/attend/pallas_call | solution.py:311
  65.4 3.4 %all-to-all-start.3 = ((bf16[8,96,128]{2,1,0:T(8,128)(2,1)}), bf16[8,96,128]{2,1,0:T(8,128)(2,1)S(1)}, u32[]{:S(2)}, u32[]{:S(2)}) async-start(bf16[8,96,128]{2,1,0:T(8,128)(2,1)} %get-tuple-element.23), calls=%async_computation.3 | async-start | bytes 393216 | tf_op jit(solution)/shard_map/all_to_all | solution.py:36
  68.8 1.2 %near.1 = (f32[64,128]{1,0:T(8,128)S(1)}, f32[64,128]{1,0:T(8,128)S(1)}, f32[64,128]{1,0:T(8,128)S(1)}) custom-call(s32[16]{0:T(128)S(1)} %copy-done.8, bf16[8,2,32,128]{3,2,1,0:T(8,128)(2,1)S(1)} %get-tuple-element.24.ready, bf16[4,32,128]{2,1,0:T(8,128)(2,1)S(1)} %get-tuple-element.25.fresh, bf16[2,256,128]{2,1,0:T(8,128)(2,1)S(1)} %bitcast.5, ...), custom_call_target="tpu_custom_call" | custom-call | flops 16777216 | bytes 262144 | tf_op jit(solution)/shard_map/near/pallas_call | solution.py:382
  70.0 6.7 %all-to-all-done.3.parts = bf16[8,96,128]{2,1,0:T(8,128)(2,1)S(1)} async-done(((bf16[8,96,128]{2,1,0:T(8,128)(2,1)}), bf16[8,96,128]{2,1,0:T(8,128)(2,1)S(1)}, u32[]{:S(2)}, u32[]{:S(2)}) %all-to-all-start.3) | async-done | bytes 196640 | tf_op jit(solution)/shard_map/all_to_all | solution.py:36
  76.7 0.8 merge.1
  77.5 10.3 %all_to_all.26.x = bf16[8,4,2048]{2,1,0:T(4,128)(2,1)S(1)} all-to-all(bf16[8,4,2048]{2,1,0:T(4,128)(2,1)S(1)} %merge.1), channel_id=1, replica_groups=mesh['head'=4,'ctx'=8] {'ctx'}, dimensions={0} | all-to-all | bytes 262144 | tf_op jit(solution)/shard_map/all_to_all | solution.py:36
  87.8 3.4 %copy-done.1 = bf16[2048,2048]{1,0:T(8,128)(2,1)S(1)} copy-done((bf16[2048,2048]{1,0:T(8,128)(2,1)S(1)}, bf16[2048,2048]{1,0:T(8,128)(2,1)}, u32[]{:S(2)}) %copy-start.1) | copy-done | bytes 8388632
  91.2 2.3 %output.1 = (bf16[8,2048]{1,0:T(8,128)(2,1)S(1)}, bf16[8,2048]{1,0:T(8,128)(2,1)S(1)}, bf16[8,2048]{1,0:T(8,128)(2,1)S(1)}, bf16[8,2048]{1,0:T(8,128)(2,1)S(1)}) custom-call(bf16[8,4,2048]{2,1,0:T(4,128)(2,1)S(1)} %all_to_all.26.x, bf16[2048,2048]{1,0:T(8,128)(2,1)S(1)} %copy-done.1), custom_call_target="tpu_custom_call" | custom-call | flops 268435456 | bytes 8388608 | tf_op jit(solution)/shard_map/output/pallas_call | solution.py:500
  93.5 1.6 %collective-permute-start.4 = (bf16[8,2048]{1,0:T(8,128)(2,1)S(1)}, bf16[8,2048]{1,0:T(8,128)(2,1)S(1)}, u32[]{:S(2)}, u32[]{:S(2)}) collective-permute-start(bf16[8,2048]{1,0:T(8,128)(2,1)S(1)} %get-tuple-element.31), channel_id=1, source_target_pairs={{0,16},{8,24},{16,0},{24,8},{1,17},{9,25},{17,1},{25,9},{2,18},{10... | collective-permute-start | bytes 98312 | tf_op jit(solution)/shard_map/ppermute | solution.py:44
  95.1 1.4 %collective-permute-start.5 = (bf16[8,2048]{1,0:T(8,128)(2,1)S(1)}, bf16[8,2048]{1,0:T(8,128)(2,1)S(1)}, u32[]{:S(2)}, u32[]{:S(2)}) collective-permute-start(bf16[8,2048]{1,0:T(8,128)(2,1)S(1)} %get-tuple-element.32), channel_id=1, source_target_pairs={{0,24},{8,0},{16,8},{24,16},{1,25},{9,1},{17,9},{25,17},{2,26},{10... | collective-permute-start | bytes 98312 | tf_op jit(solution)/shard_map/ppermute | solution.py:44
  96.5 0.3 collective-permute-done.3
  96.8 0.7 collective-permute-done.4
  97.5 0.6 collective-permute-done.5
  98.1 0.6 reshape.39
  (22 shorter events, 0.4 us)
Async XLA Ops:
  0.0 31.9 %copy-start.6 = (f32[4096]{0:T(1024)S(1)}, f32[4096]{0:T(1024)}, u32[]{:S(2)}) copy-start(f32[4096]{0:T(1024)} %param.13) | copy-start | bytes 49156
  0.0 0.7 copy-start.7
  0.7 22.7 %copy-start.8 = (s32[16]{0:T(128)S(1)}, s32[16]{0:T(128)}, u32[]{:S(2)}) copy-start(s32[16]{0:T(128)} %lengths.1) | copy-start | bytes 196
  0.7 58.0 %copy-start.2 = (bf16[2,4096,128]{2,1,0:T(8,128)(2,1)S(1)}, bf16[2,4096,128]{2,1,0:T(8,128)(2,1)}, u32[]{:S(2)}) copy-start(bf16[2,4096,128]{2,1,0:T(8,128)(2,1)} %keys.1) | copy-start | bytes 6291460
  19.6 49.2 %copy-start.4 = (bf16[2,128,2,128]{3,2,1,0:T(2,128)(2,1)S(1)}, bf16[2,128,2,128]{3,2,1,0:T(2,128)(2,1)}, u32[]{:S(2)}) copy-start(bf16[2,128,2,128]{3,2,1,0:T(2,128)(2,1)} %param.18) | copy-start | bytes 393220
  19.6 49.2 %copy-start.5 = (bf16[2,128,2,128]{3,2,1,0:T(2,128)(2,1)S(1)}, bf16[2,128,2,128]{3,2,1,0:T(2,128)(2,1)}, u32[]{:S(2)}) copy-start(bf16[2,128,2,128]{3,2,1,0:T(2,128)(2,1)} %param.19) | copy-start | bytes 393220
  19.6 12.3 %all-to-all-start.1 = ((bf16[8,32,512]{2,1,0:T(8,128)(2,1)}), bf16[8,32,512]{2,1,0:T(8,128)(2,1)S(1)}, u32[]{:S(2)}, u32[]{:S(2)}) async-start(bf16[8,32,512]{2,1,0:T(8,128)(2,1)} %join.1), calls=%async_computation.1 | async-start | bytes 524288 | tf_op jit(solution)/shard_map/all_to_all | solution.py:36
  31.9 4.0 %copy-start = (bf16[4096,8,160]{0,2,1:T(8,128)(2,1)S(1)}, bf16[4096,8,160]{0,2,1:T(8,128)(2,1)}, u32[]{:S(2)}) copy-start(bf16[4096,8,160]{0,2,1:T(8,128)(2,1)} %param.14) | copy-start | bytes 31457284
  40.8 3.6 %collective-permute-start = (f32[32,384]{1,0:T(8,128)S(1)}, f32[32,384]{1,0:T(8,128)S(1)}, u32[]{:S(2)}, u32[]{:S(2)}) collective-permute-start(f32[32,384]{1,0:T(8,128)S(1)} %get-tuple-element.20), channel_id=1, source_target_pairs={{0,8},{8,16},{16,24},{24,0},{1,9},{9,17},{17,25},{25,1},{2,10},{10... | collective-permute-start | bytes 147464 | tf_op jit(solution)/shard_map/ppermute | solution.py:44
  40.9 4.2 %collective-permute-start.1 = (f32[32,384]{1,0:T(8,128)S(1)}, f32[32,384]{1,0:T(8,128)S(1)}, u32[]{:S(2)}, u32[]{:S(2)}) collective-permute-start(f32[32,384]{1,0:T(8,128)S(1)} %get-tuple-element.21), channel_id=1, source_target_pairs={{0,16},{8,24},{16,0},{24,8},{1,17},{9,25},{17,1},{25,9},{2,18},{10... | collective-permute-start | bytes 147464 | tf_op jit(solution)/shard_map/ppermute | solution.py:44
  42.4 3.1 %collective-permute-start.2 = (f32[32,384]{1,0:T(8,128)S(1)}, f32[32,384]{1,0:T(8,128)S(1)}, u32[]{:S(2)}, u32[]{:S(2)}) collective-permute-start(f32[32,384]{1,0:T(8,128)S(1)} %get-tuple-element.22), channel_id=1, source_target_pairs={{0,24},{8,0},{16,8},{24,16},{1,25},{9,1},{17,9},{25,17},{2,26},{10... | collective-permute-start | bytes 147464 | tf_op jit(solution)/shard_map/ppermute | solution.py:44
  46.3 12.4 %all-to-all-start.2 = ((bf16[8,32,384]{2,1,0:T(8,128)(2,1)}), bf16[8,32,384]{2,1,0:T(8,128)(2,1)S(1)}, u32[]{:S(2)}, u32[]{:S(2)}) async-start(bf16[8,32,384]{2,1,0:T(8,128)(2,1)} %norm.1), calls=%async_computation.2 | async-start | bytes 393216 | tf_op jit(solution)/shard_map/all_to_all | solution.py:36
  58.7 1.6 %copy-start.3 = (bf16[2,4096,128]{2,1,0:T(8,128)(2,1)S(1)}, bf16[2,4096,128]{2,1,0:T(8,128)(2,1)}, u32[]{:S(2)}) copy-start(bf16[2,4096,128]{2,1,0:T(8,128)(2,1)} %values.1) | copy-start | bytes 6291460
  65.4 11.3 %all-to-all-start.3 = ((bf16[8,96,128]{2,1,0:T(8,128)(2,1)}), bf16[8,96,128]{2,1,0:T(8,128)(2,1)S(1)}, u32[]{:S(2)}, u32[]{:S(2)}) async-start(bf16[8,96,128]{2,1,0:T(8,128)(2,1)} %get-tuple-element.23), calls=%async_computation.3 | async-start | bytes 393216 | tf_op jit(solution)/shard_map/all_to_all | solution.py:36
  87.8 3.4 %copy-start.1 = (bf16[2048,2048]{1,0:T(8,128)(2,1)S(1)}, bf16[2048,2048]{1,0:T(8,128)(2,1)}, u32[]{:S(2)}) copy-start(bf16[2048,2048]{1,0:T(8,128)(2,1)} %weight.1) | copy-start | bytes 25165828
  93.5 3.4 %collective-permute-start.3 = (bf16[8,2048]{1,0:T(8,128)(2,1)S(1)}, bf16[8,2048]{1,0:T(8,128)(2,1)S(1)}, u32[]{:S(2)}, u32[]{:S(2)}) collective-permute-start(bf16[8,2048]{1,0:T(8,128)(2,1)S(1)} %get-tuple-element.30), channel_id=1, source_target_pairs={{0,8},{8,16},{16,24},{24,0},{1,9},{9,17},{17,25},{25,1},{2,10},{10... | collective-permute-start | bytes 98312 | tf_op jit(solution)/shard_map/ppermute | solution.py:44
  93.5 4.0 %collective-permute-start.4 = (bf16[8,2048]{1,0:T(8,128)(2,1)S(1)}, bf16[8,2048]{1,0:T(8,128)(2,1)S(1)}, u32[]{:S(2)}, u32[]{:S(2)}) collective-permute-start(bf16[8,2048]{1,0:T(8,128)(2,1)S(1)} %get-tuple-element.31), channel_id=1, source_target_pairs={{0,16},{8,24},{16,0},{24,8},{1,17},{9,25},{17,1},{25,9},{2,18},{10... | collective-permute-start | bytes 98312 | tf_op jit(solution)/shard_map/ppermute | solution.py:44
  95.1 3.0 %collective-permute-start.5 = (bf16[8,2048]{1,0:T(8,128)(2,1)S(1)}, bf16[8,2048]{1,0:T(8,128)(2,1)S(1)}, u32[]{:S(2)}, u32[]{:S(2)}) collective-permute-start(bf16[8,2048]{1,0:T(8,128)(2,1)S(1)} %get-tuple-element.32), channel_id=1, source_target_pairs={{0,24},{8,0},{16,8},{24,16},{1,25},{9,1},{17,9},{25,17},{2,26},{10... | collective-permute-start | bytes 98312 | tf_op jit(solution)/shard_map/ppermute | solution.py:44

commit v3 on v2

--- a/solution.py
+++ b/solution.py
@@ -132,19 +132,10 @@
 
 def project_kernel(heads_here, x, gain, weight, *refs):
     count = weight.shape[0] // heads_here
-    outs, (held, scaled, sem) = refs[:count], refs[count:]
+    outs, scaled = refs[:count], refs[count]
     chunks, rows, chunk_width = x.shape
     columns = weight.shape[1]
     here = lax.axis_index("head")
-
-    def copy(shift):
-        first = lax.rem(here + shift, count) * heads_here
-        return pltpu.make_async_copy(
-            weight.at[pl.ds(first, heads_here)], held.at[shift], sem.at[shift]
-        )
-
-    for shift in range(count):
-        copy(shift).start()
     squares = jnp.zeros((rows, 1), F32)
     for chunk in range(chunks):
         span = slice(chunk * chunk_width, (chunk + 1) * chunk_width)
@@ -154,9 +145,9 @@
     used = heads_here * columns
     rest = outs[0].shape[1] - used
     for shift in range(count):
-        copy(shift).wait()
+        first = lax.rem(here + shift, count) * heads_here
         products = [
-            lax.dot_general(scaled[...], held[shift, head], NT, preferred_element_type=F32)
+            lax.dot_general(scaled[...], weight[first + head], NT, preferred_element_type=F32)
             for head in range(heads_here)
         ]
         outs[shift][...] = jnp.concatenate(
@@ -174,14 +165,10 @@
     return pl.pallas_call(
         functools.partial(project_kernel, heads_here),
         out_shape=[jax.ShapeDtypeStruct((rows, wide), F32)] * count,
-        in_specs=[VMEM, VMEM, HBM],
+        in_specs=[VMEM, VMEM, VMEM],
         out_specs=[VMEM] * count,
-        scratch_shapes=[
-            pltpu.VMEM((count, heads_here, columns, width), BF16),
-            pltpu.VMEM((rows, width), BF16),
-            pltpu.SemaphoreType.DMA((count,)),
-        ],
-        compiler_params=params(size + 10 * MIB),
+        scratch_shapes=[pltpu.VMEM((rows, width), BF16)],
+        compiler_params=params(8 * MIB),
         cost_estimate=cost(2 * rows * weight.size, size),
         name="project",
     )(x, attn_gain.reshape(1, width), weight)
@@ -217,23 +204,13 @@
 
 
 def attend_kernel(columns, group, united, cosine, sine, keys, values, packet, ready, fresh, *scratch):
-    key_buf, value_buf, query_buf, score_buf, key_sem, value_sem = scratch
+    query_buf, score_buf = scratch
     chunks, rows, _ = united.shape
     heads, context, head_dim = keys.shape
     per_dest = rows // chunks
     block = per_dest * group
     tile = min(512, context)
     tiles = context // tile
-
-    def key_copy(head):
-        return pltpu.make_async_copy(keys.at[head], key_buf.at[head], key_sem.at[head])
-
-    def value_copy(head):
-        return pltpu.make_async_copy(values.at[head], value_buf.at[head], value_sem.at[head])
-
-    for head in range(heads):
-        key_copy(head).start()
-        value_copy(head).start()
 
     cos = cosine[...]
     sin = sine[...]
@@ -263,25 +240,23 @@
         query = query_buf[head].astype(BF16)
         for dest in range(chunks):
             ready[dest, head] = query[dest * block : (dest + 1) * block]
-        key_copy(head).wait()
         highest = None
         for step in range(tiles):
             span = slice(step * tile, (step + 1) * tile)
             scores = lax.dot_general(
-                query, key_buf[head, span, :], NT, preferred_element_type=F32
+                query, keys[head, span, :], NT, preferred_element_type=F32
             )
             score_buf[:, span] = scores
             for part in range(tile // LANES):
                 piece = scores[:, part * LANES : (part + 1) * LANES]
                 highest = piece if highest is None else jnp.maximum(highest, piece)
         maxima = jnp.max(highest, axis=-1, keepdims=True)
-        value_copy(head).wait()
         sums = jnp.zeros((chunks * block, head_dim), F32)
         totals = jnp.zeros((chunks * block, LANES), F32)
         for step in range(tiles):
             span = slice(step * tile, (step + 1) * tile)
             weights = jnp.exp(score_buf[:, span] - maxima).astype(BF16)
-            sums = sums + jnp.dot(weights, value_buf[head, span, :], preferred_element_type=F32)
+            sums = sums + jnp.dot(weights, values[head, span, :], preferred_element_type=F32)
             wide = weights.astype(F32)
             for part in range(tile // LANES):
                 totals = totals + wide[:, part * LANES : (part + 1) * LANES]
@@ -315,17 +290,13 @@
             jax.ShapeDtypeStruct((chunks, heads, block, head_dim), BF16),
             jax.ShapeDtypeStruct((2 * heads, rows, head_dim), BF16),
         ],
-        in_specs=[VMEM, VMEM, VMEM, HBM, HBM],
+        in_specs=[VMEM] * 5,
         out_specs=[VMEM] * 3,
         scratch_shapes=[
-            pltpu.VMEM(keys.shape, BF16),
-            pltpu.VMEM(keys.shape, BF16),
             pltpu.VMEM((heads, flat, head_dim), F32),
             pltpu.VMEM((flat, context), F32),
-            pltpu.SemaphoreType.DMA((heads,)),
-            pltpu.SemaphoreType.DMA((heads,)),
         ],
-        compiler_params=params(2 * size + flat * context * 4 + 16 * MIB),
+        compiler_params=params(flat * context * 4 + 12 * MIB),
         cost_estimate=cost(4 * heads * flat * context * head_dim, 2 * size, heads * flat * context),
         name="attend",
     )(united, cosine, sine, keys, values)
@@ -459,31 +430,14 @@
 
 def output_kernel(x, weight, *refs):
     chunks, per_dest, depth = x.shape
-    held, rows_f32, total, sem = refs[-4:]
-    outs = refs[:-4]
+    rows_f32, total = refs[-2:]
+    outs = refs[:-2]
     count = len(outs)
-    pieces = held.shape[0]
-    step = depth // pieces
-
-    def copy(piece):
-        return pltpu.make_async_copy(
-            weight.at[pl.ds(piece * step, step), :], held.at[piece], sem.at[piece]
-        )
-
-    for piece in range(pieces):
-        copy(piece).start()
     for chunk in range(chunks):
         rows_f32[chunk * per_dest : (chunk + 1) * per_dest, :] = x[chunk].astype(F32)
-    rows = rows_f32[...].astype(BF16)
-    for piece in range(pieces):
-        copy(piece).wait()
-        product = jnp.dot(
-            rows[:, piece * step : (piece + 1) * step], held[piece], preferred_element_type=F32
-        )
-        if piece == 0:
-            total[...] = product
-        else:
-            total[...] += product
+    total[...] = jnp.dot(
+        rows_f32[...].astype(BF16), weight[...], preferred_element_type=F32
+    )
     here = lax.axis_index("head")
     height = total.shape[0] // count
     for shift in range(count):
@@ -496,19 +450,13 @@
     chunks, per_dest, depth = x.shape
     rows = chunks * per_dest
     width = weight.shape[1]
-    pieces = 8
     return pl.pallas_call(
         output_kernel,
         out_shape=[jax.ShapeDtypeStruct((rows // count, width), BF16)] * count,
-        in_specs=[VMEM, HBM],
+        in_specs=[VMEM, VMEM],
         out_specs=[VMEM] * count,
-        scratch_shapes=[
-            pltpu.VMEM((pieces, depth // pieces, width), BF16),
-            pltpu.VMEM((rows, depth), F32),
-            pltpu.VMEM((rows, width), F32),
-            pltpu.SemaphoreType.DMA((pieces,)),
-        ],
-        compiler_params=params(weight.size * 2 + 10 * MIB),
+        scratch_shapes=[pltpu.VMEM((rows, depth), F32), pltpu.VMEM((rows, width), F32)],
+        compiler_params=params(8 * MIB),
         cost_estimate=cost(2 * rows * weight.size, weight.size * 2),
         name="output",
     )(x, weight)
@@ -544,6 +492,7 @@
     cosine = jnp.concatenate([cosine, cosine], axis=1)
     sine = jnp.concatenate([-sine, sine], axis=1)
 
+    token_ids, cosine, sine = lax.optimization_barrier((token_ids, cosine, sine))
     picked = lookup_rows(token_ids, embedding)
     joined = join_copies(exchange(picked, "ctx"))
     features = exchange(joined, "ctx")
@@ -552,8 +501,9 @@
     united = norm_copies(pieces, heads * columns, width * n_head)
     united = exchange(united, "ctx")
     packet, ready, fresh = attend(united, columns, cosine, sine, prefix_keys, prefix_values)
+    sums, maxima, totals = near(suffix_lengths, ready, fresh, suffix_keys, suffix_values)
+    packet, sums, maxima, totals = lax.optimization_barrier((packet, sums, maxima, totals))
     parts = exchange(packet, "ctx")
-    sums, maxima, totals = near(suffix_lengths, ready, fresh, suffix_keys, suffix_values)
     attention = merge_copies(parts, sums, maxima, totals, group, rows // n_ctx)
     attention = exchange(attention, "ctx")
     pieces = send_pieces(project_out(attention, out_weight), "head")

time: 99.6 us -> 87.8 us (0.88)
  blocking collectives: 26 us -> 62.2 us
  waiting for transfers between devices: 27 us -> 3.35 us
  starting transfers between devices: 16.7 us -> 6.02 us
  local copies, waits for them, and re-layouts: 10.4 us -> 1.47 us
  Pallas kernels: 18.2 us -> 13.2 us
    all_to_all x2 -> x5, blocking collectives: 26 us -> 62.2 us  [exchange(): return lax.all_to_all(blocks, axis, 0, 0)]
    all_to_all x3 -> x0, waiting for transfers between devices: 23.7 us -> none  [exchange(): return lax.all_to_all(blocks, axis, 0, 0)]
    all_to_all x3 -> x0, starting transfers between devices: 10.7 us -> none  [exchange(): return lax.all_to_all(blocks, axis, 0, 0)]
    unnamed x18 -> x20, local copies, waits for them, and re-layouts: 9.66 us -> 0.73 us
    pallas_call x1, Pallas kernels: 4.89 us -> 3.47 us  [project(): pl.pallas_call(functools.partial(project_kernel, heads_here), out_shape=[...]
    pallas_call x1, Pallas kernels: 5.08 us -> 3.76 us  [attend(): pl.pallas_call(functools.partial(attend_kernel, columns, group), out_shap...]
  transfers between devices with their start and end apart: 9 -> 6, of which waited for: 9 -> 6; matrix products, arithmetic and copies ran while one was open for 0% -> 0% of each run, Pallas kernels for 1% -> 0%
where the time goes in v3:
time: 87.8 us; the launch traced here: 87.4 us
  blocking collectives  62.2 us (71%)
  Pallas kernels  13.2 us (15%)
  starting transfers between devices  6.02 us (7%)
  waiting for transfers between devices  3.35 us (4%)
  local copies, waits for them, and re-layouts  1.47 us (2%)
  other arithmetic  0.99 us (1%)
    all_to_all x5, blocking collectives, exchange(): return lax.all_to_all(blocks, axis, 0, 0)  62.2 us
    ppermute x6, starting transfers between devices, send_pieces(): received.append(lax.ppermute(pieces[shift], axis, pairs))  6.02 us
    pallas_call x1, Pallas kernels, attend(): pl.pallas_call(functools.partial(attend_kernel, columns, group), out_shap...  3.76 us
    pallas_call x1, Pallas kernels, project(): pl.pallas_call(functools.partial(project_kernel, heads_here), out_shape=[...  3.47 us
    ppermute x6, waiting for transfers between devices, send_pieces(): received.append(lax.ppermute(pieces[shift], axis, pairs))  3.35 us
    pallas_call x1, Pallas kernels, lookup_rows(): pl.pallas_call(lookup_kernel, out_shape=jax.ShapeDtypeStruct((chunks, row...  2.33 us
  transfers between devices with their start and end apart: 6, of which 6 were waited for; matrix products, arithmetic and copies ran while one was open for 0% of the time, Pallas kernels for 0%

profile of v3, /device:TPU:0, one launch (start us, length us, event | category | flops | bytes accessed | tf_op | source)
XLA Modules:
  0.0 87.4 jit_solution(9206170756495481100)
XLA Ops:
  0.0 0.7 broadcast_add_fusion
  0.7 0.1 add_convert_fusion.1
  0.7 0.1 convert_element_type.33
  0.8 0.1 fusion
  1.0 0.1 pad_maximum_fusion
  1.1 0.7 copy-done.6
  1.8 2.3 %lookup.1 = bf16[8,32,512]{2,1,0:T(8,128)(2,1)S(1)} custom-call(s32[2,16]{1,0:T(2,128)S(1)} %copy-done.6, bf16[8016,4096]{1,0:T(8,128)(2,1)} %table.1), custom_call_target="tpu_custom_call" | custom-call | flops 131072 | bytes 2097152 | tf_op jit(solution)/shard_map/lookup/pallas_call | solution.py:92
  4.1 0.0 copy-start.1
  4.1 16.6 %all_to_all.25.parts = bf16[8,32,512]{2,1,0:T(8,128)(2,1)S(1)} all-to-all(bf16[8,32,512]{2,1,0:T(8,128)(2,1)S(1)} %lookup.1), channel_id=1, replica_groups=mesh['head'=4,'ctx'=8] {'ctx'}, dimensions={0} | all-to-all | bytes 524288 | tf_op jit(solution)/shard_map/all_to_all | solution.py:36
  20.8 12.1 %all_to_all.26.x = bf16[8,32,512]{2,1,0:T(8,128)(2,1)S(1)} all-to-all(bf16[8,32,512]{2,1,0:T(8,128)(2,1)S(1)} %join.1), channel_id=1, replica_groups=mesh['head'=4,'ctx'=8] {'ctx'}, dimensions={0} | all-to-all | bytes 524288 | tf_op jit(solution)/shard_map/all_to_all | solution.py:36
  32.9 3.5 %project.1 = (f32[32,384]{1,0:T(8,128)S(1)}, f32[32,384]{1,0:T(8,128)S(1)}, f32[32,384]{1,0:T(8,128)S(1)}, f32[32,384]{1,0:T(8,128)S(1)}) custom-call(bf16[8,32,512]{2,1,0:T(8,128)(2,1)S(1)} %all_to_all.26.x, f32[1,4096]{1,0:T(1,128)S(1)} %bitcast.9, bf16[8,160,4096]{2,1,0:T(8,128)(2,1)S(1)} %bitcast.4), custom_call_target="tpu_custom_call" | custom-call | flops 335544320 | bytes 10485760 | tf_op jit(solution)/shard_map/project/pallas_call | solution.py:165
  36.3 0.1 collective-permute-start
  36.4 1.6 %collective-permute-start.1 = (f32[32,384]{1,0:T(8,128)S(1)}, f32[32,384]{1,0:T(8,128)S(1)}, u32[]{:S(2)}, u32[]{:S(2)}) collective-permute-start(f32[32,384]{1,0:T(8,128)S(1)} %get-tuple-element.29), channel_id=1, source_target_pairs={{0,16},{8,24},{16,0},{24,8},{1,17},{9,25},{17,1},{25,9},{2,18},{10... | collective-permute-start | bytes 147464 | tf_op jit(solution)/shard_map/ppermute | solution.py:44
  38.0 1.4 %collective-permute-start.2 = (f32[32,384]{1,0:T(8,128)S(1)}, f32[32,384]{1,0:T(8,128)S(1)}, u32[]{:S(2)}, u32[]{:S(2)}) collective-permute-start(f32[32,384]{1,0:T(8,128)S(1)} %get-tuple-element.30), channel_id=1, source_target_pairs={{0,24},{8,0},{16,8},{24,16},{1,25},{9,1},{17,9},{25,17},{2,26},{10... | collective-permute-start | bytes 147464 | tf_op jit(solution)/shard_map/ppermute | solution.py:44
  39.4 0.6 collective-permute-done.refs_1_
  39.9 0.7 collective-permute-done.1.refs_2_
  40.6 0.5 collective-permute-done.2.refs_3_
  41.1 0.1 norm.1
  41.2 12.2 %all_to_all.27.united = bf16[8,32,384]{2,1,0:T(8,128)(2,1)S(1)} all-to-all(bf16[8,32,384]{2,1,0:T(8,128)(2,1)S(1)} %norm.1), channel_id=1, replica_groups=mesh['head'=4,'ctx'=8] {'ctx'}, dimensions={0} | all-to-all | bytes 393216 | tf_op jit(solution)/shard_map/all_to_all | solution.py:36
  53.4 3.8 %attend.1 = (bf16[8,96,128]{2,1,0:T(8,128)(2,1)S(1)}, bf16[8,2,32,128]{3,2,1,0:T(8,128)(2,1)S(1)}, bf16[4,32,128]{2,1,0:T(8,128)(2,1)S(1)}) custom-call(bf16[8,32,384]{2,1,0:T(8,128)(2,1)S(1)} %all_to_all.27.united, f32[32,128]{1,0:T(8,128)S(1)} %get-tuple-element.31.cosine, f32[32,128]{1,0:T(8,128)S(1)} %get-tuple-element.32.sine, ...), custom_call_target="tpu_custom_call" | custom-call | flops 1073741824 | bytes 4194304 | tf_op jit(solution)/shard_map/attend/pallas_call | solution.py:286
  57.2 1.2 %near.1 = (f32[64,128]{1,0:T(8,128)S(1)}, f32[64,128]{1,0:T(8,128)S(1)}, f32[64,128]{1,0:T(8,128)S(1)}) custom-call(s32[16]{0:T(128)S(1)} %copy-done.7, bf16[8,2,32,128]{3,2,1,0:T(8,128)(2,1)S(1)} %get-tuple-element.34.ready, bf16[4,32,128]{2,1,0:T(8,128)(2,1)S(1)} %get-tuple-element.35.fresh, bf16[2,256,128]{2,1,0:T(8,128)(2,1)S(1)} %bitcast.7, ...), custom_call_target="tpu_custom_call" | custom-call | flops 16777216 | bytes 262144 | tf_op jit(solution)/shard_map/near/pallas_call | solution.py:353
  58.4 11.1 %all_to_all.28.parts = bf16[8,96,128]{2,1,0:T(8,128)(2,1)S(1)} all-to-all(bf16[8,96,128]{2,1,0:T(8,128)(2,1)S(1)} %get-tuple-element.39), channel_id=1, replica_groups=mesh['head'=4,'ctx'=8] {'ctx'}, dimensions={0} | all-to-all | bytes 393216 | tf_op jit(solution)/shard_map/all_to_all | solution.py:36
  69.5 0.8 merge.1
  70.2 10.3 %all_to_all.29.x = bf16[8,4,2048]{2,1,0:T(4,128)(2,1)S(1)} all-to-all(bf16[8,4,2048]{2,1,0:T(4,128)(2,1)S(1)} %merge.1), channel_id=1, replica_groups=mesh['head'=4,'ctx'=8] {'ctx'}, dimensions={0} | all-to-all | bytes 262144 | tf_op jit(solution)/shard_map/all_to_all | solution.py:36
  80.5 1.6 %output.1 = (bf16[8,2048]{1,0:T(8,128)(2,1)S(1)}, bf16[8,2048]{1,0:T(8,128)(2,1)S(1)}, bf16[8,2048]{1,0:T(8,128)(2,1)S(1)}, bf16[8,2048]{1,0:T(8,128)(2,1)S(1)}) custom-call(bf16[8,4,2048]{2,1,0:T(4,128)(2,1)S(1)} %all_to_all.29.x, bf16[2048,2048]{1,0:T(8,128)(2,1)S(1)} %bitcast.6), custom_call_target="tpu_custom_call" | custom-call | flops 268435456 | bytes 8388608 | tf_op jit(solution)/shard_map/output/pallas_call | solution.py:453
  82.1 0.1 collective-permute-start.3
  82.2 1.6 %collective-permute-start.4 = (bf16[8,2048]{1,0:T(8,128)(2,1)S(1)}, bf16[8,2048]{1,0:T(8,128)(2,1)S(1)}, u32[]{:S(2)}, u32[]{:S(2)}) collective-permute-start(bf16[8,2048]{1,0:T(8,128)(2,1)S(1)} %get-tuple-element.45), channel_id=1, source_target_pairs={{0,16},{8,24},{16,0},{24,8},{1,17},{9,25},{17,1},{25,9},{2,18},{10... | collective-permute-start | bytes 98312 | tf_op jit(solution)/shard_map/ppermute | solution.py:44
  83.8 1.4 %collective-permute-start.5 = (bf16[8,2048]{1,0:T(8,128)(2,1)S(1)}, bf16[8,2048]{1,0:T(8,128)(2,1)S(1)}, u32[]{:S(2)}, u32[]{:S(2)}) collective-permute-start(bf16[8,2048]{1,0:T(8,128)(2,1)S(1)} %get-tuple-element.46), channel_id=1, source_target_pairs={{0,24},{8,0},{16,8},{24,16},{1,25},{9,1},{17,9},{25,17},{2,26},{10... | collective-permute-start | bytes 98312 | tf_op jit(solution)/shard_map/ppermute | solution.py:44
  85.1 0.4 collective-permute-done.3
  85.5 0.7 collective-permute-done.4
  86.2 0.6 collective-permute-done.5
  86.8 0.6 reshape.39
  (22 shorter events, 0.1 us)
Async XLA Ops:
  1.1 0.7 copy-start.6
  1.8 31.1 %copy-start = (bf16[4096,8,160]{0,2,1:T(8,128)(2,1)S(1)}, bf16[4096,8,160]{0,2,1:T(8,128)(2,1)}, u32[]{:S(2)}) copy-start(bf16[4096,8,160]{0,2,1:T(8,128)(2,1)} %param.14) | copy-start | bytes 31457284
  1.8 31.1 %copy-start.5 = (f32[4096]{0:T(1024)S(1)}, f32[4096]{0:T(1024)}, u32[]{:S(2)}) copy-start(f32[4096]{0:T(1024)} %param.13) | copy-start | bytes 49156
  4.1 49.3 %copy-start.1 = (bf16[2,4096,128]{2,1,0:T(8,128)(2,1)S(1)}, bf16[2,4096,128]{2,1,0:T(8,128)(2,1)}, u32[]{:S(2)}) copy-start(bf16[2,4096,128]{2,1,0:T(8,128)(2,1)} %keys.1) | copy-start | bytes 6291460
  4.1 49.3 %copy-start.2 = (bf16[2,4096,128]{2,1,0:T(8,128)(2,1)S(1)}, bf16[2,4096,128]{2,1,0:T(8,128)(2,1)}, u32[]{:S(2)}) copy-start(bf16[2,4096,128]{2,1,0:T(8,128)(2,1)} %values.1) | copy-start | bytes 6291460
  20.7 36.4 %copy-start.3 = (bf16[2,128,2,128]{3,2,1,0:T(2,128)(2,1)S(1)}, bf16[2,128,2,128]{3,2,1,0:T(2,128)(2,1)}, u32[]{:S(2)}) copy-start(bf16[2,128,2,128]{3,2,1,0:T(2,128)(2,1)} %param.18) | copy-start | bytes 393220
  20.7 36.4 %copy-start.4 = (bf16[2,128,2,128]{3,2,1,0:T(2,128)(2,1)S(1)}, bf16[2,128,2,128]{3,2,1,0:T(2,128)(2,1)}, u32[]{:S(2)}) copy-start(bf16[2,128,2,128]{3,2,1,0:T(2,128)(2,1)} %param.19) | copy-start | bytes 393220
  20.8 36.4 %copy-start.7 = (s32[16]{0:T(128)S(1)}, s32[16]{0:T(128)}, u32[]{:S(2)}) copy-start(s32[16]{0:T(128)} %lengths.1) | copy-start | bytes 196
  32.9 47.7 %slice-start = ((s8[8388608]{0:T(1024)(128)(4,1)}), s8[4194304]{0:T(1024)(128)(4,1)S(1)}, s32[]{:S(2)}) async-start(s8[8388608]{0:T(1024)(128)(4,1)} %bitcast.5), calls=%async_computation.5 | async-start | bytes 8388608
  32.9 47.7 %slice-start.1 = ((s8[8388608]{0:T(1024)(128)(4,1)}), s8[4194304]{0:T(1024)(128)(4,1)S(1)}, s32[]{:S(2)}) async-start(s8[8388608]{0:T(1024)(128)(4,1)} %bitcast.5), calls=%async_computation.6 | async-start | bytes 8388608
  36.3 3.6 %collective-permute-start = (f32[32,384]{1,0:T(8,128)S(1)}, f32[32,384]{1,0:T(8,128)S(1)}, u32[]{:S(2)}, u32[]{:S(2)}) collective-permute-start(f32[32,384]{1,0:T(8,128)S(1)} %get-tuple-element.28), channel_id=1, source_target_pairs={{0,8},{8,16},{16,24},{24,0},{1,9},{9,17},{17,25},{25,1},{2,10},{10... | collective-permute-start | bytes 147464 | tf_op jit(solution)/shard_map/ppermute | solution.py:44
  36.4 4.2 %collective-permute-start.1 = (f32[32,384]{1,0:T(8,128)S(1)}, f32[32,384]{1,0:T(8,128)S(1)}, u32[]{:S(2)}, u32[]{:S(2)}) collective-permute-start(f32[32,384]{1,0:T(8,128)S(1)} %get-tuple-element.29), channel_id=1, source_target_pairs={{0,16},{8,24},{16,0},{24,8},{1,17},{9,25},{17,1},{25,9},{2,18},{10... | collective-permute-start | bytes 147464 | tf_op jit(solution)/shard_map/ppermute | solution.py:44
  38.0 3.1 %collective-permute-start.2 = (f32[32,384]{1,0:T(8,128)S(1)}, f32[32,384]{1,0:T(8,128)S(1)}, u32[]{:S(2)}, u32[]{:S(2)}) collective-permute-start(f32[32,384]{1,0:T(8,128)S(1)} %get-tuple-element.30), channel_id=1, source_target_pairs={{0,24},{8,0},{16,8},{24,16},{1,25},{9,1},{17,9},{25,17},{2,26},{10... | collective-permute-start | bytes 147464 | tf_op jit(solution)/shard_map/ppermute | solution.py:44
  82.1 3.4 %collective-permute-start.3 = (bf16[8,2048]{1,0:T(8,128)(2,1)S(1)}, bf16[8,2048]{1,0:T(8,128)(2,1)S(1)}, u32[]{:S(2)}, u32[]{:S(2)}) collective-permute-start(bf16[8,2048]{1,0:T(8,128)(2,1)S(1)} %get-tuple-element.44), channel_id=1, source_target_pairs={{0,8},{8,16},{16,24},{24,0},{1,9},{9,17},{17,25},{25,1},{2,10},{10... | collective-permute-start | bytes 98312 | tf_op jit(solution)/shard_map/ppermute | solution.py:44
  82.2 4.0 %collective-permute-start.4 = (bf16[8,2048]{1,0:T(8,128)(2,1)S(1)}, bf16[8,2048]{1,0:T(8,128)(2,1)S(1)}, u32[]{:S(2)}, u32[]{:S(2)}) collective-permute-start(bf16[8,2048]{1,0:T(8,128)(2,1)S(1)} %get-tuple-element.45), channel_id=1, source_target_pairs={{0,16},{8,24},{16,0},{24,8},{1,17},{9,25},{17,1},{25,9},{2,18},{10... | collective-permute-start | bytes 98312 | tf_op jit(solution)/shard_map/ppermute | solution.py:44
  83.8 3.0 %collective-permute-start.5 = (bf16[8,2048]{1,0:T(8,128)(2,1)S(1)}, bf16[8,2048]{1,0:T(8,128)(2,1)S(1)}, u32[]{:S(2)}, u32[]{:S(2)}) collective-permute-start(bf16[8,2048]{1,0:T(8,128)(2,1)S(1)} %get-tuple-element.46), channel_id=1, source_target_pairs={{0,24},{8,0},{16,8},{24,16},{1,25},{9,1},{17,9},{25,17},{2,26},{10... | collective-permute-start | bytes 98312 | tf_op jit(solution)/shard_map/ppermute | solution.py:44

commit v4 on v3

--- a/solution.py
+++ b/solution.py
@@ -45,14 +45,44 @@
     return received
 
 
-def lookup_kernel(tokens, table, out, blocks, rows_f32, sem):
-    steps, batch = tokens.shape
-    chunks, rows, width = out.shape
+def token_at(tokens, row):
+    steps = tokens.shape[0]
+    return tokens[row % steps, row // steps]
+
+
+def assign_slots(tokens, rows, owners, local_rows, capacity):
+    lanes = round_up(rows, LANES)
+    down = lax.broadcasted_iota(jnp.int32, (rows, lanes), 0)
+    across = lax.broadcasted_iota(jnp.int32, (rows, lanes), 1)
+    column = jnp.zeros((rows, lanes), jnp.int32)
+    line = jnp.full((rows, lanes), -1, jnp.int32)
+    for row in range(rows):
+        token = token_at(tokens, row)
+        column = jnp.where(down == row, token, column)
+        line = jnp.where(across == row, token, line)
+    owner_column = jnp.zeros((rows, lanes), F32)
+    owner_line = jnp.zeros((rows, lanes), F32)
+    for owner in range(1, owners):
+        owner_column += jnp.where(column >= owner * local_rows, 1.0, 0.0)
+        owner_line += jnp.where(line >= owner * local_rows, 1.0, 0.0)
+    same = jnp.where(column == line, 1.0, 0.0)
+    index = across.astype(F32)
+    earliest = jnp.min(jnp.where(same > 0, index, float(lanes)), axis=1, keepdims=True)
+    repeated = jnp.max(jnp.where(down < across, same, 0.0), axis=0, keepdims=True)
+    counted = jnp.where((repeated == 0) & (across < rows) & (index < earliest), 1.0, 0.0)
+    slot = jnp.sum(jnp.where(owner_column == owner_line, counted, 0.0), axis=1, keepdims=True)
+    place = jnp.where(slot < capacity, owner_column[:, :1] * capacity + slot, -1.0)
+    first = earliest == down[:, :1].astype(F32)
+    return place, first
+
+
+def fetch_rows(tokens, table, blocks, rows_f32, sem, between=None):
+    rows = rows_f32.shape[0]
     local_rows = table.shape[0]
     base = lax.axis_index("ctx") * local_rows
 
-    def place(row):
-        offset = tokens[row % steps, row // steps] - base
+    def find(row):
+        offset = token_at(tokens, row) - base
         return offset, (offset >= 0) & (offset < local_rows)
 
     def copy(row, offset):
@@ -62,16 +92,17 @@
         )
 
     for row in range(rows):
-        offset, inside = place(row)
+        offset, inside = find(row)
 
         @pl.when(inside)
         def _():
             copy(row, offset).start()
 
     rows_f32[...] = jnp.zeros_like(rows_f32)
+    result = None if between is None else between()
     sublane = lax.broadcasted_iota(jnp.int32, (8, 1), 0)
     for row in range(rows):
-        offset, inside = place(row)
+        offset, inside = find(row)
 
         @pl.when(inside)
         def _():
@@ -79,30 +110,102 @@
             picked = jnp.where(sublane == offset % 8, blocks[row].astype(F32), 0.0)
             rows_f32[row : row + 1, :] = jnp.sum(picked, axis=0, keepdims=True)
 
+    return result
+
+
+def lookup_kernel(owners, tokens, table, packed, places, crowded, blocks, rows_f32, sem):
+    capacity, _ = packed.shape
+    rows = rows_f32.shape[0]
+
+    def between():
+        return assign_slots(tokens, rows, owners, table.shape[0], capacity)
+
+    place, first = fetch_rows(tokens, table, blocks, rows_f32, sem, between)
+    places[...] = jnp.broadcast_to(place, places.shape)
+    crowded[0] = jnp.max(jnp.where(place < 0, 1, 0))
+    slot = lax.broadcasted_iota(jnp.int32, (rows, capacity), 1) + lax.axis_index("ctx") * capacity
+    chosen = jnp.where((place == slot.astype(F32)) & first, 1.0, 0.0).astype(BF16)
+    packed[...] = lax.dot_general(
+        chosen, rows_f32[...].astype(BF16), (((0,), (0,)), ((), ())), preferred_element_type=F32
+    ).astype(BF16)
+
+
+def rest_kernel(tokens, places, table, out, blocks, rows_f32, sem):
+    chunks, rows, width = out.shape
+    fetch_rows(tokens, table, blocks, rows_f32, sem)
+    left = places[...][:, :1] < 0
     for chunk in range(chunks):
-        out[chunk] = rows_f32[:, chunk * width : (chunk + 1) * width].astype(BF16)
-
-
-def lookup_rows(token_ids, embedding):
+        found = rows_f32[:, chunk * width : (chunk + 1) * width]
+        out[chunk] = jnp.where(left, found, 0.0).astype(BF16)
+
+
+def fetch_scratch(rows, width):
+    return [
+        pltpu.VMEM((rows, 8, width), BF16),
+        pltpu.VMEM((rows, width), F32),
+        pltpu.SemaphoreType.DMA((rows,)),
+    ]
+
+
+def spread_kernel(block, first, out):
+    for target in range(out.shape[0]):
+        out[target] = block[...]
+
+
+def spread(block, first, hint):
+    count = lax.axis_size("ctx")
+    return pl.pallas_call(
+        spread_kernel,
+        out_shape=jax.ShapeDtypeStruct((count,) + block.shape, block.dtype),
+        in_specs=[VMEM, HBM],
+        out_specs=VMEM,
+        compiler_params=params(8 * MIB),
+        cost_estimate=cost(400 * hint, hint),
+        name="spread",
+    )(block, first)
+
+
+def lookup_packed(token_ids, embedding, capacity):
+    steps, batch = token_ids.shape
+    rows = steps * batch
+    owners = lax.axis_size("ctx")
+    _, width = embedding.shape
+    return pl.pallas_call(
+        functools.partial(lookup_kernel, owners),
+        out_shape=[
+            jax.ShapeDtypeStruct((capacity, width), BF16),
+            jax.ShapeDtypeStruct((rows, LANES), F32),
+            jax.ShapeDtypeStruct((1,), jnp.int32),
+        ],
+        in_specs=[SMEM, HBM],
+        out_specs=[VMEM, VMEM, SMEM],
+        scratch_shapes=fetch_scratch(rows, width),
+        compiler_params=params(6 * rows * width * 8),
+        cost_estimate=cost(rows * width, rows * width * 16),
+        name="lookup",
+    )(token_ids, embedding)
+
+
+def lookup_rest(token_ids, places, embedding):
+    rows = places.shape[0]
+    chunks = lax.axis_size("ctx")
+    _, width = embedding.shape
+    return pl.pallas_call(
+        rest_kernel,
+        out_shape=jax.ShapeDtypeStruct((chunks, rows, width // chunks), BF16),
+        in_specs=[SMEM, VMEM, HBM],
+        out_specs=VMEM,
+        scratch_shapes=fetch_scratch(rows, width),
+        compiler_params=params(6 * rows * width * 8),
+        name="rest",
+    )(token_ids, places, embedding)
+
+
+def lookup_all(token_ids, embedding):
     steps, batch = token_ids.shape
     rows = steps * batch
     chunks = lax.axis_size("ctx")
     local_rows, width = embedding.shape
-    if local_rows % 8 == 0:
-        return pl.pallas_call(
-            lookup_kernel,
-            out_shape=jax.ShapeDtypeStruct((chunks, rows, width // chunks), BF16),
-            in_specs=[SMEM, HBM],
-            out_specs=VMEM,
-            scratch_shapes=[
-                pltpu.VMEM((rows, 8, width), BF16),
-                pltpu.VMEM((rows, width), F32),
-                pltpu.SemaphoreType.DMA((rows,)),
-            ],
-            compiler_params=params(6 * rows * width * 8),
-            cost_estimate=cost(rows * width, rows * width * 16),
-            name="lookup",
-        )(token_ids, embedding)
     offsets = token_ids.T.reshape(rows) - lax.axis_index("ctx") * local_rows
     inside = (offsets >= 0) & (offsets < local_rows)
     picked = jnp.take(embedding, jnp.clip(offsets, 0, local_rows - 1), axis=0)
@@ -130,16 +233,25 @@
     )(parts)
 
 
-def project_kernel(heads_here, x, gain, weight, *refs):
+def project_kernel(heads_here, packed, x, gain, weight, *refs):
+    if packed:
+        slots, places, *refs = refs
     count = weight.shape[0] // heads_here
     outs, scaled = refs[:count], refs[count]
     chunks, rows, chunk_width = x.shape
+    if packed:
+        owners, capacity, width = slots.shape
+        held = slots[...].astype(F32).reshape(owners * capacity, width).astype(BF16)
+        slot = lax.broadcasted_iota(jnp.int32, (rows, owners * capacity), 1).astype(F32)
+        chosen = jnp.where(places[...][:, :1] == slot, 1.0, 0.0).astype(BF16)
     columns = weight.shape[1]
     here = lax.axis_index("head")
     squares = jnp.zeros((rows, 1), F32)
     for chunk in range(chunks):
         span = slice(chunk * chunk_width, (chunk + 1) * chunk_width)
         features = x[chunk].astype(F32)
+        if packed:
+            features += jnp.dot(chosen, held[:, span], preferred_element_type=F32)
         squares = squares + jnp.sum(features * features, axis=-1, keepdims=True)
         scaled[:, span] = (features * gain[:, span]).astype(BF16)
     used = heads_here * columns
@@ -155,7 +267,7 @@
         )
 
 
-def project(x, attn_gain, weight):
+def project(x, attn_gain, weight, packed=()):
     count = lax.axis_size("head")
     chunks, rows, chunk_width = x.shape
     heads, columns, width = weight.shape
@@ -163,15 +275,15 @@
     wide = round_up(heads_here * columns + 1, LANES)
     size = weight.size * 2
     return pl.pallas_call(
-        functools.partial(project_kernel, heads_here),
+        functools.partial(project_kernel, heads_here, bool(packed)),
         out_shape=[jax.ShapeDtypeStruct((rows, wide), F32)] * count,
-        in_specs=[VMEM, VMEM, VMEM],
+        in_specs=[VMEM] * (3 + len(packed)),
         out_specs=[VMEM] * count,
         scratch_shapes=[pltpu.VMEM((rows, width), BF16)],
         compiler_params=params(8 * MIB),
         cost_estimate=cost(2 * rows * weight.size, size),
         name="project",
-    )(x, attn_gain.reshape(1, width), weight)
+    )(x, attn_gain.reshape(1, width), weight, *packed)
 
 
 def norm_kernel(used, model_width, *refs):
@@ -493,10 +605,24 @@
     sine = jnp.concatenate([-sine, sine], axis=1)
 
     token_ids, cosine, sine = lax.optimization_barrier((token_ids, cosine, sine))
-    picked = lookup_rows(token_ids, embedding)
-    joined = join_copies(exchange(picked, "ctx"))
-    features = exchange(joined, "ctx")
-    pieces = project(features, attn_gain, jnp.transpose(qkv_weight, (1, 2, 0)))
+    capacity = 2 * rows // n_ctx
+    qkv_weight = jnp.transpose(qkv_weight, (1, 2, 0))
+    if embedding.shape[0] % 8 == 0 and capacity % 8 == 0:
+        packed, places, crowded = lookup_packed(token_ids, embedding, capacity)
+
+        def rest():
+            found = lookup_rest(token_ids, places, embedding)
+            return exchange(join_copies(exchange(found, "ctx")), "ctx")
+
+        def nothing():
+            return jnp.zeros((n_ctx, rows, width // n_ctx), BF16)
+
+        features = lax.cond(crowded[0] > 0, rest, nothing)
+        packed = exchange(spread(packed, features, 4 * qkv_weight.size), "ctx")
+        pieces = project(features, attn_gain, qkv_weight, (packed, places))
+    else:
+        joined = join_copies(exchange(lookup_all(token_ids, embedding), "ctx"))
+        pieces = project(exchange(joined, "ctx"), attn_gain, qkv_weight)
     pieces = send_pieces(pieces, "head")
     united = norm_copies(pieces, heads * columns, width * n_head)
     united = exchange(united, "ctx")

time: 87.8 us -> 82.1 us (0.935)
  blocking collectives: 62.2 us -> 55.3 us
  Pallas kernels: 13.2 us -> 14.4 us
    all_to_all x5 -> x4, blocking collectives: 62.2 us -> 55.3 us  [exchange(): return lax.all_to_all(blocks, axis, 0, 0)]
    pallas_call x3, Pallas kernels: 5.84 us -> 6.99 us  [the longest x1 3.71 us: project(): pl.pallas_call(functools.partial(project_kernel, heads_here, bool(packed)...]
where the time goes in v4:
time: 82.1 us; the launch traced here: 81.7 us
  blocking collectives  55.3 us (67%)
  Pallas kernels  14.4 us (18%)
  starting transfers between devices  6.01 us (7%)
  waiting for transfers between devices  3.35 us (4%)
  other arithmetic  0.99 us (1%)
  between operations  0.84 us (1%)
    all_to_all x4, blocking collectives, exchange(): return lax.all_to_all(blocks, axis, 0, 0)  55.3 us
    ppermute x6, starting transfers between devices, send_pieces(): received.append(lax.ppermute(pieces[shift], axis, pairs))  6.01 us
    pallas_call x1, Pallas kernels, attend(): pl.pallas_call(functools.partial(attend_kernel, columns, group), out_shap...  3.81 us
    pallas_call x1, Pallas kernels, project(): pl.pallas_call(functools.partial(project_kernel, heads_here, bool(packed)...  3.71 us
    ppermute x6, waiting for transfers between devices, send_pieces(): received.append(lax.ppermute(pieces[shift], axis, pairs))  3.35 us
    pallas_call x1, Pallas kernels, lookup_packed(): pl.pallas_call(functools.partial(lookup_kernel, owners), out_shape=[jax.S...  3.24 us
  transfers between devices with their start and end apart: 6, of which 6 were waited for; matrix products, arithmetic and copies ran while one was open for 0% of the time, Pallas kernels for 0%

profile of v4, /device:TPU:0, one launch (start us, length us, event | category | flops | bytes accessed | tf_op | source)
XLA Modules:
  0.0 81.7 jit_solution(11498656800442574439)
XLA Ops:
  0.0 0.7 broadcast_add_fusion
  0.7 0.1 add_convert_fusion.1
  0.7 0.1 convert_element_type.39
  0.8 0.1 fusion
  1.0 0.1 pad_maximum_fusion
  1.1 3.2 %lookup.1 = (bf16[8,4096]{1,0:T(8,128)(2,1)S(1)}, f32[32,128]{1,0:T(8,128)S(1)}, s32[1]{0:T(128)}) custom-call(s32[2,16]{1,0:T(2,128)} %tokens, bf16[8016,4096]{1,0:T(8,128)(2,1)} %table.1), custom_call_target="tpu_custom_call" | custom-call | flops 131072 | bytes 2097152 | tf_op jit(solution)/shard_map/lookup/pallas_call | solution.py:173
  5.0 0.0 copy-start
  5.0 0.0 copy-start.5
  5.1 0.0 copy-start.1
  5.1 21.7 %all_to_all.30.refs_0_ = bf16[8,8,4096]{2,1,0:T(8,128)(2,1)S(1)} all-to-all(bf16[8,8,4096]{2,1,0:T(8,128)(2,1)S(1)} %spread.1), channel_id=1, replica_groups=mesh['head'=4,'ctx'=8] {'ctx'}, dimensions={0} | all-to-all | bytes 1048576 | tf_op jit(solution)/shard_map/all_to_all | solution.py:36
  26.9 3.7 %project.1 = (f32[32,384]{1,0:T(8,128)S(1)}, f32[32,384]{1,0:T(8,128)S(1)}, f32[32,384]{1,0:T(8,128)S(1)}, f32[32,384]{1,0:T(8,128)S(1)}) custom-call(bf16[8,32,512]{2,1,0:T(8,128)(2,1)S(1)} %get-tuple-element.70.first.x, f32[1,4096]{1,0:T(1,128)S(1)} %bitcast.10, bf16[8,160,4096]{2,1,0:T(8,128)(2,1)S(1)} %bitcast.5, ...), custom_call_target="tpu_custom_call" | custom-call | flops 335544320 | bytes 10485760 | tf_op jit(solution)/shard_map/project/pallas_call | solution.py:277
  30.6 0.1 collective-permute-start
  30.6 1.6 %collective-permute-start.1 = (f32[32,384]{1,0:T(8,128)S(1)}, f32[32,384]{1,0:T(8,128)S(1)}, u32[]{:S(2)}, u32[]{:S(2)}) collective-permute-start(f32[32,384]{1,0:T(8,128)S(1)} %get-tuple-element.47), channel_id=1, source_target_pairs={{0,16},{8,24},{16,0},{24,8},{1,17},{9,25},{17,1},{25,9},{2,18},{10... | collective-permute-start | bytes 147464 | tf_op jit(solution)/shard_map/ppermute | solution.py:44
  32.2 1.4 %collective-permute-start.2 = (f32[32,384]{1,0:T(8,128)S(1)}, f32[32,384]{1,0:T(8,128)S(1)}, u32[]{:S(2)}, u32[]{:S(2)}) collective-permute-start(f32[32,384]{1,0:T(8,128)S(1)} %get-tuple-element.48), channel_id=1, source_target_pairs={{0,24},{8,0},{16,8},{24,16},{1,25},{9,1},{17,9},{25,17},{2,26},{10... | collective-permute-start | bytes 147464 | tf_op jit(solution)/shard_map/ppermute | solution.py:44
  33.6 0.6 collective-permute-done.refs_1_
  34.1 0.7 collective-permute-done.1.refs_2_
  34.8 0.5 collective-permute-done.2.refs_3_
  35.3 0.1 norm.1
  35.4 12.2 %all_to_all.31.united = bf16[8,32,384]{2,1,0:T(8,128)(2,1)S(1)} all-to-all(bf16[8,32,384]{2,1,0:T(8,128)(2,1)S(1)} %norm.1), channel_id=1, replica_groups=mesh['head'=4,'ctx'=8] {'ctx'}, dimensions={0} | all-to-all | bytes 393216 | tf_op jit(solution)/shard_map/all_to_all | solution.py:36
  47.6 3.8 %attend.1 = (bf16[8,96,128]{2,1,0:T(8,128)(2,1)S(1)}, bf16[8,2,32,128]{3,2,1,0:T(8,128)(2,1)S(1)}, bf16[4,32,128]{2,1,0:T(8,128)(2,1)S(1)}) custom-call(bf16[8,32,384]{2,1,0:T(8,128)(2,1)S(1)} %all_to_all.31.united, f32[32,128]{1,0:T(8,128)S(1)} %get-tuple-element.49.cosine, f32[32,128]{1,0:T(8,128)S(1)} %get-tuple-element.50.sine, ...), custom_call_target="tpu_custom_call" | custom-call | flops 1073741824 | bytes 4194304 | tf_op jit(solution)/shard_map/attend/pallas_call | solution.py:398
  51.5 1.2 %near.1 = (f32[64,128]{1,0:T(8,128)S(1)}, f32[64,128]{1,0:T(8,128)S(1)}, f32[64,128]{1,0:T(8,128)S(1)}) custom-call(s32[16]{0:T(128)S(1)} %copy-done.6, bf16[8,2,32,128]{3,2,1,0:T(8,128)(2,1)S(1)} %get-tuple-element.52.ready, bf16[4,32,128]{2,1,0:T(8,128)(2,1)S(1)} %get-tuple-element.53.fresh, bf16[2,256,128]{2,1,0:T(8,128)(2,1)S(1)} %bitcast.8, ...), custom_call_target="tpu_custom_call" | custom-call | flops 16777216 | bytes 262144 | tf_op jit(solution)/shard_map/near/pallas_call | solution.py:465
  52.6 11.1 %all_to_all.32.parts = bf16[8,96,128]{2,1,0:T(8,128)(2,1)S(1)} all-to-all(bf16[8,96,128]{2,1,0:T(8,128)(2,1)S(1)} %get-tuple-element.57), channel_id=1, replica_groups=mesh['head'=4,'ctx'=8] {'ctx'}, dimensions={0} | all-to-all | bytes 393216 | tf_op jit(solution)/shard_map/all_to_all | solution.py:36
  63.8 0.8 merge.1
  64.5 10.3 %all_to_all.33.x = bf16[8,4,2048]{2,1,0:T(4,128)(2,1)S(1)} all-to-all(bf16[8,4,2048]{2,1,0:T(4,128)(2,1)S(1)} %merge.1), channel_id=1, replica_groups=mesh['head'=4,'ctx'=8] {'ctx'}, dimensions={0} | all-to-all | bytes 262144 | tf_op jit(solution)/shard_map/all_to_all | solution.py:36
  74.8 1.6 %output.1 = (bf16[8,2048]{1,0:T(8,128)(2,1)S(1)}, bf16[8,2048]{1,0:T(8,128)(2,1)S(1)}, bf16[8,2048]{1,0:T(8,128)(2,1)S(1)}, bf16[8,2048]{1,0:T(8,128)(2,1)S(1)}) custom-call(bf16[8,4,2048]{2,1,0:T(4,128)(2,1)S(1)} %all_to_all.33.x, bf16[2048,2048]{1,0:T(8,128)(2,1)S(1)} %bitcast.7), custom_call_target="tpu_custom_call" | custom-call | flops 268435456 | bytes 8388608 | tf_op jit(solution)/shard_map/output/pallas_call | solution.py:565
  76.4 0.1 collective-permute-start.3
  76.5 1.6 %collective-permute-start.4 = (bf16[8,2048]{1,0:T(8,128)(2,1)S(1)}, bf16[8,2048]{1,0:T(8,128)(2,1)S(1)}, u32[]{:S(2)}, u32[]{:S(2)}) collective-permute-start(bf16[8,2048]{1,0:T(8,128)(2,1)S(1)} %get-tuple-element.63), channel_id=1, source_target_pairs={{0,16},{8,24},{16,0},{24,8},{1,17},{9,25},{17,1},{25,9},{2,18},{10... | collective-permute-start | bytes 98312 | tf_op jit(solution)/shard_map/ppermute | solution.py:44
  78.0 1.4 %collective-permute-start.5 = (bf16[8,2048]{1,0:T(8,128)(2,1)S(1)}, bf16[8,2048]{1,0:T(8,128)(2,1)S(1)}, u32[]{:S(2)}, u32[]{:S(2)}) collective-permute-start(bf16[8,2048]{1,0:T(8,128)(2,1)S(1)} %get-tuple-element.64), channel_id=1, source_target_pairs={{0,24},{8,0},{16,8},{24,16},{1,25},{9,1},{17,9},{25,17},{2,26},{10... | collective-permute-start | bytes 98312 | tf_op jit(solution)/shard_map/ppermute | solution.py:44
  79.4 0.4 collective-permute-done.3
  79.8 0.7 collective-permute-done.4
  80.4 0.6 collective-permute-done.5
  81.0 0.6 reshape.43
  (23 shorter events, 0.2 us)
Async XLA Ops:
  1.1 3.9 %copy-start.7 = (s32[2,16]{1,0:T(2,128)S(1)}, s32[2,16]{1,0:T(2,128)}, u32[]{:S(2)}) copy-start(s32[2,16]{1,0:T(2,128)} %tokens) | copy-start | bytes 388
  5.0 21.8 %copy-start = (bf16[4096,8,160]{0,2,1:T(8,128)(2,1)S(1)}, bf16[4096,8,160]{0,2,1:T(8,128)(2,1)}, u32[]{:S(2)}) copy-start(bf16[4096,8,160]{0,2,1:T(8,128)(2,1)} %param.16) | copy-start | bytes 31457284
  5.0 21.8 %copy-start.5 = (f32[4096]{0:T(1024)S(1)}, f32[4096]{0:T(1024)}, u32[]{:S(2)}) copy-start(f32[4096]{0:T(1024)} %param.15) | copy-start | bytes 49156
  5.1 42.5 %copy-start.1 = (bf16[2,4096,128]{2,1,0:T(8,128)(2,1)S(1)}, bf16[2,4096,128]{2,1,0:T(8,128)(2,1)}, u32[]{:S(2)}) copy-start(bf16[2,4096,128]{2,1,0:T(8,128)(2,1)} %keys.1) | copy-start | bytes 6291460
  5.1 42.5 %copy-start.2 = (bf16[2,4096,128]{2,1,0:T(8,128)(2,1)S(1)}, bf16[2,4096,128]{2,1,0:T(8,128)(2,1)}, u32[]{:S(2)}) copy-start(bf16[2,4096,128]{2,1,0:T(8,128)(2,1)} %values.1) | copy-start | bytes 6291460
  26.8 24.6 %copy-start.3 = (bf16[2,128,2,128]{3,2,1,0:T(2,128)(2,1)S(1)}, bf16[2,128,2,128]{3,2,1,0:T(2,128)(2,1)}, u32[]{:S(2)}) copy-start(bf16[2,128,2,128]{3,2,1,0:T(2,128)(2,1)} %param.20) | copy-start | bytes 393220
  26.8 24.6 %copy-start.4 = (bf16[2,128,2,128]{3,2,1,0:T(2,128)(2,1)S(1)}, bf16[2,128,2,128]{3,2,1,0:T(2,128)(2,1)}, u32[]{:S(2)}) copy-start(bf16[2,128,2,128]{3,2,1,0:T(2,128)(2,1)} %param.21) | copy-start | bytes 393220
  26.8 24.6 %copy-start.6 = (s32[16]{0:T(128)S(1)}, s32[16]{0:T(128)}, u32[]{:S(2)}) copy-start(s32[16]{0:T(128)} %lengths.1) | copy-start | bytes 196
  26.8 48.0 %slice-start = ((s8[8388608]{0:T(1024)(128)(4,1)}), s8[4194304]{0:T(1024)(128)(4,1)S(1)}, s32[]{:S(2)}) async-start(s8[8388608]{0:T(1024)(128)(4,1)} %bitcast.6), calls=%async_computation.6 | async-start | bytes 8388608
  26.8 48.0 %slice-start.1 = ((s8[8388608]{0:T(1024)(128)(4,1)}), s8[4194304]{0:T(1024)(128)(4,1)S(1)}, s32[]{:S(2)}) async-start(s8[8388608]{0:T(1024)(128)(4,1)} %bitcast.6), calls=%async_computation.7 | async-start | bytes 8388608
  30.6 3.6 %collective-permute-start = (f32[32,384]{1,0:T(8,128)S(1)}, f32[32,384]{1,0:T(8,128)S(1)}, u32[]{:S(2)}, u32[]{:S(2)}) collective-permute-start(f32[32,384]{1,0:T(8,128)S(1)} %get-tuple-element.46), channel_id=1, source_target_pairs={{0,8},{8,16},{16,24},{24,0},{1,9},{9,17},{17,25},{25,1},{2,10},{10... | collective-permute-start | bytes 147464 | tf_op jit(solution)/shard_map/ppermute | solution.py:44
  30.6 4.2 %collective-permute-start.1 = (f32[32,384]{1,0:T(8,128)S(1)}, f32[32,384]{1,0:T(8,128)S(1)}, u32[]{:S(2)}, u32[]{:S(2)}) collective-permute-start(f32[32,384]{1,0:T(8,128)S(1)} %get-tuple-element.47), channel_id=1, source_target_pairs={{0,16},{8,24},{16,0},{24,8},{1,17},{9,25},{17,1},{25,9},{2,18},{10... | collective-permute-start | bytes 147464 | tf_op jit(solution)/shard_map/ppermute | solution.py:44
  32.2 3.1 %collective-permute-start.2 = (f32[32,384]{1,0:T(8,128)S(1)}, f32[32,384]{1,0:T(8,128)S(1)}, u32[]{:S(2)}, u32[]{:S(2)}) collective-permute-start(f32[32,384]{1,0:T(8,128)S(1)} %get-tuple-element.48), channel_id=1, source_target_pairs={{0,24},{8,0},{16,8},{24,16},{1,25},{9,1},{17,9},{25,17},{2,26},{10... | collective-permute-start | bytes 147464 | tf_op jit(solution)/shard_map/ppermute | solution.py:44
  76.4 3.4 %collective-permute-start.3 = (bf16[8,2048]{1,0:T(8,128)(2,1)S(1)}, bf16[8,2048]{1,0:T(8,128)(2,1)S(1)}, u32[]{:S(2)}, u32[]{:S(2)}) collective-permute-start(bf16[8,2048]{1,0:T(8,128)(2,1)S(1)} %get-tuple-element.62), channel_id=1, source_target_pairs={{0,8},{8,16},{16,24},{24,0},{1,9},{9,17},{17,25},{25,1},{2,10},{10... | collective-permute-start | bytes 98312 | tf_op jit(solution)/shard_map/ppermute | solution.py:44
  76.5 4.0 %collective-permute-start.4 = (bf16[8,2048]{1,0:T(8,128)(2,1)S(1)}, bf16[8,2048]{1,0:T(8,128)(2,1)S(1)}, u32[]{:S(2)}, u32[]{:S(2)}) collective-permute-start(bf16[8,2048]{1,0:T(8,128)(2,1)S(1)} %get-tuple-element.63), channel_id=1, source_target_pairs={{0,16},{8,24},{16,0},{24,8},{1,17},{9,25},{17,1},{25,9},{2,18},{10... | collective-permute-start | bytes 98312 | tf_op jit(solution)/shard_map/ppermute | solution.py:44
  78.0 3.0 %collective-permute-start.5 = (bf16[8,2048]{1,0:T(8,128)(2,1)S(1)}, bf16[8,2048]{1,0:T(8,128)(2,1)S(1)}, u32[]{:S(2)}, u32[]{:S(2)}) collective-permute-start(bf16[8,2048]{1,0:T(8,128)(2,1)S(1)} %get-tuple-element.64), channel_id=1, source_target_pairs={{0,24},{8,0},{16,8},{24,16},{1,25},{9,1},{17,9},{25,17},{2,26},{10... | collective-permute-start | bytes 98312 | tf_op jit(solution)/shard_map/ppermute | solution.py:44

commit v5 on v4

--- a/solution.py
+++ b/solution.py
@@ -2,6 +2,7 @@
 
 import jax
 import jax.numpy as jnp
+import numpy as np
 from jax import lax
 from jax.experimental import pallas as pl
 from jax.experimental.pallas import tpu as pltpu
@@ -76,6 +77,39 @@
     return place, first
 
 
+def rotary_tables(lengths, steps, rows, context, head_dim):
+    half = head_dim // 2
+    down = lax.broadcasted_iota(jnp.int32, (rows, head_dim), 0)
+    across = lax.broadcasted_iota(jnp.int32, (1, head_dim), 1)
+    frequency = jnp.zeros((1, head_dim), F32)
+    for i in range(half):
+        value = float(np.float32(ROTARY_THETA ** (-2.0 * i / head_dim)))
+        frequency = jnp.where(across % half == i, value, frequency)
+    length = jnp.zeros((rows, head_dim), jnp.int32)
+    for sequence in range(rows // steps):
+        length = jnp.where(down // steps == sequence, lengths[sequence], length)
+    positions = (context + length + down % steps).astype(F32)
+    angles = positions * frequency
+    sine = jnp.sin(angles)
+    return jnp.cos(angles), jnp.where(across < half, -sine, sine)
+
+
+def tables_kernel(steps, context, lengths, cosine, sine):
+    rows, head_dim = cosine.shape
+    cosine[...], sine[...] = rotary_tables(lengths, steps, rows, context, head_dim)
+
+
+def tables(lengths, steps, rows, context, head_dim):
+    return pl.pallas_call(
+        functools.partial(tables_kernel, steps, context),
+        out_shape=[jax.ShapeDtypeStruct((rows, head_dim), F32)] * 2,
+        in_specs=[SMEM],
+        out_specs=[VMEM] * 2,
+        compiler_params=params(8 * MIB),
+        name="tables",
+    )(lengths)
+
+
 def fetch_rows(tokens, table, blocks, rows_f32, sem, between=None):
     rows = rows_f32.shape[0]
     local_rows = table.shape[0]
@@ -113,11 +147,14 @@
     return result
 
 
-def lookup_kernel(owners, tokens, table, packed, places, crowded, blocks, rows_f32, sem):
+def lookup_kernel(
+    owners, context, tokens, lengths, table, packed, places, crowded, cosine, sine, blocks, rows_f32, sem
+):
     capacity, _ = packed.shape
-    rows = rows_f32.shape[0]
+    rows, head_dim = cosine.shape
 
     def between():
+        cosine[...], sine[...] = rotary_tables(lengths, tokens.shape[0], rows, context, head_dim)
         return assign_slots(tokens, rows, owners, table.shape[0], capacity)
 
     place, first = fetch_rows(tokens, table, blocks, rows_f32, sem, between)
@@ -165,25 +202,27 @@
     )(block, first)
 
 
-def lookup_packed(token_ids, embedding, capacity):
+def lookup_packed(token_ids, lengths, embedding, capacity, context, head_dim):
     steps, batch = token_ids.shape
     rows = steps * batch
     owners = lax.axis_size("ctx")
     _, width = embedding.shape
     return pl.pallas_call(
-        functools.partial(lookup_kernel, owners),
+        functools.partial(lookup_kernel, owners, context),
         out_shape=[
             jax.ShapeDtypeStruct((capacity, width), BF16),
             jax.ShapeDtypeStruct((rows, LANES), F32),
             jax.ShapeDtypeStruct((1,), jnp.int32),
+            jax.ShapeDtypeStruct((rows, head_dim), F32),
+            jax.ShapeDtypeStruct((rows, head_dim), F32),
         ],
-        in_specs=[SMEM, HBM],
-        out_specs=[VMEM, VMEM, SMEM],
+        in_specs=[SMEM, SMEM, HBM],
+        out_specs=[VMEM, VMEM, SMEM, VMEM, VMEM],
         scratch_shapes=fetch_scratch(rows, width),
         compiler_params=params(6 * rows * width * 8),
         cost_estimate=cost(rows * width, rows * width * 16),
         name="lookup",
-    )(token_ids, embedding)
+    )(token_ids, lengths, embedding)
 
 
 def lookup_rest(token_ids, places, embedding):
@@ -315,21 +354,73 @@
     return first, second, value - first - second
 
 
-def attend_kernel(columns, group, united, cosine, sine, keys, values, packet, ready, fresh, *scratch):
-    query_buf, score_buf = scratch
+def near_block(query, fresh_key, fresh_value, keys, values, head, heads, steps, lengths):
+    owned, slots_all, _ = keys.shape
+    block = query.shape[0]
+    rows = fresh_key.shape[0]
+    mine = lax.axis_index("ctx")
+
+    def iota(shape, axis):
+        return lax.broadcasted_iota(jnp.int32, shape, axis)
+
+    query_place = iota((block, 1), 0) % (owned * steps)
+    sequence = query_place // steps
+    step = query_place % steps
+    slot = iota((1, slots_all), 1)
+    fresh_row = iota((1, rows), 1)
+    fresh_here = (fresh_row // steps == mine * owned + sequence) & (fresh_row % steps <= step)
+    fresh_scores = lax.dot_general(query, fresh_key, NT, preferred_element_type=F32)
+    scores = [jnp.where(fresh_here, fresh_scores, MASKED)]
+    highest = jnp.max(scores[0], axis=-1, keepdims=True)
+    for s in range(owned):
+        found = lax.dot_general(query, keys[s], NT, preferred_element_type=F32)
+        live = (sequence == s) & (slot % heads == head)
+        live = live & (slot // heads < lengths[mine * owned + s])
+        found = jnp.where(live, found, MASKED)
+        scores.append(found)
+        highest = jnp.maximum(highest, jnp.max(found, axis=-1, keepdims=True))
+    total = jnp.zeros((block, 1), F32)
+    result = jnp.zeros((block, fresh_value.shape[1]), F32)
+    for found, value in zip(scores, [fresh_value] + [values[s] for s in range(owned)]):
+        weights = jnp.exp(found - highest).astype(BF16)
+        total = total + jnp.sum(weights.astype(F32), axis=-1, keepdims=True)
+        result = result + jnp.dot(weights, value, preferred_element_type=F32)
+    return highest, total, result
+
+
+def attend_kernel(
+    columns,
+    group,
+    owned,
+    lengths,
+    united,
+    cosine,
+    sine,
+    keys,
+    values,
+    slot_keys,
+    slot_values,
+    packet,
+    near_sums,
+    near_maxima,
+    near_totals,
+    query_buf,
+    score_buf,
+):
     chunks, rows, _ = united.shape
     heads, context, head_dim = keys.shape
     per_dest = rows // chunks
     block = per_dest * group
     tile = min(512, context)
     tiles = context // tile
-
     cos = cosine[...]
     sin = sine[...]
+    mine = lax.axis_index("ctx")
 
     def rotated(vectors):
         return vectors * cos + pltpu.roll(vectors, head_dim // 2, 1) * sin
 
+    fresh = []
     for head in range(heads):
         first = head * columns
         whole = jnp.concatenate(
@@ -343,15 +434,14 @@
                 query_buf[head, start : start + per_dest, :] = query[
                     dest * per_dest : (dest + 1) * per_dest
                 ]
-        new_key = whole[:, group * head_dim : (group + 1) * head_dim]
-        fresh[head] = rotated(new_key).astype(BF16)
-        fresh[heads + head] = whole[:, (group + 1) * head_dim :].astype(BF16)
+        new_key = rotated(whole[:, group * head_dim : (group + 1) * head_dim])
+        new_value = whole[:, (group + 1) * head_dim :]
+        fresh.append((new_key.astype(BF16), new_value.astype(BF16)))
 
     lane = lax.broadcasted_iota(jnp.int32, (chunks * block, LANES), 1)
+    table = jnp.zeros((chunks * block, LANES), F32)
     for head in range(heads):
         query = query_buf[head].astype(BF16)
-        for dest in range(chunks):
-            ready[dest, head] = query[dest * block : (dest + 1) * block]
         highest = None
         for step in range(tiles):
             span = slice(step * tile, (step + 1) * tile)
@@ -373,37 +463,54 @@
             for part in range(tile // LANES):
                 totals = totals + wide[:, part * LANES : (part + 1) * LANES]
         total = jnp.sum(totals, axis=-1, keepdims=True)
-        table = jnp.zeros((chunks * block, LANES), F32)
         for index, piece in enumerate(split3(maxima) + split3(total)):
-            table = jnp.where(lane == index, piece, table)
+            table = jnp.where(lane == head * 8 + index, piece, table)
         rounded = sums.astype(BF16)
         for dest in range(chunks):
             packet[dest, head * block : (head + 1) * block] = rounded[
                 dest * block : (dest + 1) * block
             ]
-        turned = jnp.transpose(table)[:16]
-        for dest in range(chunks):
-            packet[dest, heads * block + head * 16 : heads * block + (head + 1) * 16, :block] = turned[
-                :, dest * block : (dest + 1) * block
-            ].astype(BF16)
-
-
-def attend(united, columns, cosine, sine, keys, values):
+        own_query = query_buf[head, pl.ds(pl.multiple_of(mine * block, block), block), :]
+        near_max, near_total, near_sum = near_block(
+            own_query.astype(BF16),
+            *fresh[head],
+            slot_keys,
+            slot_values,
+            head,
+            heads,
+            per_dest // owned,
+            lengths,
+        )
+        span = slice(head * block, (head + 1) * block)
+        near_sums[span, :] = near_sum
+        near_maxima[span, :] = jnp.broadcast_to(near_max, (block, head_dim))
+        near_totals[span, :] = jnp.broadcast_to(near_total, (block, head_dim))
+    low = heads * block
+    pieces = packet.shape[1] - low
+    turned = jnp.transpose(table)[:pieces]
+    for dest in range(chunks):
+        packet[dest, low:, :block] = turned[:, dest * block : (dest + 1) * block].astype(BF16)
+
+
+def attend(united, columns, cosine, sine, keys, values, lengths, slot_keys, slot_values):
     chunks, rows, _ = united.shape
     heads, context, head_dim = keys.shape
+    owned, slots, _, _ = slot_keys.shape
     group = columns * chunks // head_dim - 2
     block = rows // chunks * group
     size = keys.size * 2
     flat = chunks * block
-    return pl.pallas_call(
-        functools.partial(attend_kernel, columns, group),
+    near = jax.ShapeDtypeStruct((heads * block, head_dim), F32)
+    return pl.pallas_call(
+        functools.partial(attend_kernel, columns, group, owned),
         out_shape=[
-            jax.ShapeDtypeStruct((chunks, heads * (block + 16), head_dim), BF16),
-            jax.ShapeDtypeStruct((chunks, heads, block, head_dim), BF16),
-            jax.ShapeDtypeStruct((2 * heads, rows, head_dim), BF16),
+            jax.ShapeDtypeStruct((chunks, heads * block + round_up(heads * 8, 16), head_dim), BF16),
+            near,
+            near,
+            near,
         ],
-        in_specs=[VMEM] * 5,
-        out_specs=[VMEM] * 3,
+        in_specs=[SMEM] + [VMEM] * 7,
+        out_specs=[VMEM] * 4,
         scratch_shapes=[
             pltpu.VMEM((heads, flat, head_dim), F32),
             pltpu.VMEM((flat, context), F32),
@@ -411,71 +518,15 @@
         compiler_params=params(flat * context * 4 + 12 * MIB),
         cost_estimate=cost(4 * heads * flat * context * head_dim, 2 * size, heads * flat * context),
         name="attend",
-    )(united, cosine, sine, keys, values)
-
-
-def near_kernel(owned, lengths, ready, fresh, keys, values, sums, maxima, totals):
-    heads, rows, head_dim = fresh.shape
-    heads //= 2
-    _, _, block, _ = ready.shape
-    slots_all = keys.shape[1]
-    per_dest = rows // ready.shape[0]
-    steps = per_dest // owned
-    mine = lax.axis_index("ctx")
-
-    def iota(shape, axis):
-        return lax.broadcasted_iota(jnp.int32, shape, axis)
-
-    query_place = iota((block, 1), 0) % per_dest
-    sequence = query_place // steps
-    step = query_place % steps
-    slot = iota((1, slots_all), 1)
-    fresh_row = iota((1, rows), 1)
-    fresh_here = (fresh_row // steps == mine * owned + sequence) & (fresh_row % steps <= step)
-    for head in range(heads):
-        query = ready[mine, head]
-        fresh_scores = lax.dot_general(query, fresh[head], NT, preferred_element_type=F32)
-        fresh_scores = jnp.where(fresh_here, fresh_scores, MASKED)
-        scores = []
-        highest = jnp.max(fresh_scores, axis=-1, keepdims=True)
-        for s in range(owned):
-            found = lax.dot_general(query, keys[s], NT, preferred_element_type=F32)
-            live = (sequence == s) & (slot % heads == head)
-            live = live & (slot // heads < lengths[mine * owned + s])
-            found = jnp.where(live, found, MASKED)
-            scores.append(found)
-            highest = jnp.maximum(highest, jnp.max(found, axis=-1, keepdims=True))
-        weights = jnp.exp(fresh_scores - highest).astype(BF16)
-        total = jnp.sum(weights.astype(F32), axis=-1, keepdims=True)
-        result = jnp.dot(weights, fresh[heads + head], preferred_element_type=F32)
-        for s in range(owned):
-            weights = jnp.exp(scores[s] - highest).astype(BF16)
-            total = total + jnp.sum(weights.astype(F32), axis=-1, keepdims=True)
-            result = result + jnp.dot(weights, values[s], preferred_element_type=F32)
-        span = slice(head * block, (head + 1) * block)
-        sums[span, :] = result
-        maxima[span, :] = jnp.broadcast_to(highest, (block, head_dim))
-        totals[span, :] = jnp.broadcast_to(total, (block, head_dim))
-
-
-def near(lengths, ready, fresh, keys, values):
-    owned, slots, heads, head_dim = keys.shape
-    block = ready.shape[2]
-    shape = jax.ShapeDtypeStruct((heads * block, head_dim), F32)
-    return pl.pallas_call(
-        functools.partial(near_kernel, owned),
-        out_shape=[shape] * 3,
-        in_specs=[SMEM, VMEM, VMEM, VMEM, VMEM],
-        out_specs=[VMEM] * 3,
-        compiler_params=params(8 * MIB),
-        cost_estimate=cost(4 * heads * block * owned * slots * heads * head_dim, keys.size * 4),
-        name="near",
     )(
         lengths,
-        ready,
-        fresh,
-        keys.reshape(owned, slots * heads, head_dim),
-        values.reshape(owned, slots * heads, head_dim),
+        united,
+        cosine,
+        sine,
+        keys,
+        values,
+        slot_keys.reshape(owned, slots * heads, head_dim),
+        slot_values.reshape(owned, slots * heads, head_dim),
     )
 
 
@@ -487,17 +538,14 @@
     heads = queries // block
     highest = near_maxima[...][:, :1]
     maxima, totals = [], []
+    pieces = parts.shape[1] - queries
     for source in range(chunks):
-        for head in range(heads):
-            low = queries + head * 16
-            found = parts[source, low : low + 16, :].astype(F32)[:8]
-            row = (source * heads + head) * 8
-            stats[row : row + 8, :] = found
+        stats[source * pieces : (source + 1) * pieces, :] = parts[source, queries:, :].astype(F32)
     turned = jnp.transpose(stats[...])[:block]
     for source in range(chunks):
         m, t = [], []
         for head in range(heads):
-            column = (source * heads + head) * 8
+            column = source * pieces + head * 8
             get = lambda k: turned[:, column + k : column + k + 1]
             m.append(get(0) + get(1) + get(2))
             t.append(get(3) + get(4) + get(5))
@@ -533,7 +581,7 @@
         out_specs=VMEM,
         scratch_shapes=[
             pltpu.VMEM((per_dest, width), F32),
-            pltpu.VMEM((chunks * heads * 8, head_dim), F32),
+            pltpu.VMEM((chunks * (parts.shape[1] - queries), head_dim), F32),
         ],
         compiler_params=params(12 * MIB),
         name="merge",
@@ -594,21 +642,13 @@
     width = embedding.shape[1]
     columns = qkv_weight.shape[2]
     group = columns * n_ctx // head_dim - 2
-    step_index = jnp.arange(steps, dtype=jnp.int32)
-    positions = block_context * n_ctx + suffix_lengths[:, None] + step_index[None, :]
-    positions = positions.astype(F32).reshape(rows)
-    half = head_dim // 2
-    frequency = ROTARY_THETA ** (-2.0 * jnp.arange(half).astype(F32) / head_dim)
-    angles = positions[:, None] * frequency
-    cosine, sine = jnp.cos(angles), jnp.sin(angles)
-    cosine = jnp.concatenate([cosine, cosine], axis=1)
-    sine = jnp.concatenate([-sine, sine], axis=1)
-
-    token_ids, cosine, sine = lax.optimization_barrier((token_ids, cosine, sine))
+    context = block_context * n_ctx
     capacity = 2 * rows // n_ctx
     qkv_weight = jnp.transpose(qkv_weight, (1, 2, 0))
     if embedding.shape[0] % 8 == 0 and capacity % 8 == 0:
-        packed, places, crowded = lookup_packed(token_ids, embedding, capacity)
+        packed, places, crowded, cosine, sine = lookup_packed(
+            token_ids, suffix_lengths, embedding, capacity, context, head_dim
+        )
 
         def rest():
             found = lookup_rest(token_ids, places, embedding)
@@ -621,14 +661,23 @@
         packed = exchange(spread(packed, features, 4 * qkv_weight.size), "ctx")
         pieces = project(features, attn_gain, qkv_weight, (packed, places))
     else:
+        cosine, sine = tables(suffix_lengths, steps, rows, context, head_dim)
         joined = join_copies(exchange(lookup_all(token_ids, embedding), "ctx"))
         pieces = project(exchange(joined, "ctx"), attn_gain, qkv_weight)
     pieces = send_pieces(pieces, "head")
     united = norm_copies(pieces, heads * columns, width * n_head)
     united = exchange(united, "ctx")
-    packet, ready, fresh = attend(united, columns, cosine, sine, prefix_keys, prefix_values)
-    sums, maxima, totals = near(suffix_lengths, ready, fresh, suffix_keys, suffix_values)
-    packet, sums, maxima, totals = lax.optimization_barrier((packet, sums, maxima, totals))
+    packet, sums, maxima, totals = attend(
+        united,
+        columns,
+        cosine,
+        sine,
+        prefix_keys,
+        prefix_values,
+        suffix_lengths,
+        suffix_keys,
+        suffix_values,
+    )
     parts = exchange(packet, "ctx")
     attention = merge_copies(parts, sums, maxima, totals, group, rows // n_ctx)
     attention = exchange(attention, "ctx")

time: 82.1 us -> 80.8 us (0.984)
  other arithmetic: 0.99 us -> 0.02 us
    pallas_call x3 -> x2, Pallas kernels: 8.24 us -> 7.82 us  [the longest x1 4.73 us: attend(): pl.pallas_call(functools.partial(attend_kernel, columns, group, owned), o...]
where the time goes in v5:
time: 80.8 us; the launch traced here: 80.3 us
  blocking collectives  54.7 us (68%)
  Pallas kernels  14 us (17%)
  starting transfers between devices  6.02 us (7%)
  waiting for transfers between devices  3.35 us (4%)
  local copies, waits for them, and re-layouts  1.38 us (2%)
  between operations  0.82 us (1%)
    all_to_all x4, blocking collectives, exchange(): return lax.all_to_all(blocks, axis, 0, 0)  54.7 us
    ppermute x6, starting transfers between devices, send_pieces(): received.append(lax.ppermute(pieces[shift], axis, pairs))  6.02 us
    pallas_call x1, Pallas kernels, attend(): pl.pallas_call(functools.partial(attend_kernel, columns, group, owned), o...  4.73 us
    pallas_call x1, Pallas kernels, project(): pl.pallas_call(functools.partial(project_kernel, heads_here, bool(packed)...  3.7 us
    ppermute x6, waiting for transfers between devices, send_pieces(): received.append(lax.ppermute(pieces[shift], axis, pairs))  3.35 us
    pallas_call x1, Pallas kernels, lookup_packed(): pl.pallas_call(functools.partial(lookup_kernel, owners, context), out_sha...  3.08 us
  transfers between devices with their start and end apart: 6, of which 6 were waited for; matrix products, arithmetic and copies ran while one was open for 0% of the time, Pallas kernels for 0%

profile of v5, /device:TPU:0, one launch (start us, length us, event | category | flops | bytes accessed | tf_op | source)
XLA Modules:
  0.0 80.3 jit_solution(12938542134596210485)
XLA Ops:
  0.0 0.7 copy-done.6
  0.7 3.1 %lookup.1 = (bf16[8,4096]{1,0:T(8,128)(2,1)S(1)}, f32[32,128]{1,0:T(8,128)S(1)}, s32[1]{0:T(128)}, f32[32,128]{1,0:T(8,128)S(1)}, f32[32,128]{1,0:T(8,128)S(1)}) custom-call(s32[2,16]{1,0:T(2,128)} %tokens.1, s32[16]{0:T(128)S(1)} %copy-done.6, bf16[8016,4096]{1,0:T(8,128)(2,1)} %table.1), custom_call_target="tpu_custom_call" | custom-call | flops 131072 | bytes 2097152 | tf_op jit(solution)/shard_map/lookup/pallas_call | solution.py:210
  4.5 0.0 copy-start
  4.5 0.0 copy-start.5
  4.5 0.0 copy-start.1
  4.5 0.0 copy-start.2
  4.5 0.0 copy-start.3
  4.6 0.0 copy-start.4
  4.6 0.0 copy-start.7
  4.6 21.8 %all_to_all.30.refs_0_ = bf16[8,8,4096]{2,1,0:T(8,128)(2,1)S(1)} all-to-all(bf16[8,8,4096]{2,1,0:T(8,128)(2,1)S(1)} %spread.1), channel_id=1, replica_groups=mesh['head'=4,'ctx'=8] {'ctx'}, dimensions={0} | all-to-all | bytes 1048576 | tf_op jit(solution)/shard_map/all_to_all | solution.py:37
  26.4 3.7 %project.1 = (f32[32,384]{1,0:T(8,128)S(1)}, f32[32,384]{1,0:T(8,128)S(1)}, f32[32,384]{1,0:T(8,128)S(1)}, f32[32,384]{1,0:T(8,128)S(1)}) custom-call(bf16[8,32,512]{2,1,0:T(8,128)(2,1)S(1)} %get-tuple-element.51.first.x, f32[1,4096]{1,0:T(1,128)S(1)} %bitcast.10, bf16[8,160,4096]{2,1,0:T(8,128)(2,1)S(1)} %bitcast.5, ...), custom_call_target="tpu_custom_call" | custom-call | flops 335544320 | bytes 10485760 | tf_op jit(solution)/shard_map/project/pallas_call | solution.py:316
  30.1 0.1 collective-permute-start
  30.2 1.6 %collective-permute-start.1 = (f32[32,384]{1,0:T(8,128)S(1)}, f32[32,384]{1,0:T(8,128)S(1)}, u32[]{:S(2)}, u32[]{:S(2)}) collective-permute-start(f32[32,384]{1,0:T(8,128)S(1)} %get-tuple-element.39), channel_id=1, source_target_pairs={{0,16},{8,24},{16,0},{24,8},{1,17},{9,25},{17,1},{25,9},{2,18},{10... | collective-permute-start | bytes 147464 | tf_op jit(solution)/shard_map/ppermute | solution.py:45
  31.8 1.4 %collective-permute-start.2 = (f32[32,384]{1,0:T(8,128)S(1)}, f32[32,384]{1,0:T(8,128)S(1)}, u32[]{:S(2)}, u32[]{:S(2)}) collective-permute-start(f32[32,384]{1,0:T(8,128)S(1)} %get-tuple-element.40), channel_id=1, source_target_pairs={{0,24},{8,0},{16,8},{24,16},{1,25},{9,1},{17,9},{25,17},{2,26},{10... | collective-permute-start | bytes 147464 | tf_op jit(solution)/shard_map/ppermute | solution.py:45
  33.2 0.6 collective-permute-done.refs_1_
  33.7 0.7 collective-permute-done.1.refs_2_
  34.4 0.5 collective-permute-done.2.refs_3_
  34.9 0.1 norm.1
  35.0 12.2 %all_to_all.31.united = bf16[8,32,384]{2,1,0:T(8,128)(2,1)S(1)} all-to-all(bf16[8,32,384]{2,1,0:T(8,128)(2,1)S(1)} %norm.1), channel_id=1, replica_groups=mesh['head'=4,'ctx'=8] {'ctx'}, dimensions={0} | all-to-all | bytes 393216 | tf_op jit(solution)/shard_map/all_to_all | solution.py:37
  47.2 0.0 copy-done.1
  47.2 4.7 %attend.1 = (bf16[8,80,128]{2,1,0:T(8,128)(2,1)S(1)}, f32[64,128]{1,0:T(8,128)S(1)}, f32[64,128]{1,0:T(8,128)S(1)}, f32[64,128]{1,0:T(8,128)S(1)}) custom-call(s32[16]{0:T(128)S(1)} %copy-done.7, bf16[8,32,384]{2,1,0:T(8,128)(2,1)S(1)} %all_to_all.31.united, f32[32,128]{1,0:T(8,128)S(1)} %get-tuple-element.41.cosine, f32[32,128]{1,0:T(8,128)S(1)} %get-tuple-element.42.sine, ...), custom_call_target="tpu_custom_call" | custom-call | flops 1073741824 | bytes 4194304 | tf_op jit(solution)/shard_map/attend/pallas_call | solution.py:504
  52.0 10.6 %all_to_all.32.parts = bf16[8,80,128]{2,1,0:T(8,128)(2,1)S(1)} all-to-all(bf16[8,80,128]{2,1,0:T(8,128)(2,1)S(1)} %get-tuple-element.43), channel_id=1, replica_groups=mesh['head'=4,'ctx'=8] {'ctx'}, dimensions={0} | all-to-all | bytes 327680 | tf_op jit(solution)/shard_map/all_to_all | solution.py:37
  62.6 0.8 merge.1
  63.4 10.1 %all_to_all.33.x = bf16[8,4,2048]{2,1,0:T(4,128)(2,1)S(1)} all-to-all(bf16[8,4,2048]{2,1,0:T(4,128)(2,1)S(1)} %merge.1), channel_id=1, replica_groups=mesh['head'=4,'ctx'=8] {'ctx'}, dimensions={0} | all-to-all | bytes 262144 | tf_op jit(solution)/shard_map/all_to_all | solution.py:37
  73.5 1.6 %output.1 = (bf16[8,2048]{1,0:T(8,128)(2,1)S(1)}, bf16[8,2048]{1,0:T(8,128)(2,1)S(1)}, bf16[8,2048]{1,0:T(8,128)(2,1)S(1)}, bf16[8,2048]{1,0:T(8,128)(2,1)S(1)}) custom-call(bf16[8,4,2048]{2,1,0:T(4,128)(2,1)S(1)} %all_to_all.33.x, bf16[2048,2048]{1,0:T(8,128)(2,1)S(1)} %bitcast.7), custom_call_target="tpu_custom_call" | custom-call | flops 268435456 | bytes 8388608 | tf_op jit(solution)/shard_map/output/pallas_call | solution.py:613
  75.0 0.1 collective-permute-start.3
  75.1 1.6 %collective-permute-start.4 = (bf16[8,2048]{1,0:T(8,128)(2,1)S(1)}, bf16[8,2048]{1,0:T(8,128)(2,1)S(1)}, u32[]{:S(2)}, u32[]{:S(2)}) collective-permute-start(bf16[8,2048]{1,0:T(8,128)(2,1)S(1)} %get-tuple-element.49), channel_id=1, source_target_pairs={{0,16},{8,24},{16,0},{24,8},{1,17},{9,25},{17,1},{25,9},{2,18},{10... | collective-permute-start | bytes 98312 | tf_op jit(solution)/shard_map/ppermute | solution.py:45
  76.7 1.4 %collective-permute-start.5 = (bf16[8,2048]{1,0:T(8,128)(2,1)S(1)}, bf16[8,2048]{1,0:T(8,128)(2,1)S(1)}, u32[]{:S(2)}, u32[]{:S(2)}) collective-permute-start(bf16[8,2048]{1,0:T(8,128)(2,1)S(1)} %get-tuple-element.50), channel_id=1, source_target_pairs={{0,24},{8,0},{16,8},{24,16},{1,25},{9,1},{17,9},{25,17},{2,26},{10... | collective-permute-start | bytes 98312 | tf_op jit(solution)/shard_map/ppermute | solution.py:45
  78.0 0.4 collective-permute-done.3
  78.4 0.7 collective-permute-done.4
  79.1 0.6 collective-permute-done.5
  79.7 0.6 reshape.19
  (18 shorter events, 0.1 us)
Async XLA Ops:
  0.0 0.7 copy-start.6
  0.7 3.7 %copy-start.8 = (s32[2,16]{1,0:T(2,128)S(1)}, s32[2,16]{1,0:T(2,128)}, u32[]{:S(2)}) copy-start(s32[2,16]{1,0:T(2,128)} %tokens.1) | copy-start | bytes 388
  4.5 22.0 %copy-start = (bf16[4096,8,160]{0,2,1:T(8,128)(2,1)S(1)}, bf16[4096,8,160]{0,2,1:T(8,128)(2,1)}, u32[]{:S(2)}) copy-start(bf16[4096,8,160]{0,2,1:T(8,128)(2,1)} %param.16) | copy-start | bytes 31457284
  4.5 22.0 %copy-start.5 = (f32[4096]{0:T(1024)S(1)}, f32[4096]{0:T(1024)}, u32[]{:S(2)}) copy-start(f32[4096]{0:T(1024)} %param.15) | copy-start | bytes 49156
  4.5 42.7 %copy-start.1 = (bf16[2,4096,128]{2,1,0:T(8,128)(2,1)S(1)}, bf16[2,4096,128]{2,1,0:T(8,128)(2,1)}, u32[]{:S(2)}) copy-start(bf16[2,4096,128]{2,1,0:T(8,128)(2,1)} %keys.1) | copy-start | bytes 6291460
  4.5 42.7 %copy-start.2 = (bf16[2,4096,128]{2,1,0:T(8,128)(2,1)S(1)}, bf16[2,4096,128]{2,1,0:T(8,128)(2,1)}, u32[]{:S(2)}) copy-start(bf16[2,4096,128]{2,1,0:T(8,128)(2,1)} %values.1) | copy-start | bytes 6291460
  4.5 42.7 %copy-start.3 = (bf16[2,128,2,128]{3,2,1,0:T(2,128)(2,1)S(1)}, bf16[2,128,2,128]{3,2,1,0:T(2,128)(2,1)}, u32[]{:S(2)}) copy-start(bf16[2,128,2,128]{3,2,1,0:T(2,128)(2,1)} %param.20) | copy-start | bytes 393220
  4.6 42.6 %copy-start.4 = (bf16[2,128,2,128]{3,2,1,0:T(2,128)(2,1)S(1)}, bf16[2,128,2,128]{3,2,1,0:T(2,128)(2,1)}, u32[]{:S(2)}) copy-start(bf16[2,128,2,128]{3,2,1,0:T(2,128)(2,1)} %param.21) | copy-start | bytes 393220
  4.6 42.6 %copy-start.7 = (s32[16]{0:T(128)S(1)}, s32[16]{0:T(128)}, u32[]{:S(2)}) copy-start(s32[16]{0:T(128)} %lengths.3) | copy-start | bytes 196
  26.4 47.0 %slice-start = ((s8[8388608]{0:T(1024)(128)(4,1)}), s8[4194304]{0:T(1024)(128)(4,1)S(1)}, s32[]{:S(2)}) async-start(s8[8388608]{0:T(1024)(128)(4,1)} %bitcast.6), calls=%async_computation.6 | async-start | bytes 8388608
  26.4 47.0 %slice-start.1 = ((s8[8388608]{0:T(1024)(128)(4,1)}), s8[4194304]{0:T(1024)(128)(4,1)S(1)}, s32[]{:S(2)}) async-start(s8[8388608]{0:T(1024)(128)(4,1)} %bitcast.6), calls=%async_computation.7 | async-start | bytes 8388608
  30.1 3.6 %collective-permute-start = (f32[32,384]{1,0:T(8,128)S(1)}, f32[32,384]{1,0:T(8,128)S(1)}, u32[]{:S(2)}, u32[]{:S(2)}) collective-permute-start(f32[32,384]{1,0:T(8,128)S(1)} %get-tuple-element.38), channel_id=1, source_target_pairs={{0,8},{8,16},{16,24},{24,0},{1,9},{9,17},{17,25},{25,1},{2,10},{10... | collective-permute-start | bytes 147464 | tf_op jit(solution)/shard_map/ppermute | solution.py:45
  30.2 4.2 %collective-permute-start.1 = (f32[32,384]{1,0:T(8,128)S(1)}, f32[32,384]{1,0:T(8,128)S(1)}, u32[]{:S(2)}, u32[]{:S(2)}) collective-permute-start(f32[32,384]{1,0:T(8,128)S(1)} %get-tuple-element.39), channel_id=1, source_target_pairs={{0,16},{8,24},{16,0},{24,8},{1,17},{9,25},{17,1},{25,9},{2,18},{10... | collective-permute-start | bytes 147464 | tf_op jit(solution)/shard_map/ppermute | solution.py:45
  31.8 3.1 %collective-permute-start.2 = (f32[32,384]{1,0:T(8,128)S(1)}, f32[32,384]{1,0:T(8,128)S(1)}, u32[]{:S(2)}, u32[]{:S(2)}) collective-permute-start(f32[32,384]{1,0:T(8,128)S(1)} %get-tuple-element.40), channel_id=1, source_target_pairs={{0,24},{8,0},{16,8},{24,16},{1,25},{9,1},{17,9},{25,17},{2,26},{10... | collective-permute-start | bytes 147464 | tf_op jit(solution)/shard_map/ppermute | solution.py:45
  75.0 3.4 %collective-permute-start.3 = (bf16[8,2048]{1,0:T(8,128)(2,1)S(1)}, bf16[8,2048]{1,0:T(8,128)(2,1)S(1)}, u32[]{:S(2)}, u32[]{:S(2)}) collective-permute-start(bf16[8,2048]{1,0:T(8,128)(2,1)S(1)} %get-tuple-element.48), channel_id=1, source_target_pairs={{0,8},{8,16},{16,24},{24,0},{1,9},{9,17},{17,25},{25,1},{2,10},{10... | collective-permute-start | bytes 98312 | tf_op jit(solution)/shard_map/ppermute | solution.py:45
  75.1 4.0 %collective-permute-start.4 = (bf16[8,2048]{1,0:T(8,128)(2,1)S(1)}, bf16[8,2048]{1,0:T(8,128)(2,1)S(1)}, u32[]{:S(2)}, u32[]{:S(2)}) collective-permute-start(bf16[8,2048]{1,0:T(8,128)(2,1)S(1)} %get-tuple-element.49), channel_id=1, source_target_pairs={{0,16},{8,24},{16,0},{24,8},{1,17},{9,25},{17,1},{25,9},{2,18},{10... | collective-permute-start | bytes 98312 | tf_op jit(solution)/shard_map/ppermute | solution.py:45
  76.7 3.0 %collective-permute-start.5 = (bf16[8,2048]{1,0:T(8,128)(2,1)S(1)}, bf16[8,2048]{1,0:T(8,128)(2,1)S(1)}, u32[]{:S(2)}, u32[]{:S(2)}) collective-permute-start(bf16[8,2048]{1,0:T(8,128)(2,1)S(1)} %get-tuple-element.50), channel_id=1, source_target_pairs={{0,24},{8,0},{16,8},{24,16},{1,25},{9,1},{17,9},{25,17},{2,26},{10... | collective-permute-start | bytes 98312 | tf_op jit(solution)/shard_map/ppermute | solution.py:45

commit v6 on v5

--- a/solution.py
+++ b/solution.py
@@ -37,11 +37,17 @@
     return lax.all_to_all(blocks, axis, 0, 0)
 
 
+def partner(here, shift, count):
+    if count & (count - 1) == 0:
+        return here ^ shift
+    return (here + shift) % count
+
+
 def send_pieces(pieces, axis):
     count = lax.axis_size(axis)
     received = [pieces[0]]
     for shift in range(1, count):
-        pairs = [(i, (i + shift) % count) for i in range(count)]
+        pairs = [(i, partner(i, shift, count)) for i in range(count)]
         received.append(lax.ppermute(pieces[shift], axis, pairs))
     return received
 
@@ -94,22 +100,6 @@
     return jnp.cos(angles), jnp.where(across < half, -sine, sine)
 
 
-def tables_kernel(steps, context, lengths, cosine, sine):
-    rows, head_dim = cosine.shape
-    cosine[...], sine[...] = rotary_tables(lengths, steps, rows, context, head_dim)
-
-
-def tables(lengths, steps, rows, context, head_dim):
-    return pl.pallas_call(
-        functools.partial(tables_kernel, steps, context),
-        out_shape=[jax.ShapeDtypeStruct((rows, head_dim), F32)] * 2,
-        in_specs=[SMEM],
-        out_specs=[VMEM] * 2,
-        compiler_params=params(8 * MIB),
-        name="tables",
-    )(lengths)
-
-
 def fetch_rows(tokens, table, blocks, rows_f32, sem, between=None):
     rows = rows_f32.shape[0]
     local_rows = table.shape[0]
@@ -148,13 +138,12 @@
 
 
 def lookup_kernel(
-    owners, context, tokens, lengths, table, packed, places, crowded, cosine, sine, blocks, rows_f32, sem
+    owners, tokens, table, packed, places, crowded, blocks, rows_f32, sem
 ):
     capacity, _ = packed.shape
-    rows, head_dim = cosine.shape
+    rows = rows_f32.shape[0]
 
     def between():
-        cosine[...], sine[...] = rotary_tables(lengths, tokens.shape[0], rows, context, head_dim)
         return assign_slots(tokens, rows, owners, table.shape[0], capacity)
 
     place, first = fetch_rows(tokens, table, blocks, rows_f32, sem, between)
@@ -202,27 +191,25 @@
     )(block, first)
 
 
-def lookup_packed(token_ids, lengths, embedding, capacity, context, head_dim):
+def lookup_packed(token_ids, embedding, capacity):
     steps, batch = token_ids.shape
     rows = steps * batch
     owners = lax.axis_size("ctx")
     _, width = embedding.shape
     return pl.pallas_call(
-        functools.partial(lookup_kernel, owners, context),
+        functools.partial(lookup_kernel, owners),
         out_shape=[
             jax.ShapeDtypeStruct((capacity, width), BF16),
             jax.ShapeDtypeStruct((rows, LANES), F32),
             jax.ShapeDtypeStruct((1,), jnp.int32),
-            jax.ShapeDtypeStruct((rows, head_dim), F32),
-            jax.ShapeDtypeStruct((rows, head_dim), F32),
         ],
-        in_specs=[SMEM, SMEM, HBM],
-        out_specs=[VMEM, VMEM, SMEM, VMEM, VMEM],
+        in_specs=[SMEM, HBM],
+        out_specs=[VMEM, VMEM, SMEM],
         scratch_shapes=fetch_scratch(rows, width),
         compiler_params=params(6 * rows * width * 8),
         cost_estimate=cost(rows * width, rows * width * 16),
         name="lookup",
-    )(token_ids, lengths, embedding)
+    )(token_ids, embedding)
 
 
 def lookup_rest(token_ids, places, embedding):
@@ -272,11 +259,11 @@
     )(parts)
 
 
-def project_kernel(heads_here, packed, x, gain, weight, *refs):
+def project_kernel(heads_here, packed, steps, context, x, gain, weight, lengths, *refs):
     if packed:
         slots, places, *refs = refs
     count = weight.shape[0] // heads_here
-    outs, scaled = refs[:count], refs[count]
+    outs, (cosine, sine, scaled) = refs[:count], refs[count:]
     chunks, rows, chunk_width = x.shape
     if packed:
         owners, capacity, width = slots.shape
@@ -296,7 +283,7 @@
     used = heads_here * columns
     rest = outs[0].shape[1] - used
     for shift in range(count):
-        first = lax.rem(here + shift, count) * heads_here
+        first = partner(here, shift, count) * heads_here
         products = [
             lax.dot_general(scaled[...], weight[first + head], NT, preferred_element_type=F32)
             for head in range(heads_here)
@@ -304,9 +291,10 @@
         outs[shift][...] = jnp.concatenate(
             products + [jnp.broadcast_to(squares, (rows, rest))], axis=1
         )
-
-
-def project(x, attn_gain, weight, packed=()):
+    cosine[...], sine[...] = rotary_tables(lengths, steps, rows, context, cosine.shape[1])
+
+
+def project(x, attn_gain, weight, lengths, steps, context, head_dim, packed):
     count = lax.axis_size("head")
     chunks, rows, chunk_width = x.shape
     heads, columns, width = weight.shape
@@ -314,15 +302,43 @@
     wide = round_up(heads_here * columns + 1, LANES)
     size = weight.size * 2
     return pl.pallas_call(
-        functools.partial(project_kernel, heads_here, bool(packed)),
-        out_shape=[jax.ShapeDtypeStruct((rows, wide), F32)] * count,
-        in_specs=[VMEM] * (3 + len(packed)),
-        out_specs=[VMEM] * count,
+        functools.partial(project_kernel, heads_here, bool(packed), steps, context),
+        out_shape=[jax.ShapeDtypeStruct((rows, wide), F32)] * count
+        + [jax.ShapeDtypeStruct((rows, head_dim), F32)] * 2,
+        in_specs=[VMEM] * 3 + [SMEM] + [VMEM] * len(packed),
+        out_specs=[VMEM] * (count + 2),
         scratch_shapes=[pltpu.VMEM((rows, width), BF16)],
         compiler_params=params(8 * MIB),
         cost_estimate=cost(2 * rows * weight.size, size),
         name="project",
-    )(x, attn_gain.reshape(1, width), weight, *packed)
+    )(x, attn_gain.reshape(1, width), weight, lengths, *packed)
+
+
+def folded(used):
+    return used % LANES == LANES // 2
+
+
+def fold(columns, used):
+    rows = columns.shape[0]
+    if not folded(used):
+        return columns
+    parts = [columns[:, i : i + LANES] for i in range(0, used - LANES // 2, LANES)]
+    rest = columns[:, used - LANES // 2 : used]
+    return jnp.concatenate(
+        parts + [jnp.concatenate([rest[: rows // 2], rest[rows // 2 :]], axis=1)], axis=0
+    )
+
+
+def unfold(block, rows, used):
+    if not folded(used):
+        return block
+    full = used // LANES
+    parts = [block[i * rows : (i + 1) * rows] for i in range(full)]
+    rest = block[full * rows :]
+    half = LANES // 2
+    return jnp.concatenate(
+        parts + [jnp.concatenate([rest[:, :half], rest[:, half:]], axis=0)], axis=1
+    )
 
 
 def norm_kernel(used, model_width, *refs):
@@ -331,13 +347,15 @@
     for piece in pieces[1:]:
         total = total + piece[...]
     factor = lax.rsqrt(total[:, used : used + 1] * (1.0 / model_width) + EPSILON)
-    united = (total * factor).astype(BF16)
+    united = fold(total * factor, used).astype(BF16)
     for target in range(out.shape[0]):
         out[target] = united
 
 
 def norm_copies(pieces, used, model_width):
     rows, wide = pieces[0].shape
+    if folded(used):
+        rows, wide = rows * used // LANES, LANES
     return pl.pallas_call(
         functools.partial(norm_kernel, used, model_width),
         out_shape=jax.ShapeDtypeStruct((lax.axis_size("ctx"), rows, wide), BF16),
@@ -407,7 +425,8 @@
     query_buf,
     score_buf,
 ):
-    chunks, rows, _ = united.shape
+    chunks = united.shape[0]
+    rows = cosine.shape[0]
     heads, context, head_dim = keys.shape
     per_dest = rows // chunks
     block = per_dest * group
@@ -421,12 +440,12 @@
         return vectors * cos + pltpu.roll(vectors, head_dim // 2, 1) * sin
 
     fresh = []
+    sources = [
+        unfold(united[chunk].astype(F32), rows, heads * columns) for chunk in range(chunks)
+    ]
     for head in range(heads):
         first = head * columns
-        whole = jnp.concatenate(
-            [united[chunk].astype(F32)[:, first : first + columns] for chunk in range(chunks)],
-            axis=1,
-        )
+        whole = jnp.concatenate([x[:, first : first + columns] for x in sources], axis=1)
         for j in range(group):
             query = rotated(whole[:, j * head_dim : (j + 1) * head_dim]) * head_dim ** (-0.5)
             for dest in range(chunks):
@@ -493,7 +512,8 @@
 
 
 def attend(united, columns, cosine, sine, keys, values, lengths, slot_keys, slot_values):
-    chunks, rows, _ = united.shape
+    chunks = united.shape[0]
+    rows = cosine.shape[0]
     heads, context, head_dim = keys.shape
     owned, slots, _, _ = slot_keys.shape
     group = columns * chunks // head_dim - 2
@@ -601,7 +621,7 @@
     here = lax.axis_index("head")
     height = total.shape[0] // count
     for shift in range(count):
-        first = pl.multiple_of(lax.rem(here + shift, count) * height, height)
+        first = pl.multiple_of(partner(here, shift, count) * height, height)
         outs[shift][...] = total[pl.ds(first, height), :].astype(BF16)
 
 
@@ -646,9 +666,7 @@
     capacity = 2 * rows // n_ctx
     qkv_weight = jnp.transpose(qkv_weight, (1, 2, 0))
     if embedding.shape[0] % 8 == 0 and capacity % 8 == 0:
-        packed, places, crowded, cosine, sine = lookup_packed(
-            token_ids, suffix_lengths, embedding, capacity, context, head_dim
-        )
+        packed, places, crowded = lookup_packed(token_ids, embedding, capacity)
 
         def rest():
             found = lookup_rest(token_ids, places, embedding)
@@ -659,11 +677,13 @@
 
         features = lax.cond(crowded[0] > 0, rest, nothing)
         packed = exchange(spread(packed, features, 4 * qkv_weight.size), "ctx")
-        pieces = project(features, attn_gain, qkv_weight, (packed, places))
+        packed = (packed, places)
     else:
-        cosine, sine = tables(suffix_lengths, steps, rows, context, head_dim)
         joined = join_copies(exchange(lookup_all(token_ids, embedding), "ctx"))
-        pieces = project(exchange(joined, "ctx"), attn_gain, qkv_weight)
+        features, packed = exchange(joined, "ctx"), ()
+    *pieces, cosine, sine = project(
+        features, attn_gain, qkv_weight, suffix_lengths, steps, context, head_dim, packed
+    )
     pieces = send_pieces(pieces, "head")
     united = norm_copies(pieces, heads * columns, width * n_head)
     united = exchange(united, "ctx")

time: 80.8 us -> 79.9 us (0.989)
  waiting for transfers between devices: 3.35 us -> 6.1 us
  starting transfers between devices: 6.02 us -> 3.84 us
  blocking collectives: 54.7 us -> 53.3 us
    ppermute x6, waiting for transfers between devices: 3.35 us -> 6.1 us  [send_pieces(): received.append(lax.ppermute(pieces[shift], axis, pairs))]
    ppermute x6, starting transfers between devices: 6.02 us -> 3.84 us  [send_pieces(): received.append(lax.ppermute(pieces[shift], axis, pairs))]
    all_to_all x4, blocking collectives: 54.7 us -> 53.3 us  [exchange(): return lax.all_to_all(blocks, axis, 0, 0)]
  transfers between devices with their start and end apart: 6 -> 6, of which waited for: 6 -> 4; matrix products, arithmetic and copies ran while one was open for 0% -> 0% of each run, Pallas kernels for 0% -> 0%
where the time goes in v6:
time: 79.9 us; the launch traced here: 79.5 us
  blocking collectives  53.3 us (67%)
  Pallas kernels  14.7 us (18%)
  waiting for transfers between devices  6.1 us (8%)
  starting transfers between devices  3.84 us (5%)
  between operations  0.83 us (1%)
    all_to_all x4, blocking collectives, exchange(): return lax.all_to_all(blocks, axis, 0, 0)  53.3 us
    ppermute x6, waiting for transfers between devices, send_pieces(): received.append(lax.ppermute(pieces[shift], axis, pairs))  6.1 us
    pallas_call x1, Pallas kernels, attend(): pl.pallas_call(functools.partial(attend_kernel, columns, group, owned), o...  4.82 us
    pallas_call x1, Pallas kernels, project(): pl.pallas_call(functools.partial(project_kernel, heads_here, bool(packed)...  4.27 us
    ppermute x6, starting transfers between devices, send_pieces(): received.append(lax.ppermute(pieces[shift], axis, pairs))  3.84 us
    pallas_call x1, Pallas kernels, lookup_packed(): pl.pallas_call(functools.partial(lookup_kernel, owners), out_shape=[jax.S...  3.14 us
  transfers between devices with their start and end apart: 6, of which 4 were waited for; matrix products, arithmetic and copies ran while one was open for 0% of the time, Pallas kernels for 0%

profile of v6, /device:TPU:0, one launch (start us, length us, event | category | flops | bytes accessed | tf_op | source)
XLA Modules:
  0.0 79.5 jit_solution(5203828961929935444)
XLA Ops:
  0.0 3.1 %lookup.1 = (bf16[8,4096]{1,0:T(8,128)(2,1)S(1)}, f32[32,128]{1,0:T(8,128)S(1)}, s32[1]{0:T(128)}) custom-call(s32[2,16]{1,0:T(2,128)} %tokens.1, bf16[8016,4096]{1,0:T(8,128)(2,1)} %table.1), custom_call_target="tpu_custom_call" | custom-call | flops 131072 | bytes 2097152 | tf_op jit(solution)/shard_map/lookup/pallas_call | solution.py:199
  3.9 0.0 copy-start
  3.9 0.0 copy-start.5
  3.9 0.0 copy-start.6
  3.9 0.0 copy-start.1
  4.0 0.0 copy-start.2
  4.0 0.0 copy-start.3
  4.0 0.0 copy-start.4
  4.0 22.0 %all_to_all.30.refs_0_ = bf16[8,8,4096]{2,1,0:T(8,128)(2,1)S(1)} all-to-all(bf16[8,8,4096]{2,1,0:T(8,128)(2,1)S(1)} %spread.1), channel_id=1, replica_groups=mesh['head'=4,'ctx'=8] {'ctx'}, dimensions={0} | all-to-all | bytes 1048576 | tf_op jit(solution)/shard_map/all_to_all | solution.py:37
  26.0 0.0 copy-done.6
  26.0 0.0 slice-start.1
  26.0 4.3 %project.1 = (f32[32,384]{1,0:T(8,128)S(1)}, f32[32,384]{1,0:T(8,128)S(1)}, f32[32,384]{1,0:T(8,128)S(1)}, f32[32,384]{1,0:T(8,128)S(1)}, f32[32,128]{1,0:T(8,128)S(1)}, /*index=5*/f32[32,128]{1,0:T(8,128)S(1)}) custom-call(bf16[8,32,512]{2,1,0:T(8,128)(2,1)S(1)} %get-tuple-element.51.first.x, f32[1,4096]{1,0:T(1,128)S(1)} %bitcast.10, ...), custom_call_target="tpu_custom_call" | custom-call | flops 335544320 | bytes 10485760 | tf_op jit(solution)/shard_map/project/pallas_call | solution.py:304
  30.3 0.1 collective-permute-start
  30.4 1.5 %collective-permute-start.1 = (f32[32,384]{1,0:T(8,128)S(1)}, f32[32,384]{1,0:T(8,128)S(1)}, u32[]{:S(2)}, u32[]{:S(2)}) collective-permute-start(f32[32,384]{1,0:T(8,128)S(1)} %get-tuple-element.39), channel_id=1, source_target_pairs={{0,16},{8,24},{16,0},{24,8},{1,17},{9,25},{17,1},{25,9},{2,18},{10... | collective-permute-start | bytes 147464 | tf_op jit(solution)/shard_map/ppermute | solution.py:51
  31.9 0.3 collective-permute-start.2
  32.2 0.0 collective-permute-done.refs_1_
  32.2 2.3 %collective-permute-done.1.refs_2_ = f32[32,384]{1,0:T(8,128)S(1)} collective-permute-done((f32[32,384]{1,0:T(8,128)S(1)}, f32[32,384]{1,0:T(8,128)S(1)}, u32[]{:S(2)}, u32[]{:S(2)}) %collective-permute-start.1) | collective-permute-done | bytes 49184 | tf_op jit(solution)/shard_map/ppermute | solution.py:51
  34.5 1.1 %collective-permute-done.2.refs_3_ = f32[32,384]{1,0:T(8,128)S(1)} collective-permute-done((f32[32,384]{1,0:T(8,128)S(1)}, f32[32,384]{1,0:T(8,128)S(1)}, u32[]{:S(2)}, u32[]{:S(2)}) %collective-permute-start.2) | collective-permute-done | bytes 49184 | tf_op jit(solution)/shard_map/ppermute | solution.py:51
  35.6 0.2 norm.1
  35.8 11.2 %all_to_all.31.united = bf16[8,80,128]{2,1,0:T(8,128)(2,1)S(1)} all-to-all(bf16[8,80,128]{2,1,0:T(8,128)(2,1)S(1)} %norm.1), channel_id=1, replica_groups=mesh['head'=4,'ctx'=8] {'ctx'}, dimensions={0} | all-to-all | bytes 327680 | tf_op jit(solution)/shard_map/all_to_all | solution.py:37
  47.0 4.8 %attend.1 = (bf16[8,80,128]{2,1,0:T(8,128)(2,1)S(1)}, f32[64,128]{1,0:T(8,128)S(1)}, f32[64,128]{1,0:T(8,128)S(1)}, f32[64,128]{1,0:T(8,128)S(1)}) custom-call(s32[16]{0:T(128)S(1)} %copy-done.6, bf16[8,80,128]{2,1,0:T(8,128)(2,1)S(1)} %all_to_all.31.united, f32[32,128]{1,0:T(8,128)S(1)} %get-tuple-element.41.cosine, f32[32,128]{1,0:T(8,128)S(1)} %get-tuple-element.42.sine, ...), custom_call_target="tpu_custom_call" | custom-call | flops 1073741824 | bytes 4194304 | tf_op jit(solution)/shard_map/attend/pallas_call | solution.py:524
  51.8 10.3 %all_to_all.32.parts = bf16[8,80,128]{2,1,0:T(8,128)(2,1)S(1)} all-to-all(bf16[8,80,128]{2,1,0:T(8,128)(2,1)S(1)} %get-tuple-element.43), channel_id=1, replica_groups=mesh['head'=4,'ctx'=8] {'ctx'}, dimensions={0} | all-to-all | bytes 327680 | tf_op jit(solution)/shard_map/all_to_all | solution.py:37
  62.1 0.8 merge.1
  62.9 9.8 %all_to_all.33.x = bf16[8,4,2048]{2,1,0:T(4,128)(2,1)S(1)} all-to-all(bf16[8,4,2048]{2,1,0:T(4,128)(2,1)S(1)} %merge.1), channel_id=1, replica_groups=mesh['head'=4,'ctx'=8] {'ctx'}, dimensions={0} | all-to-all | bytes 262144 | tf_op jit(solution)/shard_map/all_to_all | solution.py:37
  72.7 1.6 %output.1 = (bf16[8,2048]{1,0:T(8,128)(2,1)S(1)}, bf16[8,2048]{1,0:T(8,128)(2,1)S(1)}, bf16[8,2048]{1,0:T(8,128)(2,1)S(1)}, bf16[8,2048]{1,0:T(8,128)(2,1)S(1)}) custom-call(bf16[8,4,2048]{2,1,0:T(4,128)(2,1)S(1)} %all_to_all.33.x, bf16[2048,2048]{1,0:T(8,128)(2,1)S(1)} %bitcast.7), custom_call_target="tpu_custom_call" | custom-call | flops 268435456 | bytes 8388608 | tf_op jit(solution)/shard_map/output/pallas_call | solution.py:633
  74.3 0.1 collective-permute-start.3
  74.3 1.2 %collective-permute-start.4 = (bf16[8,2048]{1,0:T(8,128)(2,1)S(1)}, bf16[8,2048]{1,0:T(8,128)(2,1)S(1)}, u32[]{:S(2)}, u32[]{:S(2)}) collective-permute-start(bf16[8,2048]{1,0:T(8,128)(2,1)S(1)} %get-tuple-element.49), channel_id=1, source_target_pairs={{0,16},{8,24},{16,0},{24,8},{1,17},{9,25},{17,1},{25,9},{2,18},{10... | collective-permute-start | bytes 98312 | tf_op jit(solution)/shard_map/ppermute | solution.py:51
  75.5 0.7 collective-permute-start.5
  76.2 0.0 collective-permute-done.3
  76.2 2.1 %collective-permute-done.4 = bf16[8,2048]{1,0:T(8,128)(2,1)S(1)} collective-permute-done((bf16[8,2048]{1,0:T(8,128)(2,1)S(1)}, bf16[8,2048]{1,0:T(8,128)(2,1)S(1)}, u32[]{:S(2)}, u32[]{:S(2)}) %collective-permute-start.4) | collective-permute-done | bytes 32800 | tf_op jit(solution)/shard_map/ppermute | solution.py:51
  78.3 0.6 collective-permute-done.5
  78.9 0.6 reshape.19
  (16 shorter events, 0.1 us)
Async XLA Ops:
  0.0 3.8 %copy-start.7 = (s32[2,16]{1,0:T(2,128)S(1)}, s32[2,16]{1,0:T(2,128)}, u32[]{:S(2)}) copy-start(s32[2,16]{1,0:T(2,128)} %tokens.1) | copy-start | bytes 388
  3.9 22.1 %copy-start = (bf16[4096,8,160]{0,2,1:T(8,128)(2,1)S(1)}, bf16[4096,8,160]{0,2,1:T(8,128)(2,1)}, u32[]{:S(2)}) copy-start(bf16[4096,8,160]{0,2,1:T(8,128)(2,1)} %param.16) | copy-start | bytes 31457284
  3.9 22.1 %copy-start.5 = (f32[4096]{0:T(1024)S(1)}, f32[4096]{0:T(1024)}, u32[]{:S(2)}) copy-start(f32[4096]{0:T(1024)} %param.15) | copy-start | bytes 49156
  3.9 22.1 %copy-start.6 = (s32[16]{0:T(128)S(1)}, s32[16]{0:T(128)}, u32[]{:S(2)}) copy-start(s32[16]{0:T(128)} %lengths.3) | copy-start | bytes 196
  3.9 43.0 %copy-start.1 = (bf16[2,4096,128]{2,1,0:T(8,128)(2,1)S(1)}, bf16[2,4096,128]{2,1,0:T(8,128)(2,1)}, u32[]{:S(2)}) copy-start(bf16[2,4096,128]{2,1,0:T(8,128)(2,1)} %keys.1) | copy-start | bytes 6291460
  4.0 43.0 %copy-start.2 = (bf16[2,4096,128]{2,1,0:T(8,128)(2,1)S(1)}, bf16[2,4096,128]{2,1,0:T(8,128)(2,1)}, u32[]{:S(2)}) copy-start(bf16[2,4096,128]{2,1,0:T(8,128)(2,1)} %values.1) | copy-start | bytes 6291460
  4.0 43.0 %copy-start.3 = (bf16[2,128,2,128]{3,2,1,0:T(2,128)(2,1)S(1)}, bf16[2,128,2,128]{3,2,1,0:T(2,128)(2,1)}, u32[]{:S(2)}) copy-start(bf16[2,128,2,128]{3,2,1,0:T(2,128)(2,1)} %param.20) | copy-start | bytes 393220
  4.0 43.0 %copy-start.4 = (bf16[2,128,2,128]{3,2,1,0:T(2,128)(2,1)S(1)}, bf16[2,128,2,128]{3,2,1,0:T(2,128)(2,1)}, u32[]{:S(2)}) copy-start(bf16[2,128,2,128]{3,2,1,0:T(2,128)(2,1)} %param.21) | copy-start | bytes 393220
  26.0 46.7 %slice-start = ((s8[8388608]{0:T(1024)(128)(4,1)}), s8[4194304]{0:T(1024)(128)(4,1)S(1)}, s32[]{:S(2)}) async-start(s8[8388608]{0:T(1024)(128)(4,1)} %bitcast.6), calls=%async_computation.6 | async-start | bytes 8388608
  26.0 46.7 %slice-start.1 = ((s8[8388608]{0:T(1024)(128)(4,1)}), s8[4194304]{0:T(1024)(128)(4,1)S(1)}, s32[]{:S(2)}) async-start(s8[8388608]{0:T(1024)(128)(4,1)} %bitcast.6), calls=%async_computation.7 | async-start | bytes 8388608
  30.3 1.9 %collective-permute-start = (f32[32,384]{1,0:T(8,128)S(1)}, f32[32,384]{1,0:T(8,128)S(1)}, u32[]{:S(2)}, u32[]{:S(2)}) collective-permute-start(f32[32,384]{1,0:T(8,128)S(1)} %get-tuple-element.38), channel_id=1, source_target_pairs={{0,8},{8,0},{16,24},{24,16},{1,9},{9,1},{17,25},{25,17},{2,10},{10... | collective-permute-start | bytes 147464 | tf_op jit(solution)/shard_map/ppermute | solution.py:51
  30.4 4.2 %collective-permute-start.1 = (f32[32,384]{1,0:T(8,128)S(1)}, f32[32,384]{1,0:T(8,128)S(1)}, u32[]{:S(2)}, u32[]{:S(2)}) collective-permute-start(f32[32,384]{1,0:T(8,128)S(1)} %get-tuple-element.39), channel_id=1, source_target_pairs={{0,16},{8,24},{16,0},{24,8},{1,17},{9,25},{17,1},{25,9},{2,18},{10... | collective-permute-start | bytes 147464 | tf_op jit(solution)/shard_map/ppermute | solution.py:51
  31.9 3.7 %collective-permute-start.2 = (f32[32,384]{1,0:T(8,128)S(1)}, f32[32,384]{1,0:T(8,128)S(1)}, u32[]{:S(2)}, u32[]{:S(2)}) collective-permute-start(f32[32,384]{1,0:T(8,128)S(1)} %get-tuple-element.40), channel_id=1, source_target_pairs={{0,24},{8,16},{16,8},{24,0},{1,25},{9,17},{17,9},{25,1},{2,26},{10... | collective-permute-start | bytes 147464 | tf_op jit(solution)/shard_map/ppermute | solution.py:51
  74.3 1.9 %collective-permute-start.3 = (bf16[8,2048]{1,0:T(8,128)(2,1)S(1)}, bf16[8,2048]{1,0:T(8,128)(2,1)S(1)}, u32[]{:S(2)}, u32[]{:S(2)}) collective-permute-start(bf16[8,2048]{1,0:T(8,128)(2,1)S(1)} %get-tuple-element.48), channel_id=1, source_target_pairs={{0,8},{8,0},{16,24},{24,16},{1,9},{9,1},{17,25},{25,17},{2,10},{10... | collective-permute-start | bytes 98312 | tf_op jit(solution)/shard_map/ppermute | solution.py:51
  74.3 4.0 %collective-permute-start.4 = (bf16[8,2048]{1,0:T(8,128)(2,1)S(1)}, bf16[8,2048]{1,0:T(8,128)(2,1)S(1)}, u32[]{:S(2)}, u32[]{:S(2)}) collective-permute-start(bf16[8,2048]{1,0:T(8,128)(2,1)S(1)} %get-tuple-element.49), channel_id=1, source_target_pairs={{0,16},{8,24},{16,0},{24,8},{1,17},{9,25},{17,1},{25,9},{2,18},{10... | collective-permute-start | bytes 98312 | tf_op jit(solution)/shard_map/ppermute | solution.py:51
  75.5 3.4 %collective-permute-start.5 = (bf16[8,2048]{1,0:T(8,128)(2,1)S(1)}, bf16[8,2048]{1,0:T(8,128)(2,1)S(1)}, u32[]{:S(2)}, u32[]{:S(2)}) collective-permute-start(bf16[8,2048]{1,0:T(8,128)(2,1)S(1)} %get-tuple-element.50), channel_id=1, source_target_pairs={{0,24},{8,16},{16,8},{24,0},{1,25},{9,17},{17,9},{25,1},{2,26},{10... | collective-permute-start | bytes 98312 | tf_op jit(solution)/shard_map/ppermute | solution.py:51

commit v7 on v6

--- a/solution.py
+++ b/solution.py
@@ -372,21 +372,24 @@
     return first, second, value - first - second
 
 
-def near_block(query, fresh_key, fresh_value, keys, values, head, heads, steps, lengths):
+def near_block(query, fresh_key, fresh_value, keys, values, heads, steps, lengths):
     owned, slots_all, _ = keys.shape
-    block = query.shape[0]
-    rows = fresh_key.shape[0]
+    block = query.shape[0] // heads
+    rows = fresh_key.shape[0] // heads
     mine = lax.axis_index("ctx")
 
     def iota(shape, axis):
         return lax.broadcasted_iota(jnp.int32, shape, axis)
 
-    query_place = iota((block, 1), 0) % (owned * steps)
-    sequence = query_place // steps
-    step = query_place % steps
+    place = iota((heads * block, 1), 0)
+    head = place // block
+    sequence = place % (owned * steps) // steps
+    step = place % steps
     slot = iota((1, slots_all), 1)
-    fresh_row = iota((1, rows), 1)
-    fresh_here = (fresh_row // steps == mine * owned + sequence) & (fresh_row % steps <= step)
+    fresh_row = iota((1, heads * rows), 1)
+    fresh_here = (fresh_row // steps == head * (rows // steps) + mine * owned + sequence) & (
+        fresh_row % steps <= step
+    )
     fresh_scores = lax.dot_general(query, fresh_key, NT, preferred_element_type=F32)
     scores = [jnp.where(fresh_here, fresh_scores, MASKED)]
     highest = jnp.max(scores[0], axis=-1, keepdims=True)
@@ -397,8 +400,8 @@
         found = jnp.where(live, found, MASKED)
         scores.append(found)
         highest = jnp.maximum(highest, jnp.max(found, axis=-1, keepdims=True))
-    total = jnp.zeros((block, 1), F32)
-    result = jnp.zeros((block, fresh_value.shape[1]), F32)
+    total = jnp.zeros((heads * block, 1), F32)
+    result = jnp.zeros((heads * block, fresh_value.shape[1]), F32)
     for found, value in zip(scores, [fresh_value] + [values[s] for s in range(owned)]):
         weights = jnp.exp(found - highest).astype(BF16)
         total = total + jnp.sum(weights.astype(F32), axis=-1, keepdims=True)
@@ -472,16 +475,14 @@
                 piece = scores[:, part * LANES : (part + 1) * LANES]
                 highest = piece if highest is None else jnp.maximum(highest, piece)
         maxima = jnp.max(highest, axis=-1, keepdims=True)
-        sums = jnp.zeros((chunks * block, head_dim), F32)
-        totals = jnp.zeros((chunks * block, LANES), F32)
+        both = jnp.zeros((chunks * block, head_dim + LANES), F32)
+        ones = jnp.ones((tile, LANES), BF16)
         for step in range(tiles):
             span = slice(step * tile, (step + 1) * tile)
             weights = jnp.exp(score_buf[:, span] - maxima).astype(BF16)
-            sums = sums + jnp.dot(weights, values[head, span, :], preferred_element_type=F32)
-            wide = weights.astype(F32)
-            for part in range(tile // LANES):
-                totals = totals + wide[:, part * LANES : (part + 1) * LANES]
-        total = jnp.sum(totals, axis=-1, keepdims=True)
+            extended = jnp.concatenate([values[head, span, :], ones], axis=1)
+            both = both + jnp.dot(weights, extended, preferred_element_type=F32)
+        sums, total = both[:, :head_dim], both[:, head_dim:]
         for index, piece in enumerate(split3(maxima) + split3(total)):
             table = jnp.where(lane == head * 8 + index, piece, table)
         rounded = sums.astype(BF16)
@@ -489,21 +490,20 @@
             packet[dest, head * block : (head + 1) * block] = rounded[
                 dest * block : (dest + 1) * block
             ]
-        own_query = query_buf[head, pl.ds(pl.multiple_of(mine * block, block), block), :]
-        near_max, near_total, near_sum = near_block(
-            own_query.astype(BF16),
-            *fresh[head],
-            slot_keys,
-            slot_values,
-            head,
-            heads,
-            per_dest // owned,
-            lengths,
-        )
-        span = slice(head * block, (head + 1) * block)
-        near_sums[span, :] = near_sum
-        near_maxima[span, :] = jnp.broadcast_to(near_max, (block, head_dim))
-        near_totals[span, :] = jnp.broadcast_to(near_total, (block, head_dim))
+    own = pl.ds(pl.multiple_of(mine * block, block), block)
+    near_max, near_total, near_sum = near_block(
+        jnp.concatenate([query_buf[head, own, :] for head in range(heads)], axis=0).astype(BF16),
+        jnp.concatenate([key for key, value in fresh], axis=0),
+        jnp.concatenate([value for key, value in fresh], axis=0),
+        slot_keys,
+        slot_values,
+        heads,
+        per_dest // owned,
+        lengths,
+    )
+    near_sums[...] = near_sum
+    near_maxima[...] = jnp.broadcast_to(near_max, near_maxima.shape)
+    near_totals[...] = jnp.broadcast_to(near_total, near_totals.shape)
     low = heads * block
     pieces = packet.shape[1] - low
     turned = jnp.transpose(table)[:pieces]

time: 79.9 us -> 79.4 us (level)
  no operation moved by 1% of the time
where the time goes in v7:
time: 79.4 us; the launch traced here: 79 us
  blocking collectives  53.1 us (67%)
  Pallas kernels  14.4 us (18%)
  waiting for transfers between devices  6.09 us (8%)
  starting transfers between devices  3.84 us (5%)
  between operations  0.83 us (1%)
    all_to_all x4, blocking collectives, exchange(): return lax.all_to_all(blocks, axis, 0, 0)  53.1 us
    ppermute x6, waiting for transfers between devices, send_pieces(): received.append(lax.ppermute(pieces[shift], axis, pairs))  6.09 us
    pallas_call x1, Pallas kernels, attend(): pl.pallas_call(functools.partial(attend_kernel, columns, group, owned), o...  4.54 us
    pallas_call x1, Pallas kernels, project(): pl.pallas_call(functools.partial(project_kernel, heads_here, bool(packed)...  4.27 us
    ppermute x6, starting transfers between devices, send_pieces(): received.append(lax.ppermute(pieces[shift], axis, pairs))  3.84 us
    pallas_call x1, Pallas kernels, lookup_packed(): pl.pallas_call(functools.partial(lookup_kernel, owners), out_shape=[jax.S...  3.11 us
  transfers between devices with their start and end apart: 6, of which 4 were waited for; matrix products, arithmetic and copies ran while one was open for 0% of the time, Pallas kernels for 0%

profile of v7, /device:TPU:0, one launch (start us, length us, event | category | flops | bytes accessed | tf_op | source)
XLA Modules:
  0.0 79.0 jit_solution(11604372398399708199)
XLA Ops:
  0.0 3.1 %lookup.1 = (bf16[8,4096]{1,0:T(8,128)(2,1)S(1)}, f32[32,128]{1,0:T(8,128)S(1)}, s32[1]{0:T(128)}) custom-call(s32[2,16]{1,0:T(2,128)} %tokens.1, bf16[8016,4096]{1,0:T(8,128)(2,1)} %table.1), custom_call_target="tpu_custom_call" | custom-call | flops 131072 | bytes 2097152 | tf_op jit(solution)/shard_map/lookup/pallas_call | solution.py:199
  3.8 0.0 copy-start
  3.8 0.0 copy-start.5
  3.8 0.0 copy-start.6
  3.9 0.0 copy-start.1
  3.9 0.0 copy-start.2
  3.9 0.0 copy-start.3
  3.9 0.0 copy-start.4
  4.0 21.8 %all_to_all.30.refs_0_ = bf16[8,8,4096]{2,1,0:T(8,128)(2,1)S(1)} all-to-all(bf16[8,8,4096]{2,1,0:T(8,128)(2,1)S(1)} %spread.1), channel_id=1, replica_groups=mesh['head'=4,'ctx'=8] {'ctx'}, dimensions={0} | all-to-all | bytes 1048576 | tf_op jit(solution)/shard_map/all_to_all | solution.py:37
  25.7 0.0 copy-done
  25.7 0.0 slice-start.1
  25.8 4.3 %project.1 = (f32[32,384]{1,0:T(8,128)S(1)}, f32[32,384]{1,0:T(8,128)S(1)}, f32[32,384]{1,0:T(8,128)S(1)}, f32[32,384]{1,0:T(8,128)S(1)}, f32[32,128]{1,0:T(8,128)S(1)}, /*index=5*/f32[32,128]{1,0:T(8,128)S(1)}) custom-call(bf16[8,32,512]{2,1,0:T(8,128)(2,1)S(1)} %get-tuple-element.51.first.x, f32[1,4096]{1,0:T(1,128)S(1)} %bitcast.10, ...), custom_call_target="tpu_custom_call" | custom-call | flops 335544320 | bytes 10485760 | tf_op jit(solution)/shard_map/project/pallas_call | solution.py:304
  30.0 0.1 collective-permute-start
  30.1 1.6 %collective-permute-start.1 = (f32[32,384]{1,0:T(8,128)S(1)}, f32[32,384]{1,0:T(8,128)S(1)}, u32[]{:S(2)}, u32[]{:S(2)}) collective-permute-start(f32[32,384]{1,0:T(8,128)S(1)} %get-tuple-element.39), channel_id=1, source_target_pairs={{0,16},{8,24},{16,0},{24,8},{1,17},{9,25},{17,1},{25,9},{2,18},{10... | collective-permute-start | bytes 147464 | tf_op jit(solution)/shard_map/ppermute | solution.py:51
  31.7 0.3 collective-permute-start.2
  32.0 0.0 collective-permute-done.refs_1_
  32.0 2.3 %collective-permute-done.1.refs_2_ = f32[32,384]{1,0:T(8,128)S(1)} collective-permute-done((f32[32,384]{1,0:T(8,128)S(1)}, f32[32,384]{1,0:T(8,128)S(1)}, u32[]{:S(2)}, u32[]{:S(2)}) %collective-permute-start.1) | collective-permute-done | bytes 49184 | tf_op jit(solution)/shard_map/ppermute | solution.py:51
  34.3 1.1 %collective-permute-done.2.refs_3_ = f32[32,384]{1,0:T(8,128)S(1)} collective-permute-done((f32[32,384]{1,0:T(8,128)S(1)}, f32[32,384]{1,0:T(8,128)S(1)}, u32[]{:S(2)}, u32[]{:S(2)}) %collective-permute-start.2) | collective-permute-done | bytes 49184 | tf_op jit(solution)/shard_map/ppermute | solution.py:51
  35.4 0.2 norm.1
  35.6 11.2 %all_to_all.31.united = bf16[8,80,128]{2,1,0:T(8,128)(2,1)S(1)} all-to-all(bf16[8,80,128]{2,1,0:T(8,128)(2,1)S(1)} %norm.1), channel_id=1, replica_groups=mesh['head'=4,'ctx'=8] {'ctx'}, dimensions={0} | all-to-all | bytes 327680 | tf_op jit(solution)/shard_map/all_to_all | solution.py:37
  46.7 4.5 %attend.1 = (bf16[8,80,128]{2,1,0:T(8,128)(2,1)S(1)}, f32[64,128]{1,0:T(8,128)S(1)}, f32[64,128]{1,0:T(8,128)S(1)}, f32[64,128]{1,0:T(8,128)S(1)}) custom-call(s32[16]{0:T(128)S(1)} %copy-done.6, bf16[8,80,128]{2,1,0:T(8,128)(2,1)S(1)} %all_to_all.31.united, f32[32,128]{1,0:T(8,128)S(1)} %get-tuple-element.41.cosine, f32[32,128]{1,0:T(8,128)S(1)} %get-tuple-element.42.sine, ...), custom_call_target="tpu_custom_call" | custom-call | flops 1073741824 | bytes 4194304 | tf_op jit(solution)/shard_map/attend/pallas_call | solution.py:524
  51.3 10.3 %all_to_all.32.parts = bf16[8,80,128]{2,1,0:T(8,128)(2,1)S(1)} all-to-all(bf16[8,80,128]{2,1,0:T(8,128)(2,1)S(1)} %get-tuple-element.43), channel_id=1, replica_groups=mesh['head'=4,'ctx'=8] {'ctx'}, dimensions={0} | all-to-all | bytes 327680 | tf_op jit(solution)/shard_map/all_to_all | solution.py:37
  61.6 0.8 merge.1
  62.3 9.8 %all_to_all.33.x = bf16[8,4,2048]{2,1,0:T(4,128)(2,1)S(1)} all-to-all(bf16[8,4,2048]{2,1,0:T(4,128)(2,1)S(1)} %merge.1), channel_id=1, replica_groups=mesh['head'=4,'ctx'=8] {'ctx'}, dimensions={0} | all-to-all | bytes 262144 | tf_op jit(solution)/shard_map/all_to_all | solution.py:37
  72.2 1.6 %output.1 = (bf16[8,2048]{1,0:T(8,128)(2,1)S(1)}, bf16[8,2048]{1,0:T(8,128)(2,1)S(1)}, bf16[8,2048]{1,0:T(8,128)(2,1)S(1)}, bf16[8,2048]{1,0:T(8,128)(2,1)S(1)}) custom-call(bf16[8,4,2048]{2,1,0:T(4,128)(2,1)S(1)} %all_to_all.33.x, bf16[2048,2048]{1,0:T(8,128)(2,1)S(1)} %bitcast.7), custom_call_target="tpu_custom_call" | custom-call | flops 268435456 | bytes 8388608 | tf_op jit(solution)/shard_map/output/pallas_call | solution.py:633
  73.7 0.1 collective-permute-start.3
  73.8 1.2 %collective-permute-start.4 = (bf16[8,2048]{1,0:T(8,128)(2,1)S(1)}, bf16[8,2048]{1,0:T(8,128)(2,1)S(1)}, u32[]{:S(2)}, u32[]{:S(2)}) collective-permute-start(bf16[8,2048]{1,0:T(8,128)(2,1)S(1)} %get-tuple-element.49), channel_id=1, source_target_pairs={{0,16},{8,24},{16,0},{24,8},{1,17},{9,25},{17,1},{25,9},{2,18},{10... | collective-permute-start | bytes 98312 | tf_op jit(solution)/shard_map/ppermute | solution.py:51
  75.0 0.7 collective-permute-start.5
  75.7 0.0 collective-permute-done.3
  75.7 2.1 %collective-permute-done.4 = bf16[8,2048]{1,0:T(8,128)(2,1)S(1)} collective-permute-done((bf16[8,2048]{1,0:T(8,128)(2,1)S(1)}, bf16[8,2048]{1,0:T(8,128)(2,1)S(1)}, u32[]{:S(2)}, u32[]{:S(2)}) %collective-permute-start.4) | collective-permute-done | bytes 32800 | tf_op jit(solution)/shard_map/ppermute | solution.py:51
  77.8 0.5 collective-permute-done.5
  78.4 0.6 reshape.19
  (16 shorter events, 0.1 us)
Async XLA Ops:
  0.0 3.8 %copy-start.7 = (s32[2,16]{1,0:T(2,128)S(1)}, s32[2,16]{1,0:T(2,128)}, u32[]{:S(2)}) copy-start(s32[2,16]{1,0:T(2,128)} %tokens.1) | copy-start | bytes 388
  3.8 21.9 %copy-start = (bf16[4096,8,160]{0,2,1:T(8,128)(2,1)S(1)}, bf16[4096,8,160]{0,2,1:T(8,128)(2,1)}, u32[]{:S(2)}) copy-start(bf16[4096,8,160]{0,2,1:T(8,128)(2,1)} %param.16) | copy-start | bytes 31457284
  3.8 21.9 %copy-start.5 = (f32[4096]{0:T(1024)S(1)}, f32[4096]{0:T(1024)}, u32[]{:S(2)}) copy-start(f32[4096]{0:T(1024)} %param.15) | copy-start | bytes 49156
  3.8 21.9 %copy-start.6 = (s32[16]{0:T(128)S(1)}, s32[16]{0:T(128)}, u32[]{:S(2)}) copy-start(s32[16]{0:T(128)} %lengths.3) | copy-start | bytes 196
  3.9 42.8 %copy-start.1 = (bf16[2,4096,128]{2,1,0:T(8,128)(2,1)S(1)}, bf16[2,4096,128]{2,1,0:T(8,128)(2,1)}, u32[]{:S(2)}) copy-start(bf16[2,4096,128]{2,1,0:T(8,128)(2,1)} %keys.1) | copy-start | bytes 6291460
  3.9 42.8 %copy-start.2 = (bf16[2,4096,128]{2,1,0:T(8,128)(2,1)S(1)}, bf16[2,4096,128]{2,1,0:T(8,128)(2,1)}, u32[]{:S(2)}) copy-start(bf16[2,4096,128]{2,1,0:T(8,128)(2,1)} %values.1) | copy-start | bytes 6291460
  3.9 42.8 %copy-start.3 = (bf16[2,128,2,128]{3,2,1,0:T(2,128)(2,1)S(1)}, bf16[2,128,2,128]{3,2,1,0:T(2,128)(2,1)}, u32[]{:S(2)}) copy-start(bf16[2,128,2,128]{3,2,1,0:T(2,128)(2,1)} %param.20) | copy-start | bytes 393220
  3.9 42.8 %copy-start.4 = (bf16[2,128,2,128]{3,2,1,0:T(2,128)(2,1)S(1)}, bf16[2,128,2,128]{3,2,1,0:T(2,128)(2,1)}, u32[]{:S(2)}) copy-start(bf16[2,128,2,128]{3,2,1,0:T(2,128)(2,1)} %param.21) | copy-start | bytes 393220
  25.7 46.4 %slice-start = ((s8[8388608]{0:T(1024)(128)(4,1)}), s8[4194304]{0:T(1024)(128)(4,1)S(1)}, s32[]{:S(2)}) async-start(s8[8388608]{0:T(1024)(128)(4,1)} %bitcast.6), calls=%async_computation.6 | async-start | bytes 8388608
  25.7 46.4 %slice-start.1 = ((s8[8388608]{0:T(1024)(128)(4,1)}), s8[4194304]{0:T(1024)(128)(4,1)S(1)}, s32[]{:S(2)}) async-start(s8[8388608]{0:T(1024)(128)(4,1)} %bitcast.6), calls=%async_computation.7 | async-start | bytes 8388608
  30.0 1.9 %collective-permute-start = (f32[32,384]{1,0:T(8,128)S(1)}, f32[32,384]{1,0:T(8,128)S(1)}, u32[]{:S(2)}, u32[]{:S(2)}) collective-permute-start(f32[32,384]{1,0:T(8,128)S(1)} %get-tuple-element.38), channel_id=1, source_target_pairs={{0,8},{8,0},{16,24},{24,16},{1,9},{9,1},{17,25},{25,17},{2,10},{10... | collective-permute-start | bytes 147464 | tf_op jit(solution)/shard_map/ppermute | solution.py:51
  30.1 4.2 %collective-permute-start.1 = (f32[32,384]{1,0:T(8,128)S(1)}, f32[32,384]{1,0:T(8,128)S(1)}, u32[]{:S(2)}, u32[]{:S(2)}) collective-permute-start(f32[32,384]{1,0:T(8,128)S(1)} %get-tuple-element.39), channel_id=1, source_target_pairs={{0,16},{8,24},{16,0},{24,8},{1,17},{9,25},{17,1},{25,9},{2,18},{10... | collective-permute-start | bytes 147464 | tf_op jit(solution)/shard_map/ppermute | solution.py:51
  31.7 3.7 %collective-permute-start.2 = (f32[32,384]{1,0:T(8,128)S(1)}, f32[32,384]{1,0:T(8,128)S(1)}, u32[]{:S(2)}, u32[]{:S(2)}) collective-permute-start(f32[32,384]{1,0:T(8,128)S(1)} %get-tuple-element.40), channel_id=1, source_target_pairs={{0,24},{8,16},{16,8},{24,0},{1,25},{9,17},{17,9},{25,1},{2,26},{10... | collective-permute-start | bytes 147464 | tf_op jit(solution)/shard_map/ppermute | solution.py:51
  73.7 1.9 %collective-permute-start.3 = (bf16[8,2048]{1,0:T(8,128)(2,1)S(1)}, bf16[8,2048]{1,0:T(8,128)(2,1)S(1)}, u32[]{:S(2)}, u32[]{:S(2)}) collective-permute-start(bf16[8,2048]{1,0:T(8,128)(2,1)S(1)} %get-tuple-element.48), channel_id=1, source_target_pairs={{0,8},{8,0},{16,24},{24,16},{1,9},{9,1},{17,25},{25,17},{2,10},{10... | collective-permute-start | bytes 98312 | tf_op jit(solution)/shard_map/ppermute | solution.py:51
  73.8 4.0 %collective-permute-start.4 = (bf16[8,2048]{1,0:T(8,128)(2,1)S(1)}, bf16[8,2048]{1,0:T(8,128)(2,1)S(1)}, u32[]{:S(2)}, u32[]{:S(2)}) collective-permute-start(bf16[8,2048]{1,0:T(8,128)(2,1)S(1)} %get-tuple-element.49), channel_id=1, source_target_pairs={{0,16},{8,24},{16,0},{24,8},{1,17},{9,25},{17,1},{25,9},{2,18},{10... | collective-permute-start | bytes 98312 | tf_op jit(solution)/shard_map/ppermute | solution.py:51
  75.0 3.4 %collective-permute-start.5 = (bf16[8,2048]{1,0:T(8,128)(2,1)S(1)}, bf16[8,2048]{1,0:T(8,128)(2,1)S(1)}, u32[]{:S(2)}, u32[]{:S(2)}) collective-permute-start(bf16[8,2048]{1,0:T(8,128)(2,1)S(1)} %get-tuple-element.50), channel_id=1, source_target_pairs={{0,24},{8,16},{16,8},{24,0},{1,25},{9,17},{17,9},{25,1},{2,26},{10... | collective-permute-start | bytes 98312 | tf_op jit(solution)/shard_map/ppermute | solution.py:51
